TPU v7x, 256 devices: a whole 4x4x8 slice. The times are simulated.
256 devices in a mesh: ep: 32 (over x, z), tp: 8 (over y, core).
Axes of the slice: x: 4, y: 4, z: 8, core: 2. Of those that a mesh axis runs over, the one named last changes fastest.
Arguments:
- tokens: bfloat16 [4096, 3072], P('ep', 'tp'), may hold values from -6 to 6
- expert_ids: int32 [4096, 2], P('ep'), may hold values from 0 to 7, all different within a row
- route_share: float32 [4096], P('ep'), may hold values from 0.5 to 0.95
- w_gate: bfloat16 [65536, 3072], P(('ep', 'tp')), may hold values from -0.109375 to 0.109375
- w_up: bfloat16 [65536, 3072], P(('ep', 'tp')), may hold values from -0.109375 to 0.109375
- w_down: bfloat16 [65536, 3072], P(('ep', 'tp')), may hold values from -0.0625 to 0.0625
- reward_head: float32 [3072], P('tp'), may hold values from -0.109375 to 0.109375
- upstream: bfloat16 [4096, 3072], P('ep', 'tp'), may hold values from -4 to 4
- pair_order: int32 [64], replicated, may hold values from 0 to 63, each once
Outputs:
- layer_out: bfloat16 [4096, 3072], P('ep', 'tp')
- rewards: float32 [64], replicated
- pair_loss: float32 [], replicated
- grad_tokens: bfloat16 [4096, 3072], P('ep', 'tp')
- grad_gate: bfloat16 [65536, 3072], P(('ep', 'tp'))
- grad_up: bfloat16 [65536, 3072], P(('ep', 'tp'))
- grad_down: bfloat16 [65536, 3072], P(('ep', 'tp'))
Inputs may be any that keep to these rules, and one draw needn't show every extreme that they name: `expert_ids`: each row names 2 different experts. `pair_order`: each of the 64 sequence indices appears once.
All inputs are finite; a program needn't handle non-finite values.
Results may differ from a plain program's by a relative error of at most 0.014.
Values may be sent and summed in bfloat16 or wider, within the bound.
No kernel may reach another device: no remote copies, remote signals or barrier semaphores. Data moves between devices by JAX's collectives and lax.ppermute only.
A program may use at most 128 MiB of HBM per device.

v0:
```python
import math

import jax
import jax.numpy as jnp
from jax import lax
from jax.experimental import pallas as pl
from jax.experimental.pallas import tpu as pltpu
from jax.sharding import Mesh
from jax.sharding import PartitionSpec as P


EXPERTS = 8
SEQ_LEN = 64
EP = ("ep_x", "ep_z")
TP = ("tp_y", "tp_c")
EP_TP = EP + TP


loss_scale = 256.0
bf16, f32 = jnp.bfloat16, jnp.float32


def route_tables(expert_ids, route_share, capacity):
    experts_iota = jnp.arange(EXPERTS, dtype=jnp.int32)
    first_hot = (expert_ids[:, 0:1] == experts_iota[None, :]).astype(jnp.int32)
    second_hot = (expert_ids[:, 1:2] == experts_iota[None, :]).astype(jnp.int32)
    first_rank = jnp.sum((jnp.cumsum(first_hot, axis=0) - first_hot) * first_hot, axis=1)
    second_before = (
        jnp.cumsum(second_hot, axis=0) - second_hot + jnp.sum(first_hot, axis=0)[None, :]
    )
    second_rank = jnp.sum(second_before * second_hot, axis=1)
    route_ranks = jnp.stack([first_rank, second_rank], axis=1)
    route_kept = route_ranks < capacity
    half = capacity // 2
    slot_index = (route_ranks // half) * (EXPERTS * half) + expert_ids * half + route_ranks % half
    slot_index = jnp.where(route_kept, slot_index, -1)
    shares = jnp.stack([route_share, 1.0 - route_share], axis=1) * route_kept.astype(f32)
    slot_iota = jnp.arange(EXPERTS * capacity, dtype=jnp.int32)
    matches = (slot_index[:, :, None] == slot_iota[None, None, :]).astype(f32)
    picker = jnp.sum(matches, axis=1)
    mixing = jnp.sum(matches * shares[:, :, None], axis=1)
    return (picker, mixing)


def rot(value, shift):
    return lax.ppermute(value, "tp_y", [(i, (i + shift) % 4) for i in range(4)])


def swap(value):
    return lax.ppermute(value, "tp_c", [(0, 1), (1, 0)])


def exchange(blocks):
    arrived = lax.all_to_all(
        blocks.transpose(1, 0, 2), EP, split_axis=1, concat_axis=1, tiled=True
    )
    return arrived.transpose(1, 0, 2)


def gather_features(rows):
    half = rows.shape[0] // 2
    back, ahead = rot(rows, 1), rot(rows, -1)
    far_low, far_high = rot(back[:half], 1), rot(ahead[half:], -1)
    return (rows, ahead, far_low, far_high, back)


def add(*terms):
    return sum((t.astype(f32) for t in terms[1:]), terms[0].astype(f32)).astype(bf16)


def scatter_start(pieces):
    own, ahead, far_low, far_high, back = pieces
    half = far_low.shape[0]
    via_low, via_high = rot(far_low, 1), rot(far_high, -1)
    onward = jnp.concatenate([add(ahead[:half], via_low), ahead[half:]], axis=0)
    backward = jnp.concatenate([back[:half], add(back[half:], via_high)], axis=0)
    return own, rot(onward, 1), rot(backward, -1)


def piece_halves(refs):
    own, ahead, far_low, far_high, back = refs
    half = far_low.shape[0]
    low, high = pl.ds(0, half), pl.ds(half, half)
    return (
        (own.at[low], own.at[high]),
        (ahead.at[low], ahead.at[high]),
        (far_low, far_high),
        (back.at[low], back.at[high]),
    )


def load_piece(step, refs, rows):
    half = rows.shape[0] // 2
    for k, (low, high) in enumerate(piece_halves(refs)):

        @pl.when(step == k)
        def _(low=low, high=high):
            rows[pl.ds(0, half)] = low[...]
            rows[pl.ds(half, half)] = high[...]


def store_piece(step, refs, rows):
    half = rows.shape[0] // 2
    for k, (low, high) in enumerate(piece_halves(refs)):

        @pl.when(step == k)
        def _(low=low, high=high):
            low[...] = rows[pl.ds(0, half)]
            high[...] = rows[pl.ds(half, half)]


def cross(a, b):
    return lax.dot_general(a, b, (((1,), (1,)), ((), ())), preferred_element_type=f32)


def plain(a, b):
    return lax.dot_general(a, b, (((1,), (0,)), ((), ())), preferred_element_type=f32)


def fwd_kernel(y_ref, *refs):
    x_refs = refs[:5]
    wg0, wg1, wu0, wu1, rh_ref, meta_ref = refs[5:11]
    slope_ref, silu_ref, hidden_ref, score_ref = refs[11:15]
    gate_acc, up_acc, rows = refs[15:]
    width = wg0.shape[0]
    left, right = pl.ds(0, width), pl.ds(width, width)
    step = pl.program_id(0)

    @pl.when(step == 0)
    def _():
        gate_acc[...] = jnp.zeros_like(gate_acc)
        up_acc[...] = jnp.zeros_like(up_acc)

    load_piece(step, x_refs, rows)
    gate_acc[:, left] += cross(rows[...], wg0[...])
    gate_acc[:, right] += cross(rows[...], wg1[...])
    up_acc[:, left] += cross(rows[...], wu0[...])
    up_acc[:, right] += cross(rows[...], wu1[...])

    @pl.when(step == 3)
    def _():
        chunk = gate_acc.shape[0] // 8

        @pl.loop(0, 8)
        def _(i):
            at = pl.ds(pl.multiple_of(i * chunk, chunk), chunk)
            gate, up = gate_acc[at], up_acc[at]
            sig = jax.nn.sigmoid(gate)
            silu = gate * sig
            hidden = (silu * up).astype(bf16)
            silu_ref[at] = silu
            slope_ref[at] = up * (sig * (1.0 + gate * (1.0 - sig)))
            hidden_ref[at] = hidden
            score = jnp.sum(hidden.astype(f32) * rh_ref[...], axis=1, keepdims=True)
            gate_acc[at, pl.ds(0, 128)] = score * meta_ref[at].astype(f32)

        scores = gate_acc[:, pl.ds(0, 128)].reshape(score_ref.shape[0], -1, 128)
        scores = jnp.sum(scores, axis=1)
        lane = lax.broadcasted_iota(jnp.int32, scores.shape, 1)
        first = jnp.sum(jnp.where(lane < 2, scores, 0.0), axis=1, keepdims=True)
        second = jnp.sum(jnp.where(lane < 2, 0.0, scores), axis=1, keepdims=True)
        score_ref[...] = jnp.where(lane == 0, first, second)


def down_kernel(y_ref, hidden_ref, wd0, wd1, *refs):
    out_refs, rows = refs[:5], refs[5]
    width = wd0.shape[0]
    left, right = pl.ds(0, width), pl.ds(width, width)
    rows[...] = (
        plain(hidden_ref[:, left], wd0[...]) + plain(hidden_ref[:, right], wd1[...])
    ).astype(bf16)
    store_piece(pl.program_id(0), out_refs, rows)


def back_kernel(y_ref, *refs):
    u_refs, (wd0, wd1, out_ref, rows) = refs[:5], refs[5:]
    width = wd0.shape[0]
    left, right = pl.ds(0, width), pl.ds(width, width)
    step = pl.program_id(0)

    @pl.when(step == 0)
    def _():
        out_ref[...] = jnp.zeros_like(out_ref)

    load_piece(step, u_refs, rows)
    out_ref[:, left] += cross(rows[...], wd0[...])
    out_ref[:, right] += cross(rows[...], wd1[...])


def bwd_kernel(y_ref, *refs):
    wg0, wg1, wu0, wu1, rh_ref, meta_ref, seq_ref, partial_ref, slope_ref, silu_ref = refs[:10]
    gate_grad_ref, up_grad_ref, coef_ref = refs[10:13]
    out_refs, rows = refs[13:18], refs[18]
    width = wg0.shape[0]
    left, right = pl.ds(0, width), pl.ds(width, width)
    step = pl.program_id(0)

    @pl.when(step == 0)
    def _():
        count = partial_ref.shape[0]
        blocks = seq_ref.shape[0]
        lane = lax.broadcasted_iota(jnp.int32, (blocks, 128), 1)
        first = jnp.broadcast_to(seq_ref[:, pl.ds(0, 1)], lane.shape)
        second = jnp.broadcast_to(seq_ref[:, pl.ds(1, 1)], lane.shape)
        by_lane = jnp.where(lane < 2, first, jnp.where(lane < 4, second, 0.0))
        shares = meta_ref[...].astype(f32).reshape(blocks, count // blocks, 128)
        terms = (shares * by_lane[:, None, :]).reshape(count, 128)
        coef_ref[...] = jnp.sum(terms, axis=1, keepdims=True)
        chunk = count // 8

        @pl.loop(0, 8)
        def _(i):
            at = pl.ds(pl.multiple_of(i * chunk, chunk), chunk)
            hidden_grad = partial_ref[at] + coef_ref[at] * rh_ref[...]
            gate_grad_ref[at] = (hidden_grad * slope_ref[at]).astype(bf16)
            up_grad_ref[at] = (hidden_grad * silu_ref[at]).astype(bf16)

    rows[...] = (
        plain(gate_grad_ref[:, left], wg0[...])
        + plain(gate_grad_ref[:, right], wg1[...])
        + plain(up_grad_ref[:, left], wu0[...])
        + plain(up_grad_ref[:, right], wu1[...])
    ).astype(bf16)
    store_piece(step, out_refs, rows)


def grad_kernel(y_ref, *refs):
    x_refs, u_refs = refs[:5], refs[5:10]
    hidden_ref, gate_grad_ref, up_grad_ref, coef_ref, rh_ref = refs[10:15]
    own_refs, other_ref = refs[15:18], refs[18]
    left, rows = refs[19:]
    width = own_refs[0].shape[0]
    step = pl.program_id(0)

    @pl.when(step == 0)
    def _():
        for i, ref in enumerate((gate_grad_ref, up_grad_ref, hidden_ref)):
            left[i] = ref[...].T

    load_piece(step, x_refs, rows)
    for i in (0, 1, 2):
        if i == 2:
            load_piece(step, u_refs, rows)
            rows[...] = (rows[...].astype(f32) + coef_ref[...] * rh_ref[...]).astype(bf16)
        total = plain(left[i], rows[...])
        own_refs[i][...] = total[:width].astype(bf16)
        other_ref[pl.ds(i * width, width)] = total[width:].astype(bf16)


def whole(shape):
    return pl.BlockSpec(shape, lambda k, y: (0,) * len(shape))


def columns(width, block):
    return pl.BlockSpec((width, block), lambda k, y: (0, (y[0] + k) % 4))


def piece_specs(rows, block):
    full, part = whole((rows, block)), whole((rows // 2, block))
    return [full, full, part, part, full]


def piece_shapes(rows, block):
    full = jax.ShapeDtypeStruct((rows, block), bf16)
    part = jax.ShapeDtypeStruct((rows // 2, block), bf16)
    return [full, full, part, part, full]


def call(kernel, in_specs, out_specs, out_shape, scratch, flops, args):
    return pl.pallas_call(
        kernel,
        grid_spec=pltpu.PrefetchScalarGridSpec(
            num_scalar_prefetch=1,
            grid=(4,),
            in_specs=in_specs,
            out_specs=out_specs,
            scratch_shapes=scratch,
        ),
        out_shape=out_shape,
        compiler_params=pltpu.CompilerParams(
            dimension_semantics=("arbitrary",), vmem_limit_bytes=36 * 1024 * 1024
        ),
        cost_estimate=pl.CostEstimate(flops=flops, bytes_accessed=20_000_000, transcendentals=0),
    )(*args)


def layer(
    tokens, expert_ids, route_share, w_gate, w_up, w_down, reward_head, upstream, pair_order
):
    tok_count, local_width = tokens.shape
    capacity = tok_count * expert_ids.shape[1] // EXPERTS
    ep_size = lax.axis_size(EP)
    replicas = ep_size // EXPERTS
    half_cap = capacity // 2
    block = 2 * local_width
    rows = ep_size * half_cap
    hid = w_gate.shape[0]
    core = lax.axis_index("tp_c")
    place = lax.axis_index("tp_y").astype(jnp.int32).reshape(1)

    wg_other, wu_other, wd_other = swap(w_gate), swap(w_up), swap(w_down)

    picker, mixing = route_tables(expert_ids, route_share, capacity)
    seq_local = tok_count // SEQ_LEN
    over_tokens = (((0,), (0,)), ((), ()))
    both = lax.dot_general(
        picker.astype(bf16),
        jnp.concatenate([tokens, upstream], axis=1),
        over_tokens,
        preferred_element_type=f32,
    )
    slot_share = jnp.sum(mixing, axis=0)
    column = lax.broadcasted_iota(jnp.int32, (1, 2 * local_width), 1)
    both = both * jnp.where(column < local_width, 1.0, slot_share[:, None])
    both = both.astype(bf16).reshape(2, EXPERTS * half_cap, 2 * local_width)
    mine = lax.dynamic_index_in_dim(both, core, 0, keepdims=False)
    theirs = swap(lax.dynamic_index_in_dim(both, 1 - core, 0, keepdims=False))
    low = jnp.where(core == 0, mine, theirs)
    high = jnp.where(core == 0, theirs, mine)
    token_block = jnp.concatenate([low[:, :local_width], high[:, :local_width]], axis=1)
    grad_block = jnp.concatenate([low[:, local_width:], high[:, local_width:]], axis=1)

    token_seq = lax.broadcasted_iota(jnp.int32, (tok_count, 128), 0) // SEQ_LEN
    lane = lax.broadcasted_iota(jnp.int32, (tok_count, 128), 1)
    my_mixing = jnp.where(
        core == 0, mixing[:, : EXPERTS * half_cap], mixing[:, EXPERTS * half_cap :]
    )
    meta = lax.dot_general(
        my_mixing,
        (token_seq == lane // 2).astype(f32),
        over_tokens,
        precision=lax.Precision.HIGHEST,
        preferred_element_type=f32,
    )
    meta_high = lax.reduce_precision(meta, 8, 7)
    meta = jnp.where(lane[:1] % 2 == 0, meta_high, meta - meta_high).astype(bf16)
    grad_block = jnp.concatenate([grad_block, meta], axis=1)

    def to_experts(block_rows):
        width = block_rows.shape[1]
        block_rows = block_rows.reshape(EXPERTS, half_cap, width)
        return exchange(jnp.repeat(block_rows, replicas, axis=0)).reshape(rows, width)

    token_rows = to_experts(token_block)
    grad_full = to_experts(grad_block)

    head = lax.all_gather(reward_head, TP, axis=0, tiled=True)
    head_own = jnp.sum(w_down.astype(f32) * head[None, :], axis=1)
    head_other = jnp.sum(wd_other.astype(f32) * head[None, :], axis=1)
    head_row = jnp.concatenate([head_own, head_other])[None, :]
    local_scores = jnp.sum(tokens.astype(f32) * reward_head[None, :], axis=1)
    local_rewards = jnp.sum(local_scores.reshape(seq_local, SEQ_LEN), axis=1)
    seq_total = pair_order.shape[0]
    offset = lax.axis_index(EP) * seq_local
    placed = lax.dynamic_update_slice(jnp.zeros((seq_total,), f32), local_rewards, (offset,))
    token_rows, head_row, placed = lax.optimization_barrier((token_rows, head_row, placed))

    token_pieces = gather_features(token_rows)
    grad_pieces = gather_features(grad_full[:, :block])

    slots_hid = (rows, 2 * hid)
    meta_spec = pl.BlockSpec((rows, 128), lambda k, y: (0, block // 128))
    work = rows * 2 * hid * 4 * block
    slope, silu, hidden, score = call(
        fwd_kernel,
        piece_specs(rows, block)
        + [columns(hid, block)] * 4
        + [whole((1, 2 * hid)), meta_spec],
        [whole(slots_hid)] * 3 + [whole((ep_size, 128))],
        [jax.ShapeDtypeStruct(slots_hid, f32)] * 2
        + [jax.ShapeDtypeStruct(slots_hid, bf16), jax.ShapeDtypeStruct((ep_size, 128), f32)],
        [pltpu.VMEM(slots_hid, f32)] * 2 + [pltpu.VMEM((rows, block), bf16)],
        4 * work,
        (place, *token_pieces, w_gate, wg_other, w_up, wu_other, head_row, grad_full),
    )
    placed = (placed + score[:, :seq_local].reshape(seq_total)).reshape(2, 1, seq_total // 2)
    everyone = lax.axis_size(EP_TP)
    spread = jnp.broadcast_to(placed, (2, everyone, seq_total // 2))
    spread = lax.all_to_all(spread, EP_TP, split_axis=1, concat_axis=1, tiled=True)
    rewards = jnp.sum(spread, axis=1).reshape(seq_total) / math.sqrt(SEQ_LEN)

    down_pieces = call(
        down_kernel,
        [whole(slots_hid)] + [columns(hid, block)] * 2,
        piece_specs(rows, block),
        piece_shapes(rows, block),
        [pltpu.VMEM((rows, block), bf16)],
        2 * work,
        (place, hidden, w_down, wd_other),
    )
    partial = call(
        back_kernel,
        piece_specs(rows, block) + [columns(hid, block)] * 2,
        [whole(slots_hid)],
        [jax.ShapeDtypeStruct(slots_hid, f32)],
        [pltpu.VMEM((rows, block), bf16)],
        2 * work,
        (place, *grad_pieces, w_down, wd_other),
    )[0]
    down_sums = scatter_start(down_pieces)

    seq_iota = jnp.arange(seq_total, dtype=jnp.int32)
    chosen_hot = (pair_order[0::2][:, None] == seq_iota[None, :]).astype(f32)
    rejected_hot = (pair_order[1::2][:, None] == seq_iota[None, :]).astype(f32)
    margin = jnp.sum((chosen_hot - rejected_hot) * rewards[None, :], axis=1)
    pair_loss = jnp.mean(jax.nn.softplus(-margin))
    pair_weight = jax.nn.sigmoid(-margin)
    seq_coef = jnp.sum(pair_weight[:, None] * (rejected_hot - chosen_hot), axis=0)
    token_coef = jnp.repeat(lax.dynamic_slice_in_dim(seq_coef, offset, seq_local), SEQ_LEN)
    grad_out = (
        upstream.astype(f32)
        + loss_scale * token_coef[:, None] * reward_head[None, :] / math.sqrt(SEQ_LEN)
    ).astype(bf16)
    scaled = (seq_coef * (loss_scale / math.sqrt(SEQ_LEN))).reshape(ep_size, seq_local)

    gate_grad, up_grad, slot_coef, *input_pieces = call(
        bwd_kernel,
        [columns(hid, block)] * 4
        + [whole((1, 2 * hid)), meta_spec, whole((ep_size, seq_local))]
        + [whole(slots_hid)] * 3,
        [whole(slots_hid)] * 2 + [whole((rows, 1))] + piece_specs(rows, block),
        [jax.ShapeDtypeStruct(slots_hid, bf16)] * 2
        + [jax.ShapeDtypeStruct((rows, 1), f32)]
        + piece_shapes(rows, block),
        [pltpu.VMEM((rows, block), bf16)],
        4 * work,
        (place, w_gate, wg_other, w_up, wu_other, head_row, grad_full, scaled)
        + (partial, slope, silu),
    )
    input_sums = scatter_start(input_pieces)

    *own_grads, other_grads = call(
        grad_kernel,
        piece_specs(rows, block) * 2
        + [whole(slots_hid)] * 3
        + [whole((rows, 1)), columns(1, block)],
        [columns(hid, block)] * 3 + [columns(3 * hid, block)],
        [jax.ShapeDtypeStruct((hid, 4 * block), bf16)] * 3
        + [jax.ShapeDtypeStruct((3 * hid, 4 * block), bf16)],
        [pltpu.VMEM((3, 2 * hid, rows), bf16), pltpu.VMEM((rows, block), bf16)],
        6 * work,
        (place, *token_pieces, *grad_pieces, hidden, gate_grad, up_grad, slot_coef, head[None, :]),
    )
    other_grads = swap(other_grads)
    grad_gate, grad_up, grad_down = (
        add(own, other_grads[i * hid : (i + 1) * hid]) for i, own in enumerate(own_grads)
    )

    def come_back(pieces):
        arrived = exchange(add(*pieces).reshape(ep_size, half_cap, block)).astype(f32)
        sums = jnp.sum(arrived.reshape(EXPERTS, replicas, half_cap, block), axis=1)
        sums = sums.astype(bf16).reshape(EXPERTS * half_cap, block)
        left, right = sums[:, :local_width], sums[:, local_width:]
        mine = jnp.where(core == 0, left, right)
        theirs = swap(jnp.where(core == 0, right, left))
        return jnp.concatenate(
            [jnp.where(core == 0, mine, theirs), jnp.where(core == 0, theirs, mine)], axis=0
        )

    mixed_sum = plain(mixing, come_back(down_sums).astype(f32))
    layer_out = (tokens.astype(f32) + mixed_sum).astype(bf16)
    returned = plain(picker.astype(bf16), come_back(input_sums))
    grad_tokens = (grad_out.astype(f32) + returned).astype(bf16)
    return (layer_out, rewards, pair_loss, grad_tokens, grad_gate, grad_up, grad_down)


def solution(mesh):
    split = Mesh(mesh.devices.reshape(4, 8, 4, 2), EP_TP)
    in_specs = (
        P(EP, TP),
        P(EP, None),
        P(EP),
        P(EP_TP, None),
        P(EP_TP, None),
        P(EP_TP, None),
        P(TP),
        P(EP, TP),
        P(),
    )
    out_specs = (P(EP, TP), P(), P(), P(EP, TP), P(EP_TP, None), P(EP_TP, None), P(EP_TP, None))
    return jax.shard_map(layer, mesh=split, in_specs=in_specs, out_specs=out_specs, check_vma=False)
```

profile of v0, /device:TPU:32, one launch (start us, length us, event | category | flops | bytes accessed | tf_op | source)
XLA Modules:
  0.0 283.3 jit_solution(8853349349762309643)
XLA Ops:
  4.4 1.3 fusion
  5.9 1.4 collective-permute-done
  9.0 11.2 %all-to-all-start = ((bf16[16,32,768]{2,0,1:T(8,128)(2,1)}), bf16[16,32,768]{2,0,1:T(8,128)(2,1)}, u32[]{:S(2)}, u32[]{:S(2)}) async-start(bf16[16,32,768]{2,0,1:T(8,128)(2,1)} %bitcast.12), calls=%async_computation | async-start | bytes 1572864 | tf_op jit(solution)/shard_map/all_to_all | solution.py:54
  21.8 21.7 %all-to-all-done = bf16[16,32,768]{2,0,1:T(8,128)(2,1)} async-done(((bf16[16,32,768]{2,0,1:T(8,128)(2,1)}), bf16[16,32,768]{2,0,1:T(8,128)(2,1)}, u32[]{:S(2)}, u32[]{:S(2)}) %all-to-all-start) | async-done | bytes 786464 | tf_op jit(solution)/shard_map/all_to_all | solution.py:54
  44.6 5.2 %all-to-all-start.1 = ((bf16[16,32,896]{2,0,1:T(8,128)(2,1)}), bf16[16,32,896]{2,0,1:T(8,128)(2,1)}, u32[]{:S(2)}, u32[]{:S(2)}) async-start(bf16[16,32,896]{2,0,1:T(8,128)(2,1)} %bitcast.58), calls=%async_computation.1 | async-start | bytes 1835008 | tf_op jit(solution)/shard_map/all_to_all | solution.py:54
  51.9 12.1 %all-gather = f32[8,1,384]{2,1,0:T(1,128)S(1)} all-gather(f32[1,1,384]{2,1,0:T(1,128)S(1)} %reshape.176), channel_id=1, replica_groups=mesh['ep_x'=4,'ep_z'=8,'tp_y'=4,'tp_c'=2] {'tp_y','tp_c'}, dimensions={0}, use_global_device_ids=true | all-gather | bytes 13824 | tf_op jit(solution)/shard_map/all_gather | solution.py:347
  64.6 1.4 collective-permute-start.3
  66.5 2.0 collective-permute-start.2
  68.5 6.8 %all-to-all-done.1 = bf16[16,32,896]{2,0,1:T(8,128)(2,1)} async-done(((bf16[16,32,896]{2,0,1:T(8,128)(2,1)}), bf16[16,32,896]{2,0,1:T(8,128)(2,1)}, u32[]{:S(2)}, u32[]{:S(2)}) %all-to-all-start.1) | async-done | bytes 917536 | tf_op jit(solution)/shard_map/all_to_all | solution.py:54
  75.2 2.1 slice.135.refs_0_.refs_5_
  77.3 1.6 collective-permute-start.14
  78.9 7.7 %collective-permute-done.3.refs_4_ = bf16[512,768]{1,0:T(8,128)(2,1)} collective-permute-done((bf16[512,768]{1,0:T(8,128)(2,1)}, bf16[512,768]{1,0:T(8,128)(2,1)}, u32[]{:S(2)}, u32[]{:S(2)}) %collective-permute-start.3) | collective-permute-done | bytes 786464 | tf_op jit(solution)/shard_map/ppermute | solution.py:46
  87.3 1.8 slice.127
  89.1 1.4 collective-permute-start.4
  90.4 1.8 slice.128
  92.2 11.3 %collective-permute-done.14.refs_4_.refs_9_ = bf16[512,768]{1,0:T(8,128)(2,1)} collective-permute-done((bf16[512,768]{1,0:T(8,128)(2,1)}, bf16[512,768]{1,0:T(8,128)(2,1)}, u32[]{:S(2)}, u32[]{:S(2)}) %collective-permute-start.14) | collective-permute-done | bytes 786464 | tf_op jit(solution)/shard_map/ppermute | solution.py:46
  105.6 1.8 slice.136
  107.3 1.4 collective-permute-start.15
  108.7 1.8 slice.137
  110.5 1.9 collective-permute-start.16
  112.4 3.3 %collective-permute-done.5.refs_3_ = bf16[256,768]{1,0:T(8,128)(2,1)} collective-permute-done((bf16[256,768]{1,0:T(8,128)(2,1)}, bf16[256,768]{1,0:T(8,128)(2,1)}, u32[]{:S(2)}, u32[]{:S(2)}) %collective-permute-start.5) | collective-permute-done | bytes 393248 | tf_op jit(solution)/shard_map/ppermute | solution.py:46
  115.7 8.6 %shard_map.144 = (f32[512,512]{1,0:T(8,128)S(1)}, f32[512,512]{1,0:T(8,128)S(1)}, bf16[512,512]{1,0:T(8,128)(2,1)S(1)}, f32[32,128]{1,0:T(8,128)S(1)}) custom-call(s32[1]{0:T(128)} %bitcast.6.y_ref, bf16[512,768]{1,0:T(8,128)(2,1)} %bitcast.14.refs_0_, bf16[512,768]{1,0:T(8,128)(2,1)} %collective-permute-done.2.refs_1_, ...), custom_call_target="tpu_custom_call" | custom-call | flops 3221225472 | bytes 20000000 | tf_op jit(solution)/shard_map/pallas_call | solution.py:270
  127.6 1.3 reshape.172
  130.1 1.3 broadcast_in_dim.80
  131.4 1.4 broadcast_in_dim.81
  132.9 11.5 %all-to-all-start.3 = ((f32[2,256,32]{2,0,1:T(2,128)}), f32[2,256,32]{2,0,1:T(2,128)}, u32[]{:S(2)}, u32[]{:S(2)}) async-start(f32[2,256,32]{2,0,1:T(2,128)} %broadcast_in_dim.81), calls=%async_computation.3 | async-start | bytes 524288 | tf_op jit(solution)/shard_map/all_to_all | solution.py:379
  145.4 3.8 %shard_map.145 = (bf16[512,768]{1,0:T(8,128)(2,1)S(1)}, bf16[512,768]{1,0:T(8,128)(2,1)S(1)}, bf16[256,768]{1,0:T(8,128)(2,1)}, bf16[256,768]{1,0:T(8,128)(2,1)}, bf16[512,768]{1,0:T(8,128)(2,1)S(1)}) custom-call(s32[1]{0:T(128)} %bitcast.6.y_ref, bf16[512,512]{1,0:T(8,128)(2,1)S(1)} %copy-done.20, bf16[256,3072]{1,0:T(8,128)(2,1)S(1)} %copy-done, ...), custom_call_target="tpu_custom_call" | custom-call | flops 1610612736 | bytes 20000000 | tf_op jit(solution)/shard_map/pallas_call | solution.py:270
  150.1 2.9 %collective-permute-start.10 = (bf16[256,768]{1,0:T(8,128)(2,1)}, bf16[256,768]{1,0:T(8,128)(2,1)}, u32[]{:S(2)}, u32[]{:S(2)}) collective-permute-start(bf16[256,768]{1,0:T(8,128)(2,1)} %get-tuple-element.38), channel_id=1, source_target_pairs={{0,6},{2,0},{4,2},{6,4},{1,7},{3,1},{5,3},{7,5},{8,14},{10,8},{12,... | collective-permute-start | bytes 1179656 | tf_op jit(solution)/shard_map/ppermute | solution.py:46
  154.6 3.4 %all-to-all-done.3 = f32[2,256,32]{2,0,1:T(2,128)} async-done(((f32[2,256,32]{2,0,1:T(2,128)}), f32[2,256,32]{2,0,1:T(2,128)}, u32[]{:S(2)}, u32[]{:S(2)}) %all-to-all-start.3) | async-done | bytes 65568 | tf_op jit(solution)/shard_map/all_to_all | solution.py:379
  158.0 1.8 reduce_sum.155
  161.0 1.3 div.59
  165.7 1.4 mul.137.refs_6_
  167.1 4.9 %shard_map.146.refs_7_ = f32[512,512]{1,0:T(8,128)S(1)} custom-call(s32[1]{0:T(128)} %bitcast.6.y_ref, bf16[512,768]{1,0:T(8,128)(2,1)} %slice.135.refs_0_.refs_5_, bf16[512,768]{1,0:T(8,128)(2,1)} %collective-permute-done.13.refs_1_.refs_6_, bf16[256,768]{1,0:T(8,128)(2,1)S(1)} %collective-permute-done.15.refs_2_.refs_7_, ...), custom_call_target="tpu_custom_call" | custom-call | flops 1610612736 | bytes 20000000 | tf_op jit(solution)/shard_map/pallas_call | solution.py:270
  173.4 1.9 collective-permute-start.11
  176.7 7.9 %shard_map.147 = (bf16[512,512]{1,0:T(8,128)(2,1)S(1)}, bf16[512,512]{1,0:T(8,128)(2,1)S(1)}, f32[512,1]{1,0:T(8,128)S(1)}, bf16[512,768]{1,0:T(8,128)(2,1)S(1)}...) custom-call(s32[1]{0:T(128)} %bitcast.6.y_ref, ...), custom_call_target="tpu_custom_call" | custom-call | flops 3221225472 | bytes 20000000 | tf_op jit(solution)/shard_map/pallas_call | solution.py:270
  184.7 3.1 %collective-permute-start.19 = (bf16[256,768]{1,0:T(8,128)(2,1)S(1)}, bf16[256,768]{1,0:T(8,128)(2,1)S(1)}, u32[]{:S(2)}, u32[]{:S(2)}) collective-permute-start(bf16[256,768]{1,0:T(8,128)(2,1)S(1)} %get-tuple-element.47), channel_id=1, source_target_pairs={{0,6},{2,0},{4,2},{6,4},{1,7},{3,1},{5,3},{7,5},{8,14},{10,8},{12,... | collective-permute-start | bytes 1179656 | tf_op jit(solution)/shard_map/ppermute | solution.py:46
  189.4 13.3 %shard_map.148 = (bf16[256,3072]{1,0:T(8,128)(2,1)S(1)}, bf16[256,3072]{1,0:T(8,128)(2,1)S(1)}, bf16[256,3072]{1,0:T(8,128)(2,1)S(1)}, bf16[768,3072]{1,0:T(8,128)(2,1)}) custom-call(s32[1]{0:T(128)} %bitcast.6.y_ref, bf16[512,768]{1,0:T(8,128)(2,1)} %bitcast.14.refs_0_, bf16[512,768]{1,0:T(8,128)(2,1)} %collective-permute-done.2.refs_1_, ...), custom_call_target="tpu_custom_call" | custom-call | flops 4831838208 | bytes 20000000 | tf_op jit(solution)/shard_map/pallas_call | solution.py:270
  205.5 8.8 %all-to-all-start.2 = ((bf16[16,32,768]{2,0,1:T(8,128)(2,1)}), bf16[16,32,768]{2,0,1:T(8,128)(2,1)}, u32[]{:S(2)}, u32[]{:S(2)}) async-start(bf16[16,32,768]{2,0,1:T(8,128)(2,1)} %bitcast.59), calls=%async_computation.2 | async-start | bytes 1572864 | tf_op jit(solution)/shard_map/all_to_all | solution.py:54
  215.5 3.3 %collective-permute-start.20 = (bf16[512,768]{1,0:T(8,128)(2,1)S(1)}, bf16[512,768]{1,0:T(8,128)(2,1)S(1)}, u32[]{:S(2)}, u32[]{:S(2)}) collective-permute-start(bf16[512,768]{1,0:T(8,128)(2,1)S(1)} %pad_maximum_fusion.3), channel_id=1, source_target_pairs={{0,6},{2,0},{4,2},{6,4},{1,7},{3,1},{5,3},{7,5},{8,14},{10,8},{12,... | collective-permute-start | bytes 2359304 | tf_op jit(solution)/shard_map/ppermute | solution.py:46
  220.1 15.0 %collective-permute-done.20 = bf16[512,768]{1,0:T(8,128)(2,1)S(1)} collective-permute-done((bf16[512,768]{1,0:T(8,128)(2,1)S(1)}, bf16[512,768]{1,0:T(8,128)(2,1)S(1)}, u32[]{:S(2)}, u32[]{:S(2)}) %collective-permute-start.20) | collective-permute-done | bytes 786464 | tf_op jit(solution)/shard_map/ppermute | solution.py:46
  235.0 4.7 %collective-permute-done.18 = bf16[512,768]{1,0:T(8,128)(2,1)S(1)} collective-permute-done((bf16[512,768]{1,0:T(8,128)(2,1)S(1)}, bf16[512,768]{1,0:T(8,128)(2,1)S(1)}, u32[]{:S(2)}, u32[]{:S(2)}) %collective-permute-start.18) | collective-permute-done | bytes 786464 | tf_op jit(solution)/shard_map/ppermute | solution.py:46
  240.9 9.8 %all-to-all-start.4 = ((bf16[16,32,768]{2,0,1:T(8,128)(2,1)}), bf16[16,32,768]{2,0,1:T(8,128)(2,1)}, u32[]{:S(2)}, u32[]{:S(2)}) async-start(bf16[16,32,768]{2,0,1:T(8,128)(2,1)} %bitcast.60), calls=%async_computation.4 | async-start | bytes 1572864 | tf_op jit(solution)/shard_map/all_to_all | solution.py:54
  250.7 1.3 bitcast_reduce_fusion.1
  254.3 1.6 broadcast_select_fusion.5
  255.9 16.3 %all-to-all-done.4 = bf16[16,32,768]{2,0,1:T(8,128)(2,1)} async-done(((bf16[16,32,768]{2,0,1:T(8,128)(2,1)}), bf16[16,32,768]{2,0,1:T(8,128)(2,1)}, u32[]{:S(2)}, u32[]{:S(2)}) %all-to-all-start.4) | async-done | bytes 786464 | tf_op jit(solution)/shard_map/all_to_all | solution.py:54
  272.2 1.4 bitcast_reduce_fusion
  273.7 1.8 fusion.1
  276.4 5.8 %add_convert_fusion = (bf16[256,3072]{1,0:T(8,128)(2,1)}, bf16[256,3072]{1,0:T(8,128)(2,1)}, bf16[256,3072]{1,0:T(8,128)(2,1)}) fusion(bf16[256,3072]{1,0:T(8,128)(2,1)S(1)} %copy-done.2, bf16[768,3072]{1,0:T(8,128)(2,1)} %collective-permute-done.22, bf16[256,3072]{1,0:T(8,128)(2,1)S(1)} %get-tuple-element.53, bf16[256,3072]{1,0:T(8,128)(2,1)S(1)} %get-tuple-element.51), kind=kLoop, calls=%fused_computation | loop fusion | flops 9437184 | bytes 14155776 | tf_op jit(solution)/shard_map/convert_element_type | solution.py:68
  (167 shorter events, 40.1 us)
Async XLA Ops:
  4.4 16.0 %copy-start.26 = (f32[128,256]{1,0:T(8,128)}, f32[128,256]{1,0:T(8,128)S(1)}, u32[]{:S(2)}) copy-start(f32[128,256]{1,0:T(8,128)S(1)} %get-tuple-element.58) | copy-start | bytes 393220
  5.8 1.5 collective-permute-start
  8.0 12.2 %copy-start = (bf16[256,3072]{1,0:T(8,128)(2,1)S(1)}, bf16[256,3072]{1,0:T(8,128)(2,1)}, u32[]{:S(2)}) copy-start(bf16[256,3072]{1,0:T(8,128)(2,1)} %refs_5_.3) | copy-start | bytes 4718596
  9.0 34.6 %all-to-all-start = ((bf16[16,32,768]{2,0,1:T(8,128)(2,1)}), bf16[16,32,768]{2,0,1:T(8,128)(2,1)}, u32[]{:S(2)}, u32[]{:S(2)}) async-start(bf16[16,32,768]{2,0,1:T(8,128)(2,1)} %bitcast.12), calls=%async_computation | async-start | bytes 1572864 | tf_op jit(solution)/shard_map/all_to_all | solution.py:54
  20.2 43.7 %collective-permute-start.1 = (bf16[256,3072]{1,0:T(8,128)(2,1)S(1)}, bf16[256,3072]{1,0:T(8,128)(2,1)S(1)}, u32[]{:S(2)}, u32[]{:S(2)}) collective-permute-start(bf16[256,3072]{1,0:T(8,128)(2,1)S(1)} %copy-done), channel_id=1, source_target_pairs={{0,1},{1,0},{2,3},{3,2},{4,5},{5,4},{6,7},{7,6},{8,9},{9,8},{10,11... | collective-permute-start | bytes 4718600 | tf_op jit(solution)/shard_map/ppermute | solution.py:50
  21.8 27.9 %copy-start.31 = (f32[384]{0:T(512)S(1)}, f32[384]{0:T(512)}, u32[]{:S(2)}) copy-start(f32[384]{0:T(512)} %param.15) | copy-start | bytes 4612
  21.8 28.0 %copy-start.28 = (bf16[128,384]{1,0:T(8,128)(2,1)S(1)}, bf16[128,384]{1,0:T(8,128)(2,1)}, u32[]{:S(2)}) copy-start(bf16[128,384]{1,0:T(8,128)(2,1)} %param.9) | copy-start | bytes 294916
  44.6 30.7 %all-to-all-start.1 = ((bf16[16,32,896]{2,0,1:T(8,128)(2,1)}), bf16[16,32,896]{2,0,1:T(8,128)(2,1)}, u32[]{:S(2)}, u32[]{:S(2)}) async-start(bf16[16,32,896]{2,0,1:T(8,128)(2,1)} %bitcast.58), calls=%async_computation.1 | async-start | bytes 1835008 | tf_op jit(solution)/shard_map/all_to_all | solution.py:54
  64.6 22.0 %collective-permute-start.3 = (bf16[512,768]{1,0:T(8,128)(2,1)}, bf16[512,768]{1,0:T(8,128)(2,1)}, u32[]{:S(2)}, u32[]{:S(2)}) collective-permute-start(bf16[512,768]{1,0:T(8,128)(2,1)} %bitcast.14.refs_0_), channel_id=1, source_target_pairs={{0,2},{2,4},{4,6},{6,0},{1,3},{3,5},{5,7},{7,1},{8,10},{10,12},{12... | collective-permute-start | bytes 2359304 | tf_op jit(solution)/shard_map/ppermute | solution.py:46
  66.0 44.5 %collective-permute-start.6 = (bf16[256,3072]{1,0:T(8,128)(2,1)}, bf16[256,3072]{1,0:T(8,128)(2,1)}, u32[]{:S(2)}, u32[]{:S(2)}) collective-permute-start(bf16[256,3072]{1,0:T(8,128)(2,1)} %refs_0_.1), channel_id=1, source_target_pairs={{0,1},{1,0},{2,3},{3,2},{4,5},{5,4},{6,7},{7,6},{8,9},{9,8},{10,11... | collective-permute-start | bytes 4718600 | tf_op jit(solution)/shard_map/ppermute | solution.py:50
  66.1 46.3 %collective-permute-start.7 = (bf16[256,3072]{1,0:T(8,128)(2,1)}, bf16[256,3072]{1,0:T(8,128)(2,1)}, u32[]{:S(2)}, u32[]{:S(2)}) collective-permute-start(bf16[256,3072]{1,0:T(8,128)(2,1)} %refs_2_.1), channel_id=1, source_target_pairs={{0,1},{1,0},{2,3},{3,2},{4,5},{5,4},{6,7},{7,6},{8,9},{9,8},{10,11... | collective-permute-start | bytes 4718600 | tf_op jit(solution)/shard_map/ppermute | solution.py:50
  66.5 22.6 %collective-permute-start.2 = (bf16[512,768]{1,0:T(8,128)(2,1)}, bf16[512,768]{1,0:T(8,128)(2,1)}, u32[]{:S(2)}, u32[]{:S(2)}) collective-permute-start(bf16[512,768]{1,0:T(8,128)(2,1)} %bitcast.14.refs_0_), channel_id=1, source_target_pairs={{0,6},{2,0},{4,2},{6,4},{1,7},{3,1},{5,3},{7,5},{8,14},{10,8},{12,... | collective-permute-start | bytes 2359304 | tf_op jit(solution)/shard_map/ppermute | solution.py:46
  75.2 28.9 %copy-start.36 = (s32[64]{0:T(128)S(1)}, s32[64]{0:T(128)}, u32[]{:S(2)}) copy-start(s32[64]{0:T(128)} %param.17) | copy-start | bytes 772
  77.3 26.2 %collective-permute-start.14 = (bf16[512,768]{1,0:T(8,128)(2,1)}, bf16[512,768]{1,0:T(8,128)(2,1)}, u32[]{:S(2)}, u32[]{:S(2)}) collective-permute-start(bf16[512,768]{1,0:T(8,128)(2,1)} %slice.135.refs_0_.refs_5_), channel_id=1, source_target_pairs={{0,2},{2,4},{4,6},{6,0},{1,3},{3,5},{5,7},{7,1},{8,10},{10,12},{12... | collective-permute-start | bytes 2359304 | tf_op jit(solution)/shard_map/ppermute | solution.py:46
  86.6 20.7 %collective-permute-start.13 = (bf16[512,768]{1,0:T(8,128)(2,1)}, bf16[512,768]{1,0:T(8,128)(2,1)}, u32[]{:S(2)}, u32[]{:S(2)}) collective-permute-start(bf16[512,768]{1,0:T(8,128)(2,1)} %slice.135.refs_0_.refs_5_), channel_id=1, source_target_pairs={{0,6},{2,0},{4,2},{6,4},{1,7},{3,1},{5,3},{7,5},{8,14},{10,8},{12,... | collective-permute-start | bytes 2359304 | tf_op jit(solution)/shard_map/ppermute | solution.py:46
  89.1 23.3 %collective-permute-start.4 = (bf16[256,768]{1,0:T(8,128)(2,1)}, bf16[256,768]{1,0:T(8,128)(2,1)}, u32[]{:S(2)}, u32[]{:S(2)}) collective-permute-start(bf16[256,768]{1,0:T(8,128)(2,1)} %slice.127), channel_id=1, source_target_pairs={{0,2},{2,4},{4,6},{6,0},{1,3},{3,5},{5,7},{7,1},{8,10},{10,12},{12... | collective-permute-start | bytes 1179656 | tf_op jit(solution)/shard_map/ppermute | solution.py:46
  103.5 12.2 %collective-permute-start.5 = (bf16[256,768]{1,0:T(8,128)(2,1)}, bf16[256,768]{1,0:T(8,128)(2,1)}, u32[]{:S(2)}, u32[]{:S(2)}) collective-permute-start(bf16[256,768]{1,0:T(8,128)(2,1)} %slice.128), channel_id=1, source_target_pairs={{0,6},{2,0},{4,2},{6,4},{1,7},{3,1},{5,3},{7,5},{8,14},{10,8},{12,... | collective-permute-start | bytes 1179656 | tf_op jit(solution)/shard_map/ppermute | solution.py:46
  107.3 59.8 %collective-permute-start.15 = (bf16[256,768]{1,0:T(8,128)(2,1)}, bf16[256,768]{1,0:T(8,128)(2,1)S(1)}, u32[]{:S(2)}, u32[]{:S(2)}) collective-permute-start(bf16[256,768]{1,0:T(8,128)(2,1)} %slice.136), channel_id=1, source_target_pairs={{0,2},{2,4},{4,6},{6,0},{1,3},{3,5},{5,7},{7,1},{8,10},{10,12},{12... | collective-permute-start | bytes 1179656 | tf_op jit(solution)/shard_map/ppermute | solution.py:46
  110.5 56.7 %collective-permute-start.16 = (bf16[256,768]{1,0:T(8,128)(2,1)}, bf16[256,768]{1,0:T(8,128)(2,1)}, u32[]{:S(2)}, u32[]{:S(2)}) collective-permute-start(bf16[256,768]{1,0:T(8,128)(2,1)} %slice.137), channel_id=1, source_target_pairs={{0,6},{2,0},{4,2},{6,4},{1,7},{3,1},{5,3},{7,5},{8,14},{10,8},{12,... | collective-permute-start | bytes 1179656 | tf_op jit(solution)/shard_map/ppermute | solution.py:46
  132.9 25.1 %all-to-all-start.3 = ((f32[2,256,32]{2,0,1:T(2,128)}), f32[2,256,32]{2,0,1:T(2,128)}, u32[]{:S(2)}, u32[]{:S(2)}) async-start(f32[2,256,32]{2,0,1:T(2,128)} %broadcast_in_dim.81), calls=%async_computation.3 | async-start | bytes 524288 | tf_op jit(solution)/shard_map/all_to_all | solution.py:379
  150.1 4.4 %copy-start.7 = (bf16[512,768]{1,0:T(8,128)(2,1)}, bf16[512,768]{1,0:T(8,128)(2,1)S(1)}, u32[]{:S(2)}) copy-start(bf16[512,768]{1,0:T(8,128)(2,1)S(1)} %get-tuple-element.37) | copy-start | bytes 2359300
  150.1 22.0 %collective-permute-start.10 = (bf16[256,768]{1,0:T(8,128)(2,1)}, bf16[256,768]{1,0:T(8,128)(2,1)}, u32[]{:S(2)}, u32[]{:S(2)}) collective-permute-start(bf16[256,768]{1,0:T(8,128)(2,1)} %get-tuple-element.38), channel_id=1, source_target_pairs={{0,6},{2,0},{4,2},{6,4},{1,7},{3,1},{5,3},{7,5},{8,14},{10,8},{12,... | collective-permute-start | bytes 1179656 | tf_op jit(solution)/shard_map/ppermute | solution.py:46
  154.6 20.7 %collective-permute-start.8 = (bf16[256,768]{1,0:T(8,128)(2,1)}, bf16[256,768]{1,0:T(8,128)(2,1)}, u32[]{:S(2)}, u32[]{:S(2)}) collective-permute-start(bf16[256,768]{1,0:T(8,128)(2,1)} %get-tuple-element.36), channel_id=1, source_target_pairs={{0,2},{2,4},{4,6},{6,0},{1,3},{3,5},{5,7},{7,1},{8,10},{10,12},{12... | collective-permute-start | bytes 1179656 | tf_op jit(solution)/shard_map/ppermute | solution.py:46
  167.1 5.0 %copy-start.8 = (bf16[512,768]{1,0:T(8,128)(2,1)S(1)}, bf16[512,768]{1,0:T(8,128)(2,1)}, u32[]{:S(2)}) copy-start(bf16[512,768]{1,0:T(8,128)(2,1)} %copy-done.7) | copy-start | bytes 2359300
  167.1 6.1 %copy-start.25 = (bf16[256,768]{1,0:T(8,128)(2,1)S(1)}, bf16[256,768]{1,0:T(8,128)(2,1)}, u32[]{:S(2)}) copy-start(bf16[256,768]{1,0:T(8,128)(2,1)} %slice.106) | copy-start | bytes 1179652
  173.4 30.3 %collective-permute-start.11 = (bf16[512,768]{1,0:T(8,128)(2,1)S(1)}, bf16[512,768]{1,0:T(8,128)(2,1)S(1)}, u32[]{:S(2)}, u32[]{:S(2)}) collective-permute-start(bf16[512,768]{1,0:T(8,128)(2,1)S(1)} %pad_maximum_fusion.1), channel_id=1, source_target_pairs={{0,6},{2,0},{4,2},{6,4},{1,7},{3,1},{5,3},{7,5},{8,14},{10,8},{12,... | collective-permute-start | bytes 2359304 | tf_op jit(solution)/shard_map/ppermute | solution.py:46
  176.4 27.2 %collective-permute-start.9 = (bf16[512,768]{1,0:T(8,128)(2,1)S(1)}, bf16[512,768]{1,0:T(8,128)(2,1)S(1)}, u32[]{:S(2)}, u32[]{:S(2)}) collective-permute-start(bf16[512,768]{1,0:T(8,128)(2,1)S(1)} %pad_maximum_fusion), channel_id=1, source_target_pairs={{0,2},{2,4},{4,6},{6,0},{1,3},{3,5},{5,7},{7,1},{8,10},{10,12},{12... | collective-permute-start | bytes 2359304 | tf_op jit(solution)/shard_map/ppermute | solution.py:46
  184.7 4.7 %copy-start.3 = (bf16[512,768]{1,0:T(8,128)(2,1)}, bf16[512,768]{1,0:T(8,128)(2,1)S(1)}, u32[]{:S(2)}) copy-start(bf16[512,768]{1,0:T(8,128)(2,1)S(1)} %get-tuple-element.44) | copy-start | bytes 2359300
  184.7 18.0 %copy-start.11 = (bf16[512,768]{1,0:T(8,128)(2,1)}, bf16[512,768]{1,0:T(8,128)(2,1)S(1)}, u32[]{:S(2)}) copy-start(bf16[512,768]{1,0:T(8,128)(2,1)S(1)} %get-tuple-element.43) | copy-start | bytes 2359300
  184.7 4.7 %copy-start.21 = (bf16[512,512]{1,0:T(8,128)(2,1)S(1)}, bf16[512,512]{1,0:T(8,128)(2,1)}, u32[]{:S(2)}) copy-start(bf16[512,512]{1,0:T(8,128)(2,1)} %copy-done.19) | copy-start | bytes 1572868
  184.7 18.1 %collective-permute-start.19 = (bf16[256,768]{1,0:T(8,128)(2,1)S(1)}, bf16[256,768]{1,0:T(8,128)(2,1)S(1)}, u32[]{:S(2)}, u32[]{:S(2)}) collective-permute-start(bf16[256,768]{1,0:T(8,128)(2,1)S(1)} %get-tuple-element.47), channel_id=1, source_target_pairs={{0,6},{2,0},{4,2},{6,4},{1,7},{3,1},{5,3},{7,5},{8,14},{10,8},{12,... | collective-permute-start | bytes 1179656 | tf_op jit(solution)/shard_map/ppermute | solution.py:46
  189.3 29.5 %collective-permute-start.17 = (bf16[256,768]{1,0:T(8,128)(2,1)}, bf16[256,768]{1,0:T(8,128)(2,1)}, u32[]{:S(2)}, u32[]{:S(2)}) collective-permute-start(bf16[256,768]{1,0:T(8,128)(2,1)} %get-tuple-element.45), channel_id=1, source_target_pairs={{0,2},{2,4},{4,6},{6,0},{1,3},{3,5},{5,7},{7,1},{8,10},{10,12},{12... | collective-permute-start | bytes 1179656 | tf_op jit(solution)/shard_map/ppermute | solution.py:46
  202.6 73.8 %collective-permute-start.22 = (bf16[768,3072]{1,0:T(8,128)(2,1)}, bf16[768,3072]{1,0:T(8,128)(2,1)}, u32[]{:S(2)}, u32[]{:S(2)}) collective-permute-start(bf16[768,3072]{1,0:T(8,128)(2,1)} %get-tuple-element.52), channel_id=1, source_target_pairs={{0,1},{1,0},{2,3},{3,2},{4,5},{5,4},{6,7},{7,6},{8,9},{9,8},{10,11... | collective-permute-start | bytes 14155784 | tf_op jit(solution)/shard_map/ppermute | solution.py:50
  205.5 8.8 %copy-start.24 = (bf16[256,768]{1,0:T(8,128)(2,1)S(1)}, bf16[256,768]{1,0:T(8,128)(2,1)}, u32[]{:S(2)}) copy-start(bf16[256,768]{1,0:T(8,128)(2,1)} %slice.118) | copy-start | bytes 1179652
  205.5 35.4 %all-to-all-start.2 = ((bf16[16,32,768]{2,0,1:T(8,128)(2,1)}), bf16[16,32,768]{2,0,1:T(8,128)(2,1)}, u32[]{:S(2)}, u32[]{:S(2)}) async-start(bf16[16,32,768]{2,0,1:T(8,128)(2,1)} %bitcast.59), calls=%async_computation.2 | async-start | bytes 1572864 | tf_op jit(solution)/shard_map/all_to_all | solution.py:54
  214.3 4.5 %copy-start.4 = (bf16[512,768]{1,0:T(8,128)(2,1)S(1)}, bf16[512,768]{1,0:T(8,128)(2,1)}, u32[]{:S(2)}) copy-start(bf16[512,768]{1,0:T(8,128)(2,1)} %copy-done.3) | copy-start | bytes 2359300
  214.3 5.6 %copy-start.22 = (bf16[256,768]{1,0:T(8,128)(2,1)S(1)}, bf16[256,768]{1,0:T(8,128)(2,1)}, u32[]{:S(2)}) copy-start(bf16[256,768]{1,0:T(8,128)(2,1)} %slice.117) | copy-start | bytes 1179652
  215.5 24.2 %copy-start.12 = (bf16[512,768]{1,0:T(8,128)(2,1)S(1)}, bf16[512,768]{1,0:T(8,128)(2,1)}, u32[]{:S(2)}) copy-start(bf16[512,768]{1,0:T(8,128)(2,1)} %copy-done.11) | copy-start | bytes 2359300
  215.5 19.6 %collective-permute-start.20 = (bf16[512,768]{1,0:T(8,128)(2,1)S(1)}, bf16[512,768]{1,0:T(8,128)(2,1)S(1)}, u32[]{:S(2)}, u32[]{:S(2)}) collective-permute-start(bf16[512,768]{1,0:T(8,128)(2,1)S(1)} %pad_maximum_fusion.3), channel_id=1, source_target_pairs={{0,6},{2,0},{4,2},{6,4},{1,7},{3,1},{5,3},{7,5},{8,14},{10,8},{12,... | collective-permute-start | bytes 2359304 | tf_op jit(solution)/shard_map/ppermute | solution.py:46
  220.0 19.7 %collective-permute-start.18 = (bf16[512,768]{1,0:T(8,128)(2,1)S(1)}, bf16[512,768]{1,0:T(8,128)(2,1)S(1)}, u32[]{:S(2)}, u32[]{:S(2)}) collective-permute-start(bf16[512,768]{1,0:T(8,128)(2,1)S(1)} %pad_maximum_fusion.2), channel_id=1, source_target_pairs={{0,2},{2,4},{4,6},{6,0},{1,3},{3,5},{5,7},{7,1},{8,10},{10,12},{12... | collective-permute-start | bytes 2359304 | tf_op jit(solution)/shard_map/ppermute | solution.py:46
  240.9 11.8 %copy-start.34 = (f32[64]{0:T(128)S(1)}, f32[64]{0:T(128)}, u32[]{:S(2)}) copy-start(f32[64]{0:T(128)} %copy-done.33) | copy-start | bytes 772
  240.9 31.3 %all-to-all-start.4 = ((bf16[16,32,768]{2,0,1:T(8,128)(2,1)}), bf16[16,32,768]{2,0,1:T(8,128)(2,1)}, u32[]{:S(2)}, u32[]{:S(2)}) async-start(bf16[16,32,768]{2,0,1:T(8,128)(2,1)} %bitcast.60), calls=%async_computation.4 | async-start | bytes 1572864 | tf_op jit(solution)/shard_map/all_to_all | solution.py:54
  250.7 23.0 %copy-start.27 = (f32[128,256]{1,0:T(8,128)S(1)}, f32[128,256]{1,0:T(8,128)}, u32[]{:S(2)}) copy-start(f32[128,256]{1,0:T(8,128)} %copy-done.26) | copy-start | bytes 393220
  252.0 23.6 %copy-start.30 = (bf16[128,256]{1,0:T(8,128)(2,1)S(1)}, bf16[128,256]{1,0:T(8,128)(2,1)}, u32[]{:S(2)}) copy-start(bf16[128,256]{1,0:T(8,128)(2,1)} %copy-done.29) | copy-start | bytes 196612
  252.0 23.6 %copy-start.32 = (f32[384]{0:T(512)S(1)}, f32[384]{0:T(512)}, u32[]{:S(2)}) copy-start(f32[384]{0:T(512)} %param.15) | copy-start | bytes 4612
  252.7 1.6 collective-permute-start.12
  272.2 4.2 %copy-start.2 = (bf16[256,3072]{1,0:T(8,128)(2,1)S(1)}, bf16[256,3072]{1,0:T(8,128)(2,1)}, u32[]{:S(2)}) copy-start(bf16[256,3072]{1,0:T(8,128)(2,1)} %copy-done.1) | copy-start | bytes 4718596
  273.6 1.9 collective-permute-start.21
  (17 other events, 35.3 us)
where the time goes:
time: 286 us; the launch traced here: 283 us
  waiting for transfers between devices  92.4 us (32%)
  starting transfers between devices  69.8 us (24%)
  Pallas kernels  38.5 us (13%)
  local copies, waits for them, and re-layouts  32.6 us (11%)
  other arithmetic  30.6 us (11%)
  blocking collectives  12.1 us (4%)
  matrix products  4.28 us (1%)
  between operations  3.04 us (1%)
    all_to_all x4, waiting for transfers between devices, exchange(): lax.all_to_all(blocks.transpose(1, 0, 2), EP, split_axis=1, concat_axis=1...  44.8 us
    ppermute x16, waiting for transfers between devices, rot(): return lax.ppermute(value, 'tp_y', [(i, (i + shift) % 4) for i in range(4)])  42 us
    pallas_call x5, Pallas kernels, call(): pl.pallas_call(kernel, grid_spec=pltpu.PrefetchScalarGridSpec(num_scalar_...  38.5 us
    all_to_all x4, starting transfers between devices, exchange(): lax.all_to_all(blocks.transpose(1, 0, 2), EP, split_axis=1, concat_axis=1...  35 us
    ppermute x16, starting transfers between devices, rot(): return lax.ppermute(value, 'tp_y', [(i, (i + shift) % 4) for i in range(4)])  22.4 us
    convert_element_type x7, other arithmetic, add(): sum((t.astype(f32) for t in terms[1:]), terms[0].astype(f32)).astype(bf16)  12.3 us
    all_gather x1, blocking collectives, layer(): head = lax.all_gather(reward_head, TP, axis=0, tiled=True)  12.1 us
    all_to_all x1, starting transfers between devices, layer(): lax.all_to_all(spread, EP_TP, split_axis=1, concat_axis=1, tiled=True)  11.5 us
  transfers between devices with their start and end apart: 28, of which 11 were waited for; matrix products, arithmetic and copies ran while one was open for 17% of the time, Pallas kernels for 14%

commit v1 on v0

--- a/solution.py
+++ b/solution.py
@@ -17,6 +17,7 @@
 
 
 loss_scale = 256.0
+VMEM_MIB = 60
 bf16, f32 = jnp.bfloat16, jnp.float32
 
 
@@ -278,7 +279,7 @@
         ),
         out_shape=out_shape,
         compiler_params=pltpu.CompilerParams(
-            dimension_semantics=("arbitrary",), vmem_limit_bytes=36 * 1024 * 1024
+            dimension_semantics=("arbitrary",), vmem_limit_bytes=VMEM_MIB * 1024 * 1024
         ),
         cost_estimate=pl.CostEstimate(flops=flops, bytes_accessed=20_000_000, transcendentals=0),
     )(*args)
@@ -447,7 +448,8 @@
     )
 
     def come_back(pieces):
-        arrived = exchange(add(*pieces).reshape(ep_size, half_cap, block)).astype(f32)
+        summed = add(*pieces).reshape(ep_size, half_cap, block)
+        arrived = exchange(summed).astype(f32)
         sums = jnp.sum(arrived.reshape(EXPERTS, replicas, half_cap, block), axis=1)
         sums = sums.astype(bf16).reshape(EXPERTS * half_cap, block)
         left, right = sums[:, :local_width], sums[:, local_width:]

time: 286 us -> 276 us (0.965)
  local copies, waits for them, and re-layouts: 32.6 us -> 15.3 us
  other arithmetic: 30.6 us -> 20.2 us
  waiting for transfers between devices: 92.4 us -> 102 us
  Pallas kernels: 38.5 us -> 46.7 us
    pallas_call x5, Pallas kernels: 38.5 us -> 46.7 us  [call(): pl.pallas_call(kernel, grid_spec=pltpu.PrefetchScalarGridSpec(num_scalar_...]
    ppermute x16, waiting for transfers between devices: 42 us -> 48 us  [rot(): return lax.ppermute(value, 'tp_y', [(i, (i + shift) % 4) for i in range(4)])]
    unnamed x75 -> x57, local copies, waits for them, and re-layouts: 6.67 us -> 1.44 us
    slice x4, local copies, waits for them, and re-layouts: 7.06 us -> 1.85 us  [gather_features(): far_low, far_high = (rot(back[:half], 1), rot(ahead[half:], -1))]
    all_to_all x4, waiting for transfers between devices: 44.8 us -> 48.7 us  [exchange(): lax.all_to_all(blocks.transpose(1, 0, 2), EP, split_axis=1, concat_axis=1...]
  transfers between devices with their start and end apart: 28 -> 28, of which waited for: 11 -> 14; matrix products, arithmetic and copies ran while one was open for 17% -> 9% of each run, Pallas kernels for 14% -> 17%
where the time goes in v1:
time: 276 us; the launch traced here: 274 us
  waiting for transfers between devices  102 us (37%)
  starting transfers between devices  70.7 us (26%)
  Pallas kernels  46.7 us (17%)
  other arithmetic  20.2 us (7%)
  local copies, waits for them, and re-layouts  15.3 us (6%)
  blocking collectives  12.1 us (4%)
  matrix products  3.29 us (1%)
  between operations  3.17 us (1%)
    all_to_all x4, waiting for transfers between devices, exchange(): lax.all_to_all(blocks.transpose(1, 0, 2), EP, split_axis=1, concat_axis=1...  48.7 us
    ppermute x16, waiting for transfers between devices, rot(): return lax.ppermute(value, 'tp_y', [(i, (i + shift) % 4) for i in range(4)])  48 us
    pallas_call x5, Pallas kernels, call(): pl.pallas_call(kernel, grid_spec=pltpu.PrefetchScalarGridSpec(num_scalar_...  46.7 us
    all_to_all x4, starting transfers between devices, exchange(): lax.all_to_all(blocks.transpose(1, 0, 2), EP, split_axis=1, concat_axis=1...  35.1 us
    ppermute x16, starting transfers between devices, rot(): return lax.ppermute(value, 'tp_y', [(i, (i + shift) % 4) for i in range(4)])  23 us
    convert_element_type x7, other arithmetic, add(): sum((t.astype(f32) for t in terms[1:]), terms[0].astype(f32)).astype(bf16)  12.9 us
    all_gather x1, blocking collectives, layer(): head = lax.all_gather(reward_head, TP, axis=0, tiled=True)  12.1 us
    all_to_all x1, starting transfers between devices, layer(): lax.all_to_all(spread, EP_TP, split_axis=1, concat_axis=1, tiled=True)  11.7 us
  transfers between devices with their start and end apart: 28, of which 14 were waited for; matrix products, arithmetic and copies ran while one was open for 9% of the time, Pallas kernels for 17%

profile of v1, /device:TPU:32, one launch (start us, length us, event | category | flops | bytes accessed | tf_op | source)
XLA Modules:
  0.0 273.8 jit_solution(10297597752742442744)
XLA Ops:
  4.4 1.3 fusion
  5.9 1.4 collective-permute-done
  8.0 0.9 broadcast_in_dim.75
  9.0 11.2 %all-to-all-start = ((bf16[16,32,768]{2,0,1:T(8,128)(2,1)}), bf16[16,32,768]{2,0,1:T(8,128)(2,1)}, u32[]{:S(2)}, u32[]{:S(2)}) async-start(bf16[16,32,768]{2,0,1:T(8,128)(2,1)} %bitcast.12), calls=%async_computation | async-start | bytes 1572864 | tf_op jit(solution)/shard_map/all_to_all | solution.py:55
  20.9 0.9 pad_maximum_fusion.4
  21.8 21.7 %all-to-all-done = bf16[16,32,768]{2,0,1:T(8,128)(2,1)} async-done(((bf16[16,32,768]{2,0,1:T(8,128)(2,1)}), bf16[16,32,768]{2,0,1:T(8,128)(2,1)}, u32[]{:S(2)}, u32[]{:S(2)}) %all-to-all-start) | async-done | bytes 786464 | tf_op jit(solution)/shard_map/all_to_all | solution.py:55
  43.6 1.0 broadcast_in_dim.79
  44.6 5.2 %all-to-all-start.1 = ((bf16[16,32,896]{2,0,1:T(8,128)(2,1)}), bf16[16,32,896]{2,0,1:T(8,128)(2,1)}, u32[]{:S(2)}, u32[]{:S(2)}) async-start(bf16[16,32,896]{2,0,1:T(8,128)(2,1)} %bitcast.53), calls=%async_computation.1 | async-start | bytes 1835008 | tf_op jit(solution)/shard_map/all_to_all | solution.py:55
  50.3 12.1 %all-gather = f32[8,1,384]{2,1,0:T(1,128)S(1)} all-gather(f32[1,1,384]{2,1,0:T(1,128)S(1)} %reshape.176), channel_id=1, replica_groups=mesh['ep_x'=4,'ep_z'=8,'tp_y'=4,'tp_c'=2] {'tp_y','tp_c'}, dimensions={0}, use_global_device_ids=true | all-gather | bytes 13824 | tf_op jit(solution)/shard_map/all_gather | solution.py:348
  64.1 1.3 collective-permute-start.3
  65.9 2.0 collective-permute-start.2
  67.9 7.3 %all-to-all-done.1 = bf16[16,32,896]{2,0,1:T(8,128)(2,1)} async-done(((bf16[16,32,896]{2,0,1:T(8,128)(2,1)}), bf16[16,32,896]{2,0,1:T(8,128)(2,1)}, u32[]{:S(2)}, u32[]{:S(2)}) %all-to-all-start.1) | async-done | bytes 917536 | tf_op jit(solution)/shard_map/all_to_all | solution.py:55
  75.2 1.2 slice.135.refs_0_.refs_5_
  76.5 1.7 collective-permute-start.14
  78.1 7.9 %collective-permute-done.3.refs_4_ = bf16[512,768]{1,0:T(8,128)(2,1)S(1)} collective-permute-done((bf16[512,768]{1,0:T(8,128)(2,1)}, bf16[512,768]{1,0:T(8,128)(2,1)S(1)}, u32[]{:S(2)}, u32[]{:S(2)}) %collective-permute-start.3) | collective-permute-done | bytes 786464 | tf_op jit(solution)/shard_map/ppermute | solution.py:47
  86.7 1.4 collective-permute-start.4
  88.1 1.8 slice.128
  89.9 12.9 %collective-permute-done.14.refs_4_.refs_9_ = bf16[512,768]{1,0:T(8,128)(2,1)S(1)} collective-permute-done((bf16[512,768]{1,0:T(8,128)(2,1)S(1)}, bf16[512,768]{1,0:T(8,128)(2,1)S(1)}, u32[]{:S(2)}, u32[]{:S(2)}) %collective-permute-start.14) | collective-permute-done | bytes 786464 | tf_op jit(solution)/shard_map/ppermute | solution.py:47
  104.3 1.0 collective-permute-start.15
  105.3 2.5 collective-permute-start.16
  107.9 3.5 %collective-permute-done.4.refs_2_ = bf16[256,768]{1,0:T(8,128)(2,1)} collective-permute-done((bf16[256,768]{1,0:T(8,128)(2,1)S(1)}, bf16[256,768]{1,0:T(8,128)(2,1)}, u32[]{:S(2)}, u32[]{:S(2)}) %collective-permute-start.4) | collective-permute-done | bytes 393248 | tf_op jit(solution)/shard_map/ppermute | solution.py:47
  111.4 3.8 %collective-permute-done.5.refs_3_ = bf16[256,768]{1,0:T(8,128)(2,1)} collective-permute-done((bf16[256,768]{1,0:T(8,128)(2,1)}, bf16[256,768]{1,0:T(8,128)(2,1)}, u32[]{:S(2)}, u32[]{:S(2)}) %collective-permute-start.5) | collective-permute-done | bytes 393248 | tf_op jit(solution)/shard_map/ppermute | solution.py:47
  115.1 10.1 %shard_map.144 = (f32[512,512]{1,0:T(8,128)}, f32[512,512]{1,0:T(8,128)}, bf16[512,512]{1,0:T(8,128)(2,1)}, f32[32,128]{1,0:T(8,128)}) custom-call(s32[1]{0:T(128)} %bitcast.6.y_ref, bf16[512,768]{1,0:T(8,128)(2,1)} %bitcast.14.refs_0_, bf16[512,768]{1,0:T(8,128)(2,1)} %collective-permute-done.2.refs_1_, bf16[256,768]{1,0:T(8,128)(2,1)} %collective-permute-done.4.refs_2_, ...), custom_call_target="tpu_custom_call" | custom-call | flops 3221225472 | bytes 20000000 | tf_op jit(solution)/shard_map/pallas_call | solution.py:271
  127.0 11.7 %all-to-all-start.3 = ((f32[2,256,32]{2,0,1:T(2,128)}), f32[2,256,32]{2,0,1:T(2,128)S(1)}, u32[]{:S(2)}, u32[]{:S(2)}) async-start(f32[2,256,32]{2,0,1:T(2,128)} %broadcast_in_dim.81), calls=%async_computation.3 | async-start | bytes 524288 | tf_op jit(solution)/shard_map/all_to_all | solution.py:380
  138.6 6.1 %shard_map.145 = (bf16[512,768]{1,0:T(8,128)(2,1)}, bf16[512,768]{1,0:T(8,128)(2,1)}, bf16[256,768]{1,0:T(8,128)(2,1)}, bf16[256,768]{1,0:T(8,128)(2,1)}, bf16[512,768]{1,0:T(8,128)(2,1)}) custom-call(s32[1]{0:T(128)} %bitcast.6.y_ref, bf16[512,512]{1,0:T(8,128)(2,1)} %get-tuple-element.33.hidden_ref.refs_10_, bf16[256,3072]{1,0:T(8,128)(2,1)} %refs_5_.3, ...), custom_call_target="tpu_custom_call" | custom-call | flops 1610612736 | bytes 20000000 | tf_op jit(solution)/shard_map/pallas_call | solution.py:271
  144.7 2.9 %collective-permute-start.10 = (bf16[256,768]{1,0:T(8,128)(2,1)}, bf16[256,768]{1,0:T(8,128)(2,1)}, u32[]{:S(2)}, u32[]{:S(2)}) collective-permute-start(bf16[256,768]{1,0:T(8,128)(2,1)} %get-tuple-element.38), channel_id=1, source_target_pairs={{0,6},{2,0},{4,2},{6,4},{1,7},{3,1},{5,3},{7,5},{8,14},{10,8},{12,... | collective-permute-start | bytes 1179656 | tf_op jit(solution)/shard_map/ppermute | solution.py:47
  147.6 1.0 slice.106
  148.6 1.0 slice.105
  149.7 3.3 %all-to-all-done.3 = f32[2,256,32]{2,0,1:T(2,128)S(1)} async-done(((f32[2,256,32]{2,0,1:T(2,128)}), f32[2,256,32]{2,0,1:T(2,128)S(1)}, u32[]{:S(2)}, u32[]{:S(2)}) %all-to-all-start.3) | async-done | bytes 65568 | tf_op jit(solution)/shard_map/all_to_all | solution.py:380
  155.2 6.4 %shard_map.146.refs_7_ = f32[512,512]{1,0:T(8,128)} custom-call(s32[1]{0:T(128)} %bitcast.6.y_ref, bf16[512,768]{1,0:T(8,128)(2,1)} %copy-done.2, bf16[512,768]{1,0:T(8,128)(2,1)} %copy-done.4, bf16[256,768]{1,0:T(8,128)(2,1)} %collective-permute-done.15.refs_2_.refs_7_, bf16[256,768]{1,0:T(8,128)(2,1)} %collective-permute-done.16.refs_3_.refs_8_, ...), custom_call_target="tpu_custom_call" | custom-call | flops 1610612736 | bytes 20000000 | tf_op jit(solution)/shard_map/pallas_call | solution.py:271
  161.7 1.2 add_convert_fusion.7
  162.9 1.8 collective-permute-start.11
  165.2 10.3 %shard_map.147 = (bf16[512,512]{1,0:T(8,128)(2,1)}, bf16[512,512]{1,0:T(8,128)(2,1)}, f32[512,1]{1,0:T(8,128)}, bf16[512,768]{1,0:T(8,128)(2,1)}, bf16[512,768]{...) custom-call(s32[1]{0:T(128)} %bitcast.6.y_ref, ...), custom_call_target="tpu_custom_call" | custom-call | flops 3221225472 | bytes 20000000 | tf_op jit(solution)/shard_map/pallas_call | solution.py:271
  175.5 3.0 %collective-permute-start.19 = (bf16[256,768]{1,0:T(8,128)(2,1)}, bf16[256,768]{1,0:T(8,128)(2,1)S(1)}, u32[]{:S(2)}, u32[]{:S(2)}) collective-permute-start(bf16[256,768]{1,0:T(8,128)(2,1)} %get-tuple-element.47), channel_id=1, source_target_pairs={{0,6},{2,0},{4,2},{6,4},{1,7},{3,1},{5,3},{7,5},{8,14},{10,8},{12,... | collective-permute-start | bytes 1179656 | tf_op jit(solution)/shard_map/ppermute | solution.py:47
  178.5 1.0 slice.118
  179.5 1.0 slice.117
  180.9 13.8 %shard_map.148 = (bf16[256,3072]{1,0:T(8,128)(2,1)}, bf16[256,3072]{1,0:T(8,128)(2,1)}, bf16[256,3072]{1,0:T(8,128)(2,1)}, bf16[768,3072]{1,0:T(8,128)(2,1)}) custom-call(s32[1]{0:T(128)} %bitcast.6.y_ref, bf16[512,768]{1,0:T(8,128)(2,1)} %bitcast.14.refs_0_, bf16[512,768]{1,0:T(8,128)(2,1)} %collective-permute-done.2.refs_1_, ...), custom_call_target="tpu_custom_call" | custom-call | flops 4831838208 | bytes 20000000 | tf_op jit(solution)/shard_map/pallas_call | solution.py:271
  195.0 0.9 copy-done.10
  195.8 2.6 add_convert_fusion.4
  198.4 8.9 %all-to-all-start.2 = ((bf16[16,32,768]{2,0,1:T(8,128)(2,1)}), bf16[16,32,768]{2,0,1:T(8,128)(2,1)S(1)}, u32[]{:S(2)}, u32[]{:S(2)}) async-start(bf16[16,32,768]{2,0,1:T(8,128)(2,1)} %bitcast.23), calls=%async_computation.2 | async-start | bytes 1572864 | tf_op jit(solution)/shard_map/all_to_all | solution.py:55
  207.3 3.3 %collective-permute-start.20 = (bf16[512,768]{1,0:T(8,128)(2,1)S(1)}, bf16[512,768]{1,0:T(8,128)(2,1)S(1)}, u32[]{:S(2)}, u32[]{:S(2)}) collective-permute-start(bf16[512,768]{1,0:T(8,128)(2,1)S(1)} %pad_maximum_fusion.3), channel_id=1, source_target_pairs={{0,6},{2,0},{4,2},{6,4},{1,7},{3,1},{5,3},{7,5},{8,14},{10,8},{12,... | collective-permute-start | bytes 2359304 | tf_op jit(solution)/shard_map/ppermute | solution.py:47
  210.7 1.1 add_convert_fusion.6
  211.9 14.8 %collective-permute-done.20 = bf16[512,768]{1,0:T(8,128)(2,1)S(1)} collective-permute-done((bf16[512,768]{1,0:T(8,128)(2,1)S(1)}, bf16[512,768]{1,0:T(8,128)(2,1)S(1)}, u32[]{:S(2)}, u32[]{:S(2)}) %collective-permute-start.20) | collective-permute-done | bytes 786464 | tf_op jit(solution)/shard_map/ppermute | solution.py:47
  226.7 4.6 %collective-permute-done.18 = bf16[512,768]{1,0:T(8,128)(2,1)S(1)} collective-permute-done((bf16[512,768]{1,0:T(8,128)(2,1)S(1)}, bf16[512,768]{1,0:T(8,128)(2,1)S(1)}, u32[]{:S(2)}, u32[]{:S(2)}) %collective-permute-start.18) | collective-permute-done | bytes 786464 | tf_op jit(solution)/shard_map/ppermute | solution.py:47
  231.3 1.2 add_convert_fusion.3
  232.5 9.8 %all-to-all-start.4 = ((bf16[16,32,768]{2,0,1:T(8,128)(2,1)}), bf16[16,32,768]{2,0,1:T(8,128)(2,1)S(1)}, u32[]{:S(2)}, u32[]{:S(2)}) async-start(bf16[16,32,768]{2,0,1:T(8,128)(2,1)} %bitcast.29), calls=%async_computation.4 | async-start | bytes 1572864 | tf_op jit(solution)/shard_map/all_to_all | solution.py:55
  243.9 19.6 %all-to-all-done.4 = bf16[16,32,768]{2,0,1:T(8,128)(2,1)S(1)} async-done(((bf16[16,32,768]{2,0,1:T(8,128)(2,1)}), bf16[16,32,768]{2,0,1:T(8,128)(2,1)S(1)}, u32[]{:S(2)}, u32[]{:S(2)}) %all-to-all-start.4) | async-done | bytes 786464 | tf_op jit(solution)/shard_map/all_to_all | solution.py:55
  265.9 6.7 %add_convert_fusion = (bf16[256,3072]{1,0:T(8,128)(2,1)}, bf16[256,3072]{1,0:T(8,128)(2,1)}, bf16[256,3072]{1,0:T(8,128)(2,1)}) fusion(bf16[256,3072]{1,0:T(8,128)(2,1)} %get-tuple-element.54, bf16[768,3072]{1,0:T(8,128)(2,1)} %collective-permute-done.22, bf16[256,3072]{1,0:T(8,128)(2,1)} %get-tuple-element.53, bf16[256,3072]{1,0:T(8,128)(2,1)S(1)} %copy-done.5), kind=kLoop, calls=%fused_computation | loop fusion | flops 9437184 | bytes 14155776 | tf_op jit(solution)/shard_map/convert_element_type | solution.py:69
  (149 shorter events, 18.5 us)
Async XLA Ops:
  4.4 16.0 %copy-start.12 = (f32[128,256]{1,0:T(8,128)}, f32[128,256]{1,0:T(8,128)S(1)}, u32[]{:S(2)}) copy-start(f32[128,256]{1,0:T(8,128)S(1)} %get-tuple-element.58) | copy-start | bytes 393220
  5.8 1.5 collective-permute-start
  8.0 12.2 %copy-start = (bf16[256,3072]{1,0:T(8,128)(2,1)S(1)}, bf16[256,3072]{1,0:T(8,128)(2,1)}, u32[]{:S(2)}) copy-start(bf16[256,3072]{1,0:T(8,128)(2,1)} %refs_5_.3) | copy-start | bytes 4718596
  9.0 34.6 %all-to-all-start = ((bf16[16,32,768]{2,0,1:T(8,128)(2,1)}), bf16[16,32,768]{2,0,1:T(8,128)(2,1)}, u32[]{:S(2)}, u32[]{:S(2)}) async-start(bf16[16,32,768]{2,0,1:T(8,128)(2,1)} %bitcast.12), calls=%async_computation | async-start | bytes 1572864 | tf_op jit(solution)/shard_map/all_to_all | solution.py:55
  20.2 42.2 %collective-permute-start.1 = (bf16[256,3072]{1,0:T(8,128)(2,1)S(1)}, bf16[256,3072]{1,0:T(8,128)(2,1)S(1)}, u32[]{:S(2)}, u32[]{:S(2)}) collective-permute-start(bf16[256,3072]{1,0:T(8,128)(2,1)S(1)} %copy-done), channel_id=1, source_target_pairs={{0,1},{1,0},{2,3},{3,2},{4,5},{5,4},{6,7},{7,6},{8,9},{9,8},{10,11... | collective-permute-start | bytes 4718600 | tf_op jit(solution)/shard_map/ppermute | solution.py:51
  21.8 27.9 %copy-start.20 = (f32[384]{0:T(512)S(1)}, f32[384]{0:T(512)}, u32[]{:S(2)}) copy-start(f32[384]{0:T(512)} %param.15) | copy-start | bytes 4612
  21.8 28.0 %copy-start.14 = (bf16[128,384]{1,0:T(8,128)(2,1)S(1)}, bf16[128,384]{1,0:T(8,128)(2,1)}, u32[]{:S(2)}) copy-start(bf16[128,384]{1,0:T(8,128)(2,1)} %param.9) | copy-start | bytes 294916
  44.6 30.7 %all-to-all-start.1 = ((bf16[16,32,896]{2,0,1:T(8,128)(2,1)}), bf16[16,32,896]{2,0,1:T(8,128)(2,1)}, u32[]{:S(2)}, u32[]{:S(2)}) async-start(bf16[16,32,896]{2,0,1:T(8,128)(2,1)} %bitcast.53), calls=%async_computation.1 | async-start | bytes 1835008 | tf_op jit(solution)/shard_map/all_to_all | solution.py:55
  50.3 12.8 %copy-start.26 = (f32[64]{0:T(128)}, f32[64]{0:T(128)S(1)}, u32[]{:S(2)}) copy-start(f32[64]{0:T(128)S(1)} %dynamic_update_slice.3) | copy-start | bytes 772
  64.1 21.8 %collective-permute-start.3 = (bf16[512,768]{1,0:T(8,128)(2,1)}, bf16[512,768]{1,0:T(8,128)(2,1)S(1)}, u32[]{:S(2)}, u32[]{:S(2)}) collective-permute-start(bf16[512,768]{1,0:T(8,128)(2,1)} %bitcast.14.refs_0_), channel_id=1, source_target_pairs={{0,2},{2,4},{4,6},{6,0},{1,3},{3,5},{5,7},{7,1},{8,10},{10,12},{12... | collective-permute-start | bytes 2359304 | tf_op jit(solution)/shard_map/ppermute | solution.py:47
  65.4 39.9 %collective-permute-start.6 = (bf16[256,3072]{1,0:T(8,128)(2,1)}, bf16[256,3072]{1,0:T(8,128)(2,1)}, u32[]{:S(2)}, u32[]{:S(2)}) collective-permute-start(bf16[256,3072]{1,0:T(8,128)(2,1)} %refs_0_.1), channel_id=1, source_target_pairs={{0,1},{1,0},{2,3},{3,2},{4,5},{5,4},{6,7},{7,6},{8,9},{9,8},{10,11... | collective-permute-start | bytes 4718600 | tf_op jit(solution)/shard_map/ppermute | solution.py:51
  65.5 42.4 %collective-permute-start.7 = (bf16[256,3072]{1,0:T(8,128)(2,1)}, bf16[256,3072]{1,0:T(8,128)(2,1)}, u32[]{:S(2)}, u32[]{:S(2)}) collective-permute-start(bf16[256,3072]{1,0:T(8,128)(2,1)} %refs_2_.1), channel_id=1, source_target_pairs={{0,1},{1,0},{2,3},{3,2},{4,5},{5,4},{6,7},{7,6},{8,9},{9,8},{10,11... | collective-permute-start | bytes 4718600 | tf_op jit(solution)/shard_map/ppermute | solution.py:51
  65.9 20.8 %collective-permute-start.2 = (bf16[512,768]{1,0:T(8,128)(2,1)}, bf16[512,768]{1,0:T(8,128)(2,1)}, u32[]{:S(2)}, u32[]{:S(2)}) collective-permute-start(bf16[512,768]{1,0:T(8,128)(2,1)} %bitcast.14.refs_0_), channel_id=1, source_target_pairs={{0,6},{2,0},{4,2},{6,4},{1,7},{3,1},{5,3},{7,5},{8,14},{10,8},{12,... | collective-permute-start | bytes 2359304 | tf_op jit(solution)/shard_map/ppermute | solution.py:47
  75.2 28.3 %copy-start.25 = (s32[64]{0:T(128)S(1)}, s32[64]{0:T(128)}, u32[]{:S(2)}) copy-start(s32[64]{0:T(128)} %param.17) | copy-start | bytes 772
  76.4 28.8 %copy-start.2 = (bf16[512,768]{1,0:T(8,128)(2,1)}, bf16[512,768]{1,0:T(8,128)(2,1)S(1)}, u32[]{:S(2)}) copy-start(bf16[512,768]{1,0:T(8,128)(2,1)S(1)} %slice.135.refs_0_.refs_5_) | copy-start | bytes 2359300
  76.5 26.4 %collective-permute-start.14 = (bf16[512,768]{1,0:T(8,128)(2,1)S(1)}, bf16[512,768]{1,0:T(8,128)(2,1)S(1)}, u32[]{:S(2)}, u32[]{:S(2)}) collective-permute-start(bf16[512,768]{1,0:T(8,128)(2,1)S(1)} %slice.135.refs_0_.refs_5_), channel_id=1, source_target_pairs={{0,2},{2,4},{4,6},{6,0},{1,3},{3,5},{5,7},{7,1},{8,10},{10,12},{12... | collective-permute-start | bytes 2359304 | tf_op jit(solution)/shard_map/ppermute | solution.py:47
  86.0 17.8 %copy-start.16 = (bf16[512,768]{1,0:T(8,128)(2,1)}, bf16[512,768]{1,0:T(8,128)(2,1)S(1)}, u32[]{:S(2)}) copy-start(bf16[512,768]{1,0:T(8,128)(2,1)S(1)} %collective-permute-done.3.refs_4_) | copy-start | bytes 2359300
  86.0 18.3 %collective-permute-start.13 = (bf16[512,768]{1,0:T(8,128)(2,1)S(1)}, bf16[512,768]{1,0:T(8,128)(2,1)S(1)}, u32[]{:S(2)}, u32[]{:S(2)}) collective-permute-start(bf16[512,768]{1,0:T(8,128)(2,1)S(1)} %slice.135.refs_0_.refs_5_), channel_id=1, source_target_pairs={{0,6},{2,0},{4,2},{6,4},{1,7},{3,1},{5,3},{7,5},{8,14},{10,8},{12,... | collective-permute-start | bytes 2359304 | tf_op jit(solution)/shard_map/ppermute | solution.py:47
  86.7 24.7 %collective-permute-start.4 = (bf16[256,768]{1,0:T(8,128)(2,1)S(1)}, bf16[256,768]{1,0:T(8,128)(2,1)}, u32[]{:S(2)}, u32[]{:S(2)}) collective-permute-start(bf16[256,768]{1,0:T(8,128)(2,1)S(1)} %slice.127), channel_id=1, source_target_pairs={{0,2},{2,4},{4,6},{6,0},{1,3},{3,5},{5,7},{7,1},{8,10},{10,12},{12... | collective-permute-start | bytes 1179656 | tf_op jit(solution)/shard_map/ppermute | solution.py:47
  102.8 22.4 %copy-start.3 = (bf16[512,768]{1,0:T(8,128)(2,1)}, bf16[512,768]{1,0:T(8,128)(2,1)S(1)}, u32[]{:S(2)}) copy-start(bf16[512,768]{1,0:T(8,128)(2,1)S(1)} %collective-permute-done.14.refs_4_.refs_9_) | copy-start | bytes 2359300
  102.8 12.3 %collective-permute-start.5 = (bf16[256,768]{1,0:T(8,128)(2,1)}, bf16[256,768]{1,0:T(8,128)(2,1)}, u32[]{:S(2)}, u32[]{:S(2)}) collective-permute-start(bf16[256,768]{1,0:T(8,128)(2,1)} %slice.128), channel_id=1, source_target_pairs={{0,6},{2,0},{4,2},{6,4},{1,7},{3,1},{5,3},{7,5},{8,14},{10,8},{12,... | collective-permute-start | bytes 1179656 | tf_op jit(solution)/shard_map/ppermute | solution.py:47
  104.3 21.0 %copy-start.4 = (bf16[512,768]{1,0:T(8,128)(2,1)}, bf16[512,768]{1,0:T(8,128)(2,1)S(1)}, u32[]{:S(2)}) copy-start(bf16[512,768]{1,0:T(8,128)(2,1)S(1)} %collective-permute-done.13.refs_1_.refs_6_) | copy-start | bytes 2359300
  104.3 50.9 %collective-permute-start.15 = (bf16[256,768]{1,0:T(8,128)(2,1)S(1)}, bf16[256,768]{1,0:T(8,128)(2,1)}, u32[]{:S(2)}, u32[]{:S(2)}) collective-permute-start(bf16[256,768]{1,0:T(8,128)(2,1)S(1)} %slice.136), channel_id=1, source_target_pairs={{0,2},{2,4},{4,6},{6,0},{1,3},{3,5},{5,7},{7,1},{8,10},{10,12},{12... | collective-permute-start | bytes 1179656 | tf_op jit(solution)/shard_map/ppermute | solution.py:47
  105.3 49.9 %collective-permute-start.16 = (bf16[256,768]{1,0:T(8,128)(2,1)S(1)}, bf16[256,768]{1,0:T(8,128)(2,1)}, u32[]{:S(2)}, u32[]{:S(2)}) collective-permute-start(bf16[256,768]{1,0:T(8,128)(2,1)S(1)} %slice.137), channel_id=1, source_target_pairs={{0,6},{2,0},{4,2},{6,4},{1,7},{3,1},{5,3},{7,5},{8,14},{10,8},{12,... | collective-permute-start | bytes 1179656 | tf_op jit(solution)/shard_map/ppermute | solution.py:47
  115.1 11.0 %copy-start.27 = (f32[64]{0:T(128)S(1)}, f32[64]{0:T(128)}, u32[]{:S(2)}) copy-start(f32[64]{0:T(128)} %copy-done.26) | copy-start | bytes 772
  127.0 26.1 %all-to-all-start.3 = ((f32[2,256,32]{2,0,1:T(2,128)}), f32[2,256,32]{2,0,1:T(2,128)S(1)}, u32[]{:S(2)}, u32[]{:S(2)}) async-start(f32[2,256,32]{2,0,1:T(2,128)} %broadcast_in_dim.81), calls=%async_computation.3 | async-start | bytes 524288 | tf_op jit(solution)/shard_map/all_to_all | solution.py:380
  144.7 16.9 %collective-permute-start.10 = (bf16[256,768]{1,0:T(8,128)(2,1)}, bf16[256,768]{1,0:T(8,128)(2,1)}, u32[]{:S(2)}, u32[]{:S(2)}) collective-permute-start(bf16[256,768]{1,0:T(8,128)(2,1)} %get-tuple-element.38), channel_id=1, source_target_pairs={{0,6},{2,0},{4,2},{6,4},{1,7},{3,1},{5,3},{7,5},{8,14},{10,8},{12,... | collective-permute-start | bytes 1179656 | tf_op jit(solution)/shard_map/ppermute | solution.py:47
  149.6 15.1 %collective-permute-start.8 = (bf16[256,768]{1,0:T(8,128)(2,1)}, bf16[256,768]{1,0:T(8,128)(2,1)S(1)}, u32[]{:S(2)}, u32[]{:S(2)}) collective-permute-start(bf16[256,768]{1,0:T(8,128)(2,1)} %get-tuple-element.36), channel_id=1, source_target_pairs={{0,2},{2,4},{4,6},{6,0},{1,3},{3,5},{5,7},{7,1},{8,10},{10,12},{12... | collective-permute-start | bytes 1179656 | tf_op jit(solution)/shard_map/ppermute | solution.py:47
  162.9 32.1 %collective-permute-start.11 = (bf16[512,768]{1,0:T(8,128)(2,1)S(1)}, bf16[512,768]{1,0:T(8,128)(2,1)}, u32[]{:S(2)}, u32[]{:S(2)}) collective-permute-start(bf16[512,768]{1,0:T(8,128)(2,1)S(1)} %pad_maximum_fusion.1), channel_id=1, source_target_pairs={{0,6},{2,0},{4,2},{6,4},{1,7},{3,1},{5,3},{7,5},{8,14},{10,8},{12,... | collective-permute-start | bytes 2359304 | tf_op jit(solution)/shard_map/ppermute | solution.py:47
  164.9 30.1 %collective-permute-start.9 = (bf16[512,768]{1,0:T(8,128)(2,1)S(1)}, bf16[512,768]{1,0:T(8,128)(2,1)}, u32[]{:S(2)}, u32[]{:S(2)}) collective-permute-start(bf16[512,768]{1,0:T(8,128)(2,1)S(1)} %pad_maximum_fusion), channel_id=1, source_target_pairs={{0,2},{2,4},{4,6},{6,0},{1,3},{3,5},{5,7},{7,1},{8,10},{10,12},{12... | collective-permute-start | bytes 2359304 | tf_op jit(solution)/shard_map/ppermute | solution.py:47
  175.5 19.3 %collective-permute-start.19 = (bf16[256,768]{1,0:T(8,128)(2,1)}, bf16[256,768]{1,0:T(8,128)(2,1)S(1)}, u32[]{:S(2)}, u32[]{:S(2)}) collective-permute-start(bf16[256,768]{1,0:T(8,128)(2,1)} %get-tuple-element.47), channel_id=1, source_target_pairs={{0,6},{2,0},{4,2},{6,4},{1,7},{3,1},{5,3},{7,5},{8,14},{10,8},{12,... | collective-permute-start | bytes 1179656 | tf_op jit(solution)/shard_map/ppermute | solution.py:47
  180.6 30.1 %collective-permute-start.17 = (bf16[256,768]{1,0:T(8,128)(2,1)}, bf16[256,768]{1,0:T(8,128)(2,1)}, u32[]{:S(2)}, u32[]{:S(2)}) collective-permute-start(bf16[256,768]{1,0:T(8,128)(2,1)} %get-tuple-element.45), channel_id=1, source_target_pairs={{0,2},{2,4},{4,6},{6,0},{1,3},{3,5},{5,7},{7,1},{8,10},{10,12},{12... | collective-permute-start | bytes 1179656 | tf_op jit(solution)/shard_map/ppermute | solution.py:47
  180.9 14.0 %copy-start.9 = (bf16[512,768]{1,0:T(8,128)(2,1)S(1)}, bf16[512,768]{1,0:T(8,128)(2,1)}, u32[]{:S(2)}) copy-start(bf16[512,768]{1,0:T(8,128)(2,1)} %get-tuple-element.46) | copy-start | bytes 2359300
  194.7 71.2 %collective-permute-start.22 = (bf16[768,3072]{1,0:T(8,128)(2,1)}, bf16[768,3072]{1,0:T(8,128)(2,1)}, u32[]{:S(2)}, u32[]{:S(2)}) collective-permute-start(bf16[768,3072]{1,0:T(8,128)(2,1)} %get-tuple-element.52), channel_id=1, source_target_pairs={{0,1},{1,0},{2,3},{3,2},{4,5},{5,4},{6,7},{7,6},{8,9},{9,8},{10,11... | collective-permute-start | bytes 14155784 | tf_op jit(solution)/shard_map/ppermute | solution.py:51
  198.4 12.2 %copy-start.6 = (bf16[512,768]{1,0:T(8,128)(2,1)S(1)}, bf16[512,768]{1,0:T(8,128)(2,1)}, u32[]{:S(2)}) copy-start(bf16[512,768]{1,0:T(8,128)(2,1)} %get-tuple-element.44) | copy-start | bytes 2359300
  198.4 34.1 %all-to-all-start.2 = ((bf16[16,32,768]{2,0,1:T(8,128)(2,1)}), bf16[16,32,768]{2,0,1:T(8,128)(2,1)S(1)}, u32[]{:S(2)}, u32[]{:S(2)}) async-start(bf16[16,32,768]{2,0,1:T(8,128)(2,1)} %bitcast.23), calls=%async_computation.2 | async-start | bytes 1572864 | tf_op jit(solution)/shard_map/all_to_all | solution.py:55
  207.3 24.0 %copy-start.11 = (bf16[512,768]{1,0:T(8,128)(2,1)S(1)}, bf16[512,768]{1,0:T(8,128)(2,1)}, u32[]{:S(2)}) copy-start(bf16[512,768]{1,0:T(8,128)(2,1)} %get-tuple-element.43) | copy-start | bytes 2359300
  207.3 19.3 %collective-permute-start.20 = (bf16[512,768]{1,0:T(8,128)(2,1)S(1)}, bf16[512,768]{1,0:T(8,128)(2,1)S(1)}, u32[]{:S(2)}, u32[]{:S(2)}) collective-permute-start(bf16[512,768]{1,0:T(8,128)(2,1)S(1)} %pad_maximum_fusion.3), channel_id=1, source_target_pairs={{0,6},{2,0},{4,2},{6,4},{1,7},{3,1},{5,3},{7,5},{8,14},{10,8},{12,... | collective-permute-start | bytes 2359304 | tf_op jit(solution)/shard_map/ppermute | solution.py:47
  211.8 19.5 %collective-permute-start.18 = (bf16[512,768]{1,0:T(8,128)(2,1)S(1)}, bf16[512,768]{1,0:T(8,128)(2,1)S(1)}, u32[]{:S(2)}, u32[]{:S(2)}) collective-permute-start(bf16[512,768]{1,0:T(8,128)(2,1)S(1)} %pad_maximum_fusion.2), channel_id=1, source_target_pairs={{0,2},{2,4},{4,6},{6,0},{1,3},{3,5},{5,7},{7,1},{8,10},{10,12},{12... | collective-permute-start | bytes 2359304 | tf_op jit(solution)/shard_map/ppermute | solution.py:47
  232.5 10.1 %copy-start.23 = (f32[64]{0:T(128)S(1)}, f32[64]{0:T(128)}, u32[]{:S(2)}) copy-start(f32[64]{0:T(128)} %copy-done.22) | copy-start | bytes 772
  232.5 31.0 %all-to-all-start.4 = ((bf16[16,32,768]{2,0,1:T(8,128)(2,1)}), bf16[16,32,768]{2,0,1:T(8,128)(2,1)S(1)}, u32[]{:S(2)}, u32[]{:S(2)}) async-start(bf16[16,32,768]{2,0,1:T(8,128)(2,1)} %bitcast.29), calls=%async_computation.4 | async-start | bytes 1572864 | tf_op jit(solution)/shard_map/all_to_all | solution.py:55
  242.3 21.5 %copy-start.13 = (f32[128,256]{1,0:T(8,128)S(1)}, f32[128,256]{1,0:T(8,128)}, u32[]{:S(2)}) copy-start(f32[128,256]{1,0:T(8,128)} %copy-done.12) | copy-start | bytes 393220
  242.3 21.5 %copy-start.15 = (bf16[128,384]{1,0:T(8,128)(2,1)S(1)}, bf16[128,384]{1,0:T(8,128)(2,1)}, u32[]{:S(2)}) copy-start(bf16[128,384]{1,0:T(8,128)(2,1)} %param.9) | copy-start | bytes 294916
  242.4 22.7 %copy-start.18 = (bf16[128,256]{1,0:T(8,128)(2,1)S(1)}, bf16[128,256]{1,0:T(8,128)(2,1)}, u32[]{:S(2)}) copy-start(bf16[128,256]{1,0:T(8,128)(2,1)} %copy-done.17) | copy-start | bytes 196612
  242.4 22.7 %copy-start.24 = (bf16[128,384]{1,0:T(8,128)(2,1)S(1)}, bf16[128,384]{1,0:T(8,128)(2,1)}, u32[]{:S(2)}) copy-start(bf16[128,384]{1,0:T(8,128)(2,1)} %param.16) | copy-start | bytes 294916
  242.5 1.4 collective-permute-start.12
  243.9 22.0 %copy-start.5 = (bf16[256,3072]{1,0:T(8,128)(2,1)S(1)}, bf16[256,3072]{1,0:T(8,128)(2,1)}, u32[]{:S(2)}) copy-start(bf16[256,3072]{1,0:T(8,128)(2,1)} %get-tuple-element.51) | copy-start | bytes 4718596
  263.7 1.4 collective-permute-start.21
  (8 other events, 15.5 us)

commit v2 on v1

--- a/solution.py
+++ b/solution.py
@@ -100,16 +100,6 @@
             rows[pl.ds(half, half)] = high[...]
 
 
-def store_piece(step, refs, rows):
-    half = rows.shape[0] // 2
-    for k, (low, high) in enumerate(piece_halves(refs)):
-
-        @pl.when(step == k)
-        def _(low=low, high=high):
-            low[...] = rows[pl.ds(0, half)]
-            high[...] = rows[pl.ds(half, half)]
-
-
 def cross(a, b):
     return lax.dot_general(a, b, (((1,), (1,)), ((), ())), preferred_element_type=f32)
 
@@ -118,59 +108,104 @@
     return lax.dot_general(a, b, (((1,), (0,)), ((), ())), preferred_element_type=f32)
 
 
-def fwd_kernel(y_ref, *refs):
-    x_refs = refs[:5]
-    wg0, wg1, wu0, wu1, rh_ref, meta_ref = refs[5:11]
-    slope_ref, silu_ref, hidden_ref, score_ref = refs[11:15]
-    gate_acc, up_acc, rows = refs[15:]
-    width = wg0.shape[0]
-    left, right = pl.ds(0, width), pl.ds(width, width)
+def near_kernel(y_ref, *refs):
+    x_refs = refs[:3]
+    weights, accs, rows = refs[3:7], refs[7:9], refs[9]
+    width = weights[0].shape[0]
     step = pl.program_id(0)
 
     @pl.when(step == 0)
     def _():
-        gate_acc[...] = jnp.zeros_like(gate_acc)
-        up_acc[...] = jnp.zeros_like(up_acc)
-
-    load_piece(step, x_refs, rows)
-    gate_acc[:, left] += cross(rows[...], wg0[...])
-    gate_acc[:, right] += cross(rows[...], wg1[...])
-    up_acc[:, left] += cross(rows[...], wu0[...])
-    up_acc[:, right] += cross(rows[...], wu1[...])
-
-    @pl.when(step == 3)
-    def _():
-        chunk = gate_acc.shape[0] // 8
-
-        @pl.loop(0, 8)
-        def _(i):
-            at = pl.ds(pl.multiple_of(i * chunk, chunk), chunk)
-            gate, up = gate_acc[at], up_acc[at]
-            sig = jax.nn.sigmoid(gate)
-            silu = gate * sig
-            hidden = (silu * up).astype(bf16)
-            silu_ref[at] = silu
-            slope_ref[at] = up * (sig * (1.0 + gate * (1.0 - sig)))
-            hidden_ref[at] = hidden
-            score = jnp.sum(hidden.astype(f32) * rh_ref[...], axis=1, keepdims=True)
-            gate_acc[at, pl.ds(0, 128)] = score * meta_ref[at].astype(f32)
-
-        scores = gate_acc[:, pl.ds(0, 128)].reshape(score_ref.shape[0], -1, 128)
-        scores = jnp.sum(scores, axis=1)
-        lane = lax.broadcasted_iota(jnp.int32, scores.shape, 1)
-        first = jnp.sum(jnp.where(lane < 2, scores, 0.0), axis=1, keepdims=True)
-        second = jnp.sum(jnp.where(lane < 2, 0.0, scores), axis=1, keepdims=True)
-        score_ref[...] = jnp.where(lane == 0, first, second)
-
-
-def down_kernel(y_ref, hidden_ref, wd0, wd1, *refs):
-    out_refs, rows = refs[:5], refs[5]
+        for acc in accs:
+            acc[...] = jnp.zeros_like(acc)
+
+    for k, ref in enumerate(x_refs):
+
+        @pl.when(step == k)
+        def _(ref=ref):
+            rows[...] = ref[...]
+
+    chunk = rows.shape[0] // 2
+
+    @pl.loop(0, 2)
+    def _(i):
+        at = pl.ds(pl.multiple_of(i * chunk, chunk), chunk)
+        for j, weight in enumerate(weights):
+            accs[j // 2][at, pl.ds(j % 2 * width, width)] += cross(rows[at], weight[...])
+
+
+def fwd_kernel(y_ref, *refs):
+    far_refs = refs[:2]
+    wg0, wg1, wu0, wu1, rh_ref, meta_ref, gate_ref, up_ref = refs[2:10]
+    slope_ref, silu_ref, hidden_ref, score_ref = refs[10:14]
+    gate_acc, up_acc, rows = refs[14:]
+    half, width = rows.shape[0] // 2, wg0.shape[0]
+    left, right = pl.ds(0, width), pl.ds(width, width)
+    rows[pl.ds(0, half)] = far_refs[0][...]
+    rows[pl.ds(half, half)] = far_refs[1][...]
+    gate_acc[:, left] = gate_ref[:, left] + cross(rows[...], wg0[...])
+    gate_acc[:, right] = gate_ref[:, right] + cross(rows[...], wg1[...])
+    up_acc[:, left] = up_ref[:, left] + cross(rows[...], wu0[...])
+    up_acc[:, right] = up_ref[:, right] + cross(rows[...], wu1[...])
+    finish_forward(
+        rh_ref, meta_ref, slope_ref, silu_ref, hidden_ref, score_ref, gate_acc, up_acc
+    )
+
+
+def finish_forward(
+    rh_ref, meta_ref, slope_ref, silu_ref, hidden_ref, score_ref, gate_acc, up_acc
+):
+    chunk = gate_acc.shape[0] // 8
+
+    @pl.loop(0, 8)
+    def _(i):
+        at = pl.ds(pl.multiple_of(i * chunk, chunk), chunk)
+        gate, up = gate_acc[at], up_acc[at]
+        sig = jax.nn.sigmoid(gate)
+        silu = gate * sig
+        hidden = (silu * up).astype(bf16)
+        silu_ref[at] = silu
+        slope_ref[at] = up * (sig * (1.0 + gate * (1.0 - sig)))
+        hidden_ref[at] = hidden
+        score = jnp.sum(hidden.astype(f32) * rh_ref[...], axis=1, keepdims=True)
+        gate_acc[at, pl.ds(0, 128)] = score * meta_ref[at].astype(f32)
+
+    scores = gate_acc[:, pl.ds(0, 128)].reshape(score_ref.shape[0], -1, 128)
+    scores = jnp.sum(scores, axis=1)
+    lane = lax.broadcasted_iota(jnp.int32, scores.shape, 1)
+    first = jnp.sum(jnp.where(lane < 2, scores, 0.0), axis=1, keepdims=True)
+    second = jnp.sum(jnp.where(lane < 2, 0.0, scores), axis=1, keepdims=True)
+    score_ref[...] = jnp.where(lane == 0, first, second)
+
+
+def down_kernel(y_ref, hidden_ref, wd0, wd1, low_ref, high_ref):
+    width, half = wd0.shape[0], low_ref.shape[0]
+    left, right = pl.ds(0, width), pl.ds(width, width)
+    for i, ref in enumerate((low_ref, high_ref)):
+        at = pl.ds(i * half, half)
+        ref[...] = (
+            plain(hidden_ref[at, left], wd0[...]) + plain(hidden_ref[at, right], wd1[...])
+        ).astype(bf16)
+
+
+def side_kernel(y_ref, hidden_ref, wd0, wd1, *refs):
+    out_refs, rows = refs[:3], refs[3]
     width = wd0.shape[0]
     left, right = pl.ds(0, width), pl.ds(width, width)
-    rows[...] = (
-        plain(hidden_ref[:, left], wd0[...]) + plain(hidden_ref[:, right], wd1[...])
-    ).astype(bf16)
-    store_piece(pl.program_id(0), out_refs, rows)
+    chunk = rows.shape[0] // 2
+
+    @pl.loop(0, 2)
+    def _(i):
+        at = pl.ds(pl.multiple_of(i * chunk, chunk), chunk)
+        rows[at] = (
+            plain(hidden_ref[at, left], wd0[...]) + plain(hidden_ref[at, right], wd1[...])
+        ).astype(bf16)
+
+    for k, ref in enumerate(out_refs):
+
+        @pl.when(pl.program_id(0) == k)
+        def _(ref=ref):
+            ref[...] = rows[...]
 
 
 def back_kernel(y_ref, *refs):
@@ -190,62 +225,84 @@
 
 def bwd_kernel(y_ref, *refs):
     wg0, wg1, wu0, wu1, rh_ref, meta_ref, seq_ref, partial_ref, slope_ref, silu_ref = refs[:10]
-    gate_grad_ref, up_grad_ref, coef_ref = refs[10:13]
-    out_refs, rows = refs[13:18], refs[18]
+    gate_grad_ref, up_grad_ref, coef_ref, low_ref, high_ref = refs[10:15]
+    width, half = wg0.shape[0], low_ref.shape[0]
+    left, right = pl.ds(0, width), pl.ds(width, width)
+    count = partial_ref.shape[0]
+    blocks = seq_ref.shape[0]
+    lane = lax.broadcasted_iota(jnp.int32, (blocks, 128), 1)
+    first = jnp.broadcast_to(seq_ref[:, pl.ds(0, 1)], lane.shape)
+    second = jnp.broadcast_to(seq_ref[:, pl.ds(1, 1)], lane.shape)
+    by_lane = jnp.where(lane < 2, first, jnp.where(lane < 4, second, 0.0))
+    shares = meta_ref[...].astype(f32).reshape(blocks, count // blocks, 128)
+    terms = (shares * by_lane[:, None, :]).reshape(count, 128)
+    coef_ref[...] = jnp.sum(terms, axis=1, keepdims=True)
+    chunk = count // 8
+
+    @pl.loop(0, 8)
+    def _(i):
+        at = pl.ds(pl.multiple_of(i * chunk, chunk), chunk)
+        hidden_grad = partial_ref[at] + coef_ref[at] * rh_ref[...]
+        gate_grad_ref[at] = (hidden_grad * slope_ref[at]).astype(bf16)
+        up_grad_ref[at] = (hidden_grad * silu_ref[at]).astype(bf16)
+
+    for i, ref in enumerate((low_ref, high_ref)):
+        at = pl.ds(i * half, half)
+        ref[...] = (
+            plain(gate_grad_ref[at, left], wg0[...])
+            + plain(gate_grad_ref[at, right], wg1[...])
+            + plain(up_grad_ref[at, left], wu0[...])
+            + plain(up_grad_ref[at, right], wu1[...])
+        ).astype(bf16)
+
+
+def rest_kernel(y_ref, *refs):
+    wg0, wg1, wu0, wu1, gate_grad_ref, up_grad_ref = refs[:6]
+    out_refs, rows = refs[6:9], refs[9]
     width = wg0.shape[0]
     left, right = pl.ds(0, width), pl.ds(width, width)
-    step = pl.program_id(0)
-
-    @pl.when(step == 0)
-    def _():
-        count = partial_ref.shape[0]
-        blocks = seq_ref.shape[0]
-        lane = lax.broadcasted_iota(jnp.int32, (blocks, 128), 1)
-        first = jnp.broadcast_to(seq_ref[:, pl.ds(0, 1)], lane.shape)
-        second = jnp.broadcast_to(seq_ref[:, pl.ds(1, 1)], lane.shape)
-        by_lane = jnp.where(lane < 2, first, jnp.where(lane < 4, second, 0.0))
-        shares = meta_ref[...].astype(f32).reshape(blocks, count // blocks, 128)
-        terms = (shares * by_lane[:, None, :]).reshape(count, 128)
-        coef_ref[...] = jnp.sum(terms, axis=1, keepdims=True)
-        chunk = count // 8
-
-        @pl.loop(0, 8)
-        def _(i):
-            at = pl.ds(pl.multiple_of(i * chunk, chunk), chunk)
-            hidden_grad = partial_ref[at] + coef_ref[at] * rh_ref[...]
-            gate_grad_ref[at] = (hidden_grad * slope_ref[at]).astype(bf16)
-            up_grad_ref[at] = (hidden_grad * silu_ref[at]).astype(bf16)
-
-    rows[...] = (
-        plain(gate_grad_ref[:, left], wg0[...])
-        + plain(gate_grad_ref[:, right], wg1[...])
-        + plain(up_grad_ref[:, left], wu0[...])
-        + plain(up_grad_ref[:, right], wu1[...])
-    ).astype(bf16)
-    store_piece(step, out_refs, rows)
+    chunk = rows.shape[0] // 2
+
+    @pl.loop(0, 2)
+    def _(i):
+        at = pl.ds(pl.multiple_of(i * chunk, chunk), chunk)
+        rows[at] = (
+            plain(gate_grad_ref[at, left], wg0[...])
+            + plain(gate_grad_ref[at, right], wg1[...])
+            + plain(up_grad_ref[at, left], wu0[...])
+            + plain(up_grad_ref[at, right], wu1[...])
+        ).astype(bf16)
+
+    for k, ref in enumerate(out_refs):
+
+        @pl.when(pl.program_id(0) == k)
+        def _(ref=ref):
+            ref[...] = rows[...]
 
 
 def grad_kernel(y_ref, *refs):
     x_refs, u_refs = refs[:5], refs[5:10]
     hidden_ref, gate_grad_ref, up_grad_ref, coef_ref, rh_ref = refs[10:15]
-    own_refs, other_ref = refs[15:18], refs[18]
-    left, rows = refs[19:]
-    width = own_refs[0].shape[0]
+    own_ref, other_ref, left, rows = refs[15:]
+    width = left.shape[1]
     step = pl.program_id(0)
 
     @pl.when(step == 0)
     def _():
         for i, ref in enumerate((gate_grad_ref, up_grad_ref, hidden_ref)):
-            left[i] = ref[...].T
-
-    load_piece(step, x_refs, rows)
-    for i in (0, 1, 2):
-        if i == 2:
-            load_piece(step, u_refs, rows)
-            rows[...] = (rows[...].astype(f32) + coef_ref[...] * rh_ref[...]).astype(bf16)
-        total = plain(left[i], rows[...])
-        own_refs[i][...] = total[:width].astype(bf16)
-        other_ref[pl.ds(i * width, width)] = total[width:].astype(bf16)
+            turned = ref[...].T
+            left[2 * i] = turned[:width]
+            left[2 * i + 1] = turned[width:]
+
+    load_piece(step, x_refs, rows.at[0])
+    load_piece(step, u_refs, rows.at[1])
+    rows[1] = (rows[1].astype(f32) + coef_ref[...] * rh_ref[...]).astype(bf16)
+
+    @pl.loop(0, 3)
+    def _(i):
+        at = pl.ds(pl.multiple_of(i * width, width), width)
+        own_ref[at] = plain(left[2 * i], rows[i // 2]).astype(bf16)
+        other_ref[at] = plain(left[2 * i + 1], rows[i // 2]).astype(bf16)
 
 
 def whole(shape):
@@ -254,6 +311,14 @@
 
 def columns(width, block):
     return pl.BlockSpec((width, block), lambda k, y: (0, (y[0] + k) % 4))
+
+
+def near_columns(width, block):
+    return pl.BlockSpec((width, block), lambda k, y: (0, (y[0] + k + k // 2) % 4))
+
+
+def far_columns(width, block):
+    return pl.BlockSpec((width, block), lambda k, y: (0, (y[0] + 2) % 4))
 
 
 def piece_specs(rows, block):
@@ -261,18 +326,12 @@
     return [full, full, part, part, full]
 
 
-def piece_shapes(rows, block):
-    full = jax.ShapeDtypeStruct((rows, block), bf16)
-    part = jax.ShapeDtypeStruct((rows // 2, block), bf16)
-    return [full, full, part, part, full]
-
-
-def call(kernel, in_specs, out_specs, out_shape, scratch, flops, args):
+def call(kernel, steps, in_specs, out_specs, out_shape, scratch, flops, args):
     return pl.pallas_call(
         kernel,
         grid_spec=pltpu.PrefetchScalarGridSpec(
             num_scalar_prefetch=1,
-            grid=(4,),
+            grid=(steps,),
             in_specs=in_specs,
             out_specs=out_specs,
             scratch_shapes=scratch,
@@ -362,17 +421,32 @@
     slots_hid = (rows, 2 * hid)
     meta_spec = pl.BlockSpec((rows, 128), lambda k, y: (0, block // 128))
     work = rows * 2 * hid * 4 * block
+    own_rows, ahead_rows, far_low, far_high, back_rows = token_pieces
+    gate_weights = (w_gate, wg_other, w_up, wu_other)
+    full, part = whole((rows, block)), whole((rows // 2, block))
+    gate, up = call(
+        near_kernel,
+        3,
+        [full] * 3 + [near_columns(hid, block)] * 4,
+        [whole(slots_hid)] * 2,
+        [jax.ShapeDtypeStruct(slots_hid, f32)] * 2,
+        [pltpu.VMEM((rows, block), bf16)],
+        3 * work,
+        (place, own_rows, ahead_rows, back_rows, *gate_weights),
+    )
     slope, silu, hidden, score = call(
         fwd_kernel,
-        piece_specs(rows, block)
-        + [columns(hid, block)] * 4
-        + [whole((1, 2 * hid)), meta_spec],
+        1,
+        [part] * 2
+        + [far_columns(hid, block)] * 4
+        + [whole((1, 2 * hid)), meta_spec]
+        + [whole(slots_hid)] * 2,
         [whole(slots_hid)] * 3 + [whole((ep_size, 128))],
         [jax.ShapeDtypeStruct(slots_hid, f32)] * 2
         + [jax.ShapeDtypeStruct(slots_hid, bf16), jax.ShapeDtypeStruct((ep_size, 128), f32)],
         [pltpu.VMEM(slots_hid, f32)] * 2 + [pltpu.VMEM((rows, block), bf16)],
-        4 * work,
-        (place, *token_pieces, w_gate, wg_other, w_up, wu_other, head_row, grad_full),
+        work,
+        (place, far_low, far_high, *gate_weights, head_row, grad_full, gate, up),
     )
     placed = (placed + score[:, :seq_local].reshape(seq_total)).reshape(2, 1, seq_total // 2)
     everyone = lax.axis_size(EP_TP)
@@ -380,17 +454,32 @@
     spread = lax.all_to_all(spread, EP_TP, split_axis=1, concat_axis=1, tiled=True)
     rewards = jnp.sum(spread, axis=1).reshape(seq_total) / math.sqrt(SEQ_LEN)
 
-    down_pieces = call(
+    half_shape = jax.ShapeDtypeStruct((rows // 2, block), bf16)
+    full_shape = jax.ShapeDtypeStruct((rows, block), bf16)
+    down_low, down_high = call(
         down_kernel,
-        [whole(slots_hid)] + [columns(hid, block)] * 2,
-        piece_specs(rows, block),
-        piece_shapes(rows, block),
+        1,
+        [whole(slots_hid)] + [far_columns(hid, block)] * 2,
+        [part] * 2,
+        [half_shape] * 2,
+        [],
+        work // 2,
+        (place, hidden, w_down, wd_other),
+    )
+    down_own, down_ahead, down_back = call(
+        side_kernel,
+        3,
+        [whole(slots_hid)] + [near_columns(hid, block)] * 2,
+        [full] * 3,
+        [full_shape] * 3,
         [pltpu.VMEM((rows, block), bf16)],
-        2 * work,
+        3 * work // 2,
         (place, hidden, w_down, wd_other),
     )
+    down_pieces = (down_own, down_ahead, down_low, down_high, down_back)
     partial = call(
         back_kernel,
+        4,
         piece_specs(rows, block) + [columns(hid, block)] * 2,
         [whole(slots_hid)],
         [jax.ShapeDtypeStruct(slots_hid, f32)],
@@ -414,37 +503,48 @@
     ).astype(bf16)
     scaled = (seq_coef * (loss_scale / math.sqrt(SEQ_LEN))).reshape(ep_size, seq_local)
 
-    gate_grad, up_grad, slot_coef, *input_pieces = call(
+    gate_grad, up_grad, slot_coef, far_low, far_high = call(
         bwd_kernel,
-        [columns(hid, block)] * 4
+        1,
+        [far_columns(hid, block)] * 4
         + [whole((1, 2 * hid)), meta_spec, whole((ep_size, seq_local))]
         + [whole(slots_hid)] * 3,
-        [whole(slots_hid)] * 2 + [whole((rows, 1))] + piece_specs(rows, block),
+        [whole(slots_hid)] * 2 + [whole((rows, 1))] + [part] * 2,
         [jax.ShapeDtypeStruct(slots_hid, bf16)] * 2
         + [jax.ShapeDtypeStruct((rows, 1), f32)]
-        + piece_shapes(rows, block),
+        + [jax.ShapeDtypeStruct((rows // 2, block), bf16)] * 2,
+        [],
+        work,
+        (place, *gate_weights, head_row, grad_full, scaled, partial, slope, silu),
+    )
+    own_sums, ahead_sums, back_sums = call(
+        rest_kernel,
+        3,
+        [near_columns(hid, block)] * 4 + [whole(slots_hid)] * 2,
+        [full] * 3,
+        [jax.ShapeDtypeStruct((rows, block), bf16)] * 3,
         [pltpu.VMEM((rows, block), bf16)],
-        4 * work,
-        (place, w_gate, wg_other, w_up, wu_other, head_row, grad_full, scaled)
-        + (partial, slope, silu),
-    )
-    input_sums = scatter_start(input_pieces)
-
-    *own_grads, other_grads = call(
+        3 * work,
+        (place, *gate_weights, gate_grad, up_grad),
+    )
+    input_sums = scatter_start((own_sums, ahead_sums, far_low, far_high, back_sums))
+
+    own_grads, other_grads = call(
         grad_kernel,
+        4,
         piece_specs(rows, block) * 2
         + [whole(slots_hid)] * 3
         + [whole((rows, 1)), columns(1, block)],
-        [columns(hid, block)] * 3 + [columns(3 * hid, block)],
-        [jax.ShapeDtypeStruct((hid, 4 * block), bf16)] * 3
-        + [jax.ShapeDtypeStruct((3 * hid, 4 * block), bf16)],
-        [pltpu.VMEM((3, 2 * hid, rows), bf16), pltpu.VMEM((rows, block), bf16)],
+        [columns(3 * hid, block)] * 2,
+        [jax.ShapeDtypeStruct((3 * hid, 4 * block), bf16)] * 2,
+        [pltpu.VMEM((6, hid, rows), bf16), pltpu.VMEM((2, rows, block), bf16)],
         6 * work,
         (place, *token_pieces, *grad_pieces, hidden, gate_grad, up_grad, slot_coef, head[None, :]),
     )
     other_grads = swap(other_grads)
     grad_gate, grad_up, grad_down = (
-        add(own, other_grads[i * hid : (i + 1) * hid]) for i, own in enumerate(own_grads)
+        add(own_grads[i * hid : (i + 1) * hid], other_grads[i * hid : (i + 1) * hid])
+        for i in range(3)
     )
 
     def come_back(pieces):

time: 276 us -> 276 us (level)
  Pallas kernels: 46.7 us -> 54.5 us
  waiting for transfers between devices: 102 us -> 94.3 us
    pallas_call x5 -> x8, Pallas kernels: 46.7 us -> 54.5 us  [call(): pl.pallas_call(kernel, grid_spec=pltpu.PrefetchScalarGridSpec(num_scalar_...]
    ppermute x16, waiting for transfers between devices: 48 us -> 41.8 us  [rot(): return lax.ppermute(value, 'tp_y', [(i, (i + shift) % 4) for i in range(4)])]
  transfers between devices with their start and end apart: 28 -> 28, of which waited for: 14 -> 14; matrix products, arithmetic and copies ran while one was open for 9% -> 9% of each run, Pallas kernels for 17% -> 20%
where the time goes in v2:
time: 276 us; the launch traced here: 273 us
  waiting for transfers between devices  94.3 us (34%)
  starting transfers between devices  69.4 us (25%)
  Pallas kernels  54.5 us (20%)
  other arithmetic  19.3 us (7%)
  local copies, waits for them, and re-layouts  17 us (6%)
  blocking collectives  12.8 us (5%)
  matrix products  3.29 us (1%)
  between operations  2.97 us (1%)
    pallas_call x8, Pallas kernels, call(): pl.pallas_call(kernel, grid_spec=pltpu.PrefetchScalarGridSpec(num_scalar_...  54.5 us
    all_to_all x4, waiting for transfers between devices, exchange(): lax.all_to_all(blocks.transpose(1, 0, 2), EP, split_axis=1, concat_axis=1...  48.8 us
    ppermute x16, waiting for transfers between devices, rot(): return lax.ppermute(value, 'tp_y', [(i, (i + shift) % 4) for i in range(4)])  41.8 us
    all_to_all x4, starting transfers between devices, exchange(): lax.all_to_all(blocks.transpose(1, 0, 2), EP, split_axis=1, concat_axis=1...  36.8 us
    ppermute x16, starting transfers between devices, rot(): return lax.ppermute(value, 'tp_y', [(i, (i + shift) % 4) for i in range(4)])  20.5 us
    all_gather x1, blocking collectives, layer(): head = lax.all_gather(reward_head, TP, axis=0, tiled=True)  12.8 us
    convert_element_type x7, other arithmetic, add(): sum((t.astype(f32) for t in terms[1:]), terms[0].astype(f32)).astype(bf16)  12 us
    all_to_all x1, starting transfers between devices, layer(): lax.all_to_all(spread, EP_TP, split_axis=1, concat_axis=1, tiled=True)  11 us
  transfers between devices with their start and end apart: 28, of which 14 were waited for; matrix products, arithmetic and copies ran while one was open for 9% of the time, Pallas kernels for 20%

profile of v2, /device:TPU:32, one launch (start us, length us, event | category | flops | bytes accessed | tf_op | source)
XLA Modules:
  0.0 273.5 jit_solution(9210463809767438758)
XLA Ops:
  4.4 1.3 fusion
  5.9 1.4 collective-permute-done
  9.0 11.2 %all-to-all-start = ((bf16[16,32,768]{2,0,1:T(8,128)(2,1)}), bf16[16,32,768]{2,0,1:T(8,128)(2,1)}, u32[]{:S(2)}, u32[]{:S(2)}) async-start(bf16[16,32,768]{2,0,1:T(8,128)(2,1)} %bitcast.12), calls=%async_computation | async-start | bytes 1572864 | tf_op jit(solution)/shard_map/all_to_all | solution.py:55
  21.8 21.7 %all-to-all-done = bf16[16,32,768]{2,0,1:T(8,128)(2,1)} async-done(((bf16[16,32,768]{2,0,1:T(8,128)(2,1)}), bf16[16,32,768]{2,0,1:T(8,128)(2,1)}, u32[]{:S(2)}, u32[]{:S(2)}) %all-to-all-start) | async-done | bytes 786464 | tf_op jit(solution)/shard_map/all_to_all | solution.py:55
  44.6 5.2 %all-to-all-start.1 = ((bf16[16,32,896]{2,0,1:T(8,128)(2,1)}), bf16[16,32,896]{2,0,1:T(8,128)(2,1)}, u32[]{:S(2)}, u32[]{:S(2)}) async-start(bf16[16,32,896]{2,0,1:T(8,128)(2,1)} %bitcast.53), calls=%async_computation.1 | async-start | bytes 1835008 | tf_op jit(solution)/shard_map/all_to_all | solution.py:55
  50.9 12.8 %all-gather = f32[8,1,384]{2,1,0:T(1,128)S(1)} all-gather(f32[1,1,384]{2,1,0:T(1,128)S(1)} %reshape.176), channel_id=1, replica_groups=mesh['ep_x'=4,'ep_z'=8,'tp_y'=4,'tp_c'=2] {'tp_y','tp_c'}, dimensions={0}, use_global_device_ids=true | all-gather | bytes 13824 | tf_op jit(solution)/shard_map/all_gather | solution.py:407
  65.4 1.3 collective-permute-start.2
  66.7 2.0 collective-permute-start.4
  68.6 6.6 %all-to-all-done.1 = bf16[16,32,896]{2,0,1:T(8,128)(2,1)} async-done(((bf16[16,32,896]{2,0,1:T(8,128)(2,1)}), bf16[16,32,896]{2,0,1:T(8,128)(2,1)}, u32[]{:S(2)}, u32[]{:S(2)}) %all-to-all-start.1) | async-done | bytes 917536 | tf_op jit(solution)/shard_map/all_to_all | solution.py:55
  75.2 1.2 slice.147.refs_0_.refs_5_
  76.5 1.7 collective-permute-start.14
  78.1 9.1 %collective-permute-done.2.refs_2_.refs_4_ = bf16[512,768]{1,0:T(8,128)(2,1)S(1)} collective-permute-done((bf16[512,768]{1,0:T(8,128)(2,1)}, bf16[512,768]{1,0:T(8,128)(2,1)S(1)}, u32[]{:S(2)}, u32[]{:S(2)}) %collective-permute-start.2) | collective-permute-done | bytes 786464 | tf_op jit(solution)/shard_map/ppermute | solution.py:47
  88.3 1.8 collective-permute-start.3
  90.1 1.8 slice.140
  91.9 1.5 collective-permute-start.5
  93.6 7.7 %shard_map.144 = (f32[512,512]{1,0:T(8,128)}, f32[512,512]{1,0:T(8,128)}) custom-call(s32[1]{0:T(128)} %bitcast.6.y_ref, bf16[512,768]{1,0:T(8,128)(2,1)} %bitcast.14.refs_0_, bf16[512,768]{1,0:T(8,128)(2,1)} %collective-permute-done.4.refs_1_, bf16[512,768]{1,0:T(8,128)(2,1)} %copy-done.17, bf16[256,3072]{1,0:T(8,128)(2,1)} %refs_0_.3, ...), custom_call_target="tpu_custom_call" | custom-call | flops 2415919104 | bytes 20000000 | tf_op jit(solution)/shard_map/pallas_call | solution.py:330
  101.3 2.8 %collective-permute-done.14.refs_4_.refs_9_ = bf16[512,768]{1,0:T(8,128)(2,1)S(1)} collective-permute-done((bf16[512,768]{1,0:T(8,128)(2,1)S(1)}, bf16[512,768]{1,0:T(8,128)(2,1)S(1)}, u32[]{:S(2)}, u32[]{:S(2)}) %collective-permute-start.14) | collective-permute-done | bytes 786464 | tf_op jit(solution)/shard_map/ppermute | solution.py:47
  104.5 3.2 %collective-permute-done.13.refs_1_.refs_6_ = bf16[512,768]{1,0:T(8,128)(2,1)S(1)} collective-permute-done((bf16[512,768]{1,0:T(8,128)(2,1)S(1)}, bf16[512,768]{1,0:T(8,128)(2,1)S(1)}, u32[]{:S(2)}, u32[]{:S(2)}) %collective-permute-start.13) | collective-permute-done | bytes 786464 | tf_op jit(solution)/shard_map/ppermute | solution.py:47
  108.5 1.2 collective-permute-start.16
  109.7 2.8 %collective-permute-done.3.refs_0_.refs_2_ = bf16[256,768]{1,0:T(8,128)(2,1)S(1)} collective-permute-done((bf16[256,768]{1,0:T(8,128)(2,1)}, bf16[256,768]{1,0:T(8,128)(2,1)S(1)}, u32[]{:S(2)}, u32[]{:S(2)}) %collective-permute-start.3) | collective-permute-done | bytes 393248 | tf_op jit(solution)/shard_map/ppermute | solution.py:47
  112.5 3.6 %collective-permute-done.5.refs_1_.refs_3_ = bf16[256,768]{1,0:T(8,128)(2,1)S(1)} collective-permute-done((bf16[256,768]{1,0:T(8,128)(2,1)}, bf16[256,768]{1,0:T(8,128)(2,1)S(1)}, u32[]{:S(2)}, u32[]{:S(2)}) %collective-permute-start.5) | collective-permute-done | bytes 393248 | tf_op jit(solution)/shard_map/ppermute | solution.py:47
  116.9 5.9 %shard_map.145 = (f32[512,512]{1,0:T(8,128)}, f32[512,512]{1,0:T(8,128)}, bf16[512,512]{1,0:T(8,128)(2,1)}, f32[32,128]{1,0:T(8,128)}) custom-call(s32[1]{0:T(128)} %bitcast.6.y_ref, bf16[256,768]{1,0:T(8,128)(2,1)} %copy-done.13, bf16[256,768]{1,0:T(8,128)(2,1)} %copy-done.14, bf16[256,3072]{1,0:T(8,128)(2,1)} %refs_0_.3, ...), custom_call_target="tpu_custom_call" | custom-call | flops 805306368 | bytes 20000000 | tf_op jit(solution)/shard_map/pallas_call | solution.py:330
  124.5 11.0 %all-to-all-start.3 = ((f32[2,256,32]{2,0,1:T(2,128)}), f32[2,256,32]{2,0,1:T(2,128)S(1)}, u32[]{:S(2)}, u32[]{:S(2)}) async-start(f32[2,256,32]{2,0,1:T(2,128)} %broadcast_in_dim.81), calls=%async_computation.3 | async-start | bytes 524288 | tf_op jit(solution)/shard_map/all_to_all | solution.py:454
  135.5 2.6 shard_map.147
  138.1 2.9 %collective-permute-start.10 = (bf16[256,768]{1,0:T(8,128)(2,1)}, bf16[256,768]{1,0:T(8,128)(2,1)S(1)}, u32[]{:S(2)}, u32[]{:S(2)}) collective-permute-start(bf16[256,768]{1,0:T(8,128)(2,1)} %get-tuple-element.40), channel_id=1, source_target_pairs={{0,6},{2,0},{4,2},{6,4},{1,7},{3,1},{5,3},{7,5},{8,14},{10,8},{12,... | collective-permute-start | bytes 1179656 | tf_op jit(solution)/shard_map/ppermute | solution.py:47
  141.0 5.4 %shard_map.146 = (bf16[512,768]{1,0:T(8,128)(2,1)}, bf16[512,768]{1,0:T(8,128)(2,1)}, bf16[512,768]{1,0:T(8,128)(2,1)}) custom-call(s32[1]{0:T(128)} %bitcast.6.y_ref, bf16[512,512]{1,0:T(8,128)(2,1)} %get-tuple-element.35.hidden_ref.refs_10_, bf16[256,3072]{1,0:T(8,128)(2,1)} %refs_5_.3, bf16[256,3072]{1,0:T(8,128)(2,1)} %copy-done.1), custom_call_target="tpu_custom_call" | custom-call | flops 1207959552 | bytes 20000000 | tf_op jit(solution)/shard_map/pallas_call | solution.py:330
  146.4 1.0 slice.115
  147.5 1.0 slice.114
  148.6 1.4 all-to-all-done.3
  152.0 6.4 %shard_map.148.refs_7_ = f32[512,512]{1,0:T(8,128)} custom-call(s32[1]{0:T(128)} %bitcast.6.y_ref, bf16[512,768]{1,0:T(8,128)(2,1)} %copy-done.2, bf16[512,768]{1,0:T(8,128)(2,1)} %copy-done.4, bf16[256,768]{1,0:T(8,128)(2,1)} %collective-permute-done.15.refs_2_.refs_7_, bf16[256,768]{1,0:T(8,128)(2,1)} %collective-permute-done.16.refs_3_.refs_8_, ...), custom_call_target="tpu_custom_call" | custom-call | flops 1610612736 | bytes 20000000 | tf_op jit(solution)/shard_map/pallas_call | solution.py:330
  158.4 5.3 %shard_map.149 = (bf16[512,512]{1,0:T(8,128)(2,1)}, bf16[512,512]{1,0:T(8,128)(2,1)}, f32[512,1]{1,0:T(8,128)}, bf16[256,768]{1,0:T(8,128)(2,1)}, bf16[256,768]{1,0:T(8,128)(2,1)}) custom-call(s32[1]{0:T(128)} %bitcast.6.y_ref, bf16[256,3072]{1,0:T(8,128)(2,1)} %refs_0_.3, bf16[256,3072]{1,0:T(8,128)(2,1)} %collective-permute-done.6.refs_4_.refs_3_.refs_1_, ...), custom_call_target="tpu_custom_call" | custom-call | flops 805306368 | bytes 20000000 | tf_op jit(solution)/shard_map/pallas_call | solution.py:330
  163.7 1.8 collective-permute-start.19
  166.6 1.4 collective-permute-start.9
  168.1 7.1 %shard_map.150 = (bf16[512,768]{1,0:T(8,128)(2,1)}, bf16[512,768]{1,0:T(8,128)(2,1)}, bf16[512,768]{1,0:T(8,128)(2,1)}) custom-call(s32[1]{0:T(128)} %bitcast.6.y_ref, bf16[256,3072]{1,0:T(8,128)(2,1)} %refs_0_.3, bf16[256,3072]{1,0:T(8,128)(2,1)} %collective-permute-done.6.refs_4_.refs_3_.refs_1_, bf16[256,3072]{1,0:T(8,128)(2,1)} %refs_2_.5, ...), custom_call_target="tpu_custom_call" | custom-call | flops 2415919104 | bytes 20000000 | tf_op jit(solution)/shard_map/pallas_call | solution.py:330
  175.1 1.0 slice.127
  176.2 1.0 slice.126
  177.6 14.1 %shard_map.151 = (bf16[768,3072]{1,0:T(8,128)(2,1)}, bf16[768,3072]{1,0:T(8,128)(2,1)}) custom-call(s32[1]{0:T(128)} %bitcast.6.y_ref, bf16[512,768]{1,0:T(8,128)(2,1)} %bitcast.14.refs_0_, bf16[512,768]{1,0:T(8,128)(2,1)} %collective-permute-done.4.refs_1_, bf16[256,768]{1,0:T(8,128)(2,1)} %copy-done.13, bf16[256,768]{1,0:T(8,128)(2,1)} %copy-done.14, ...), custom_call_target="tpu_custom_call" | custom-call | flops 4831838208 | bytes 20000000 | tf_op jit(solution)/shard_map/pallas_call | solution.py:330
  191.8 1.2 add_convert_fusion.5
  193.0 2.6 add_convert_fusion.4
  195.6 10.6 %all-to-all-start.2 = ((bf16[16,32,768]{2,0,1:T(8,128)(2,1)}), bf16[16,32,768]{2,0,1:T(8,128)(2,1)S(1)}, u32[]{:S(2)}, u32[]{:S(2)}) async-start(bf16[16,32,768]{2,0,1:T(8,128)(2,1)} %bitcast.23), calls=%async_computation.2 | async-start | bytes 1572864 | tf_op jit(solution)/shard_map/all_to_all | solution.py:55
  206.3 3.3 %collective-permute-start.20 = (bf16[512,768]{1,0:T(8,128)(2,1)S(1)}, bf16[512,768]{1,0:T(8,128)(2,1)S(1)}, u32[]{:S(2)}, u32[]{:S(2)}) collective-permute-start(bf16[512,768]{1,0:T(8,128)(2,1)S(1)} %pad_maximum_fusion.3), channel_id=1, source_target_pairs={{0,6},{2,0},{4,2},{6,4},{1,7},{3,1},{5,3},{7,5},{8,14},{10,8},{12,... | collective-permute-start | bytes 2359304 | tf_op jit(solution)/shard_map/ppermute | solution.py:47
  209.6 1.1 add_convert_fusion.6
  210.8 15.6 %collective-permute-done.20 = bf16[512,768]{1,0:T(8,128)(2,1)S(1)} collective-permute-done((bf16[512,768]{1,0:T(8,128)(2,1)S(1)}, bf16[512,768]{1,0:T(8,128)(2,1)S(1)}, u32[]{:S(2)}, u32[]{:S(2)}) %collective-permute-start.20) | collective-permute-done | bytes 786464 | tf_op jit(solution)/shard_map/ppermute | solution.py:47
  226.4 4.6 %collective-permute-done.18 = bf16[512,768]{1,0:T(8,128)(2,1)S(1)} collective-permute-done((bf16[512,768]{1,0:T(8,128)(2,1)S(1)}, bf16[512,768]{1,0:T(8,128)(2,1)S(1)}, u32[]{:S(2)}, u32[]{:S(2)}) %collective-permute-start.18) | collective-permute-done | bytes 786464 | tf_op jit(solution)/shard_map/ppermute | solution.py:47
  231.0 1.2 add_convert_fusion.3
  232.2 9.8 %all-to-all-start.4 = ((bf16[16,32,768]{2,0,1:T(8,128)(2,1)}), bf16[16,32,768]{2,0,1:T(8,128)(2,1)S(1)}, u32[]{:S(2)}, u32[]{:S(2)}) async-start(bf16[16,32,768]{2,0,1:T(8,128)(2,1)} %bitcast.29), calls=%async_computation.4 | async-start | bytes 1572864 | tf_op jit(solution)/shard_map/all_to_all | solution.py:55
  243.6 20.4 %all-to-all-done.4 = bf16[16,32,768]{2,0,1:T(8,128)(2,1)S(1)} async-done(((bf16[16,32,768]{2,0,1:T(8,128)(2,1)}), bf16[16,32,768]{2,0,1:T(8,128)(2,1)S(1)}, u32[]{:S(2)}, u32[]{:S(2)}) %all-to-all-start.4) | async-done | bytes 786464 | tf_op jit(solution)/shard_map/all_to_all | solution.py:55
  266.5 5.9 %add_convert_fusion = (bf16[256,3072]{1,0:T(8,128)(2,1)}, bf16[256,3072]{1,0:T(8,128)(2,1)}, bf16[256,3072]{1,0:T(8,128)(2,1)}) fusion(bf16[768,3072]{1,0:T(8,128)(2,1)} %collective-permute-done.22, bf16[768,3072]{1,0:T(8,128)(2,1)} %get-tuple-element.53), kind=kLoop, calls=%fused_computation | loop fusion | flops 9437184 | bytes 14155776 | tf_op jit(solution)/shard_map/convert_element_type | solution.py:69
  (154 shorter events, 23.0 us)
Async XLA Ops:
  4.4 16.0 %copy-start.11 = (f32[128,256]{1,0:T(8,128)}, f32[128,256]{1,0:T(8,128)S(1)}, u32[]{:S(2)}) copy-start(f32[128,256]{1,0:T(8,128)S(1)} %get-tuple-element.58) | copy-start | bytes 393220
  5.8 1.5 collective-permute-start
  8.0 12.2 %copy-start = (bf16[256,3072]{1,0:T(8,128)(2,1)S(1)}, bf16[256,3072]{1,0:T(8,128)(2,1)}, u32[]{:S(2)}) copy-start(bf16[256,3072]{1,0:T(8,128)(2,1)} %refs_5_.3) | copy-start | bytes 4718596
  9.0 34.6 %all-to-all-start = ((bf16[16,32,768]{2,0,1:T(8,128)(2,1)}), bf16[16,32,768]{2,0,1:T(8,128)(2,1)}, u32[]{:S(2)}, u32[]{:S(2)}) async-start(bf16[16,32,768]{2,0,1:T(8,128)(2,1)} %bitcast.12), calls=%async_computation | async-start | bytes 1572864 | tf_op jit(solution)/shard_map/all_to_all | solution.py:55
  20.2 43.4 %collective-permute-start.1 = (bf16[256,3072]{1,0:T(8,128)(2,1)S(1)}, bf16[256,3072]{1,0:T(8,128)(2,1)S(1)}, u32[]{:S(2)}, u32[]{:S(2)}) collective-permute-start(bf16[256,3072]{1,0:T(8,128)(2,1)S(1)} %copy-done), channel_id=1, source_target_pairs={{0,1},{1,0},{2,3},{3,2},{4,5},{5,4},{6,7},{7,6},{8,9},{9,8},{10,11... | collective-permute-start | bytes 4718600 | tf_op jit(solution)/shard_map/ppermute | solution.py:51
  21.8 28.5 %copy-start.21 = (f32[384]{0:T(512)S(1)}, f32[384]{0:T(512)}, u32[]{:S(2)}) copy-start(f32[384]{0:T(512)} %param.15) | copy-start | bytes 4612
  21.8 28.5 %copy-start.15 = (bf16[128,384]{1,0:T(8,128)(2,1)S(1)}, bf16[128,384]{1,0:T(8,128)(2,1)}, u32[]{:S(2)}) copy-start(bf16[128,384]{1,0:T(8,128)(2,1)} %param.9) | copy-start | bytes 294916
  44.6 30.7 %all-to-all-start.1 = ((bf16[16,32,896]{2,0,1:T(8,128)(2,1)}), bf16[16,32,896]{2,0,1:T(8,128)(2,1)}, u32[]{:S(2)}, u32[]{:S(2)}) async-start(bf16[16,32,896]{2,0,1:T(8,128)(2,1)} %bitcast.53), calls=%async_computation.1 | async-start | bytes 1835008 | tf_op jit(solution)/shard_map/all_to_all | solution.py:55
  49.7 42.1 %collective-permute-start.6 = (bf16[256,3072]{1,0:T(8,128)(2,1)}, bf16[256,3072]{1,0:T(8,128)(2,1)}, u32[]{:S(2)}, u32[]{:S(2)}) collective-permute-start(bf16[256,3072]{1,0:T(8,128)(2,1)} %refs_0_.3), channel_id=1, source_target_pairs={{0,1},{1,0},{2,3},{3,2},{4,5},{5,4},{6,7},{7,6},{8,9},{9,8},{10,11... | collective-permute-start | bytes 4718600 | tf_op jit(solution)/shard_map/ppermute | solution.py:51
  49.8 43.7 %collective-permute-start.7 = (bf16[256,3072]{1,0:T(8,128)(2,1)}, bf16[256,3072]{1,0:T(8,128)(2,1)}, u32[]{:S(2)}, u32[]{:S(2)}) collective-permute-start(bf16[256,3072]{1,0:T(8,128)(2,1)} %refs_2_.5), channel_id=1, source_target_pairs={{0,1},{1,0},{2,3},{3,2},{4,5},{5,4},{6,7},{7,6},{8,9},{9,8},{10,11... | collective-permute-start | bytes 4718600 | tf_op jit(solution)/shard_map/ppermute | solution.py:51
  50.9 13.5 %copy-start.27 = (f32[64]{0:T(128)}, f32[64]{0:T(128)S(1)}, u32[]{:S(2)}) copy-start(f32[64]{0:T(128)S(1)} %dynamic_update_slice.3) | copy-start | bytes 772
  65.4 21.8 %collective-permute-start.2 = (bf16[512,768]{1,0:T(8,128)(2,1)}, bf16[512,768]{1,0:T(8,128)(2,1)S(1)}, u32[]{:S(2)}, u32[]{:S(2)}) collective-permute-start(bf16[512,768]{1,0:T(8,128)(2,1)} %bitcast.14.refs_0_), channel_id=1, source_target_pairs={{0,2},{2,4},{4,6},{6,0},{1,3},{3,5},{5,7},{7,1},{8,10},{10,12},{12... | collective-permute-start | bytes 2359304 | tf_op jit(solution)/shard_map/ppermute | solution.py:47
  66.7 21.6 %collective-permute-start.4 = (bf16[512,768]{1,0:T(8,128)(2,1)}, bf16[512,768]{1,0:T(8,128)(2,1)}, u32[]{:S(2)}, u32[]{:S(2)}) collective-permute-start(bf16[512,768]{1,0:T(8,128)(2,1)} %bitcast.14.refs_0_), channel_id=1, source_target_pairs={{0,6},{2,0},{4,2},{6,4},{1,7},{3,1},{5,3},{7,5},{8,14},{10,8},{12,... | collective-permute-start | bytes 2359304 | tf_op jit(solution)/shard_map/ppermute | solution.py:47
  75.2 18.1 %copy-start.26 = (s32[64]{0:T(128)S(1)}, s32[64]{0:T(128)}, u32[]{:S(2)}) copy-start(s32[64]{0:T(128)} %param.17) | copy-start | bytes 772
  76.4 24.8 %copy-start.2 = (bf16[512,768]{1,0:T(8,128)(2,1)}, bf16[512,768]{1,0:T(8,128)(2,1)S(1)}, u32[]{:S(2)}) copy-start(bf16[512,768]{1,0:T(8,128)(2,1)S(1)} %slice.147.refs_0_.refs_5_) | copy-start | bytes 2359300
  76.5 27.6 %collective-permute-start.14 = (bf16[512,768]{1,0:T(8,128)(2,1)S(1)}, bf16[512,768]{1,0:T(8,128)(2,1)S(1)}, u32[]{:S(2)}, u32[]{:S(2)}) collective-permute-start(bf16[512,768]{1,0:T(8,128)(2,1)S(1)} %slice.147.refs_0_.refs_5_), channel_id=1, source_target_pairs={{0,2},{2,4},{4,6},{6,0},{1,3},{3,5},{5,7},{7,1},{8,10},{10,12},{12... | collective-permute-start | bytes 2359304 | tf_op jit(solution)/shard_map/ppermute | solution.py:47
  87.2 20.4 %collective-permute-start.13 = (bf16[512,768]{1,0:T(8,128)(2,1)S(1)}, bf16[512,768]{1,0:T(8,128)(2,1)S(1)}, u32[]{:S(2)}, u32[]{:S(2)}) collective-permute-start(bf16[512,768]{1,0:T(8,128)(2,1)S(1)} %slice.147.refs_0_.refs_5_), channel_id=1, source_target_pairs={{0,6},{2,0},{4,2},{6,4},{1,7},{3,1},{5,3},{7,5},{8,14},{10,8},{12,... | collective-permute-start | bytes 2359304 | tf_op jit(solution)/shard_map/ppermute | solution.py:47
  88.3 24.2 %collective-permute-start.3 = (bf16[256,768]{1,0:T(8,128)(2,1)}, bf16[256,768]{1,0:T(8,128)(2,1)S(1)}, u32[]{:S(2)}, u32[]{:S(2)}) collective-permute-start(bf16[256,768]{1,0:T(8,128)(2,1)} %slice.139), channel_id=1, source_target_pairs={{0,2},{2,4},{4,6},{6,0},{1,3},{3,5},{5,7},{7,1},{8,10},{10,12},{12... | collective-permute-start | bytes 1179656 | tf_op jit(solution)/shard_map/ppermute | solution.py:47
  91.9 24.2 %collective-permute-start.5 = (bf16[256,768]{1,0:T(8,128)(2,1)}, bf16[256,768]{1,0:T(8,128)(2,1)S(1)}, u32[]{:S(2)}, u32[]{:S(2)}) collective-permute-start(bf16[256,768]{1,0:T(8,128)(2,1)} %slice.140), channel_id=1, source_target_pairs={{0,6},{2,0},{4,2},{6,4},{1,7},{3,1},{5,3},{7,5},{8,14},{10,8},{12,... | collective-permute-start | bytes 1179656 | tf_op jit(solution)/shard_map/ppermute | solution.py:47
  104.1 18.7 %copy-start.3 = (bf16[512,768]{1,0:T(8,128)(2,1)}, bf16[512,768]{1,0:T(8,128)(2,1)S(1)}, u32[]{:S(2)}) copy-start(bf16[512,768]{1,0:T(8,128)(2,1)S(1)} %collective-permute-done.14.refs_4_.refs_9_) | copy-start | bytes 2359300
  104.1 47.9 %collective-permute-start.15 = (bf16[256,768]{1,0:T(8,128)(2,1)S(1)}, bf16[256,768]{1,0:T(8,128)(2,1)}, u32[]{:S(2)}, u32[]{:S(2)}) collective-permute-start(bf16[256,768]{1,0:T(8,128)(2,1)S(1)} %slice.148), channel_id=1, source_target_pairs={{0,2},{2,4},{4,6},{6,0},{1,3},{3,5},{5,7},{7,1},{8,10},{10,12},{12... | collective-permute-start | bytes 1179656 | tf_op jit(solution)/shard_map/ppermute | solution.py:47
  107.7 15.1 %copy-start.4 = (bf16[512,768]{1,0:T(8,128)(2,1)}, bf16[512,768]{1,0:T(8,128)(2,1)S(1)}, u32[]{:S(2)}) copy-start(bf16[512,768]{1,0:T(8,128)(2,1)S(1)} %collective-permute-done.13.refs_1_.refs_6_) | copy-start | bytes 2359300
  108.5 43.5 %collective-permute-start.16 = (bf16[256,768]{1,0:T(8,128)(2,1)}, bf16[256,768]{1,0:T(8,128)(2,1)}, u32[]{:S(2)}, u32[]{:S(2)}) collective-permute-start(bf16[256,768]{1,0:T(8,128)(2,1)} %slice.149), channel_id=1, source_target_pairs={{0,6},{2,0},{4,2},{6,4},{1,7},{3,1},{5,3},{7,5},{8,14},{10,8},{12,... | collective-permute-start | bytes 1179656 | tf_op jit(solution)/shard_map/ppermute | solution.py:47
  116.9 6.8 %copy-start.28 = (f32[64]{0:T(128)S(1)}, f32[64]{0:T(128)}, u32[]{:S(2)}) copy-start(f32[64]{0:T(128)} %copy-done.27) | copy-start | bytes 772
  124.5 25.5 %all-to-all-start.3 = ((f32[2,256,32]{2,0,1:T(2,128)}), f32[2,256,32]{2,0,1:T(2,128)S(1)}, u32[]{:S(2)}, u32[]{:S(2)}) async-start(f32[2,256,32]{2,0,1:T(2,128)} %broadcast_in_dim.81), calls=%async_computation.3 | async-start | bytes 524288 | tf_op jit(solution)/shard_map/all_to_all | solution.py:454
  138.1 27.4 %collective-permute-start.10 = (bf16[256,768]{1,0:T(8,128)(2,1)}, bf16[256,768]{1,0:T(8,128)(2,1)S(1)}, u32[]{:S(2)}, u32[]{:S(2)}) collective-permute-start(bf16[256,768]{1,0:T(8,128)(2,1)} %get-tuple-element.40), channel_id=1, source_target_pairs={{0,6},{2,0},{4,2},{6,4},{1,7},{3,1},{5,3},{7,5},{8,14},{10,8},{12,... | collective-permute-start | bytes 1179656 | tf_op jit(solution)/shard_map/ppermute | solution.py:47
  148.5 18.0 %collective-permute-start.8 = (bf16[256,768]{1,0:T(8,128)(2,1)}, bf16[256,768]{1,0:T(8,128)(2,1)S(1)}, u32[]{:S(2)}, u32[]{:S(2)}) collective-permute-start(bf16[256,768]{1,0:T(8,128)(2,1)} %get-tuple-element.38), channel_id=1, source_target_pairs={{0,2},{2,4},{4,6},{6,0},{1,3},{3,5},{5,7},{7,1},{8,10},{10,12},{12... | collective-permute-start | bytes 1179656 | tf_op jit(solution)/shard_map/ppermute | solution.py:47
  151.3 7.1 %copy-start.23 = (f32[64]{0:T(128)}, f32[64]{0:T(128)S(1)}, u32[]{:S(2)}) copy-start(f32[64]{0:T(128)S(1)} %fusion.31) | copy-start | bytes 772
  158.4 7.2 %copy-start.7 = (bf16[512,768]{1,0:T(8,128)(2,1)S(1)}, bf16[512,768]{1,0:T(8,128)(2,1)}, u32[]{:S(2)}) copy-start(bf16[512,768]{1,0:T(8,128)(2,1)} %get-tuple-element.39) | copy-start | bytes 2359300
  163.7 28.1 %collective-permute-start.19 = (bf16[256,768]{1,0:T(8,128)(2,1)}, bf16[256,768]{1,0:T(8,128)(2,1)}, u32[]{:S(2)}, u32[]{:S(2)}) collective-permute-start(bf16[256,768]{1,0:T(8,128)(2,1)} %get-tuple-element.51), channel_id=1, source_target_pairs={{0,6},{2,0},{4,2},{6,4},{1,7},{3,1},{5,3},{7,5},{8,14},{10,8},{12,... | collective-permute-start | bytes 1179656 | tf_op jit(solution)/shard_map/ppermute | solution.py:47
  165.7 27.3 %collective-permute-start.11 = (bf16[512,768]{1,0:T(8,128)(2,1)S(1)}, bf16[512,768]{1,0:T(8,128)(2,1)}, u32[]{:S(2)}, u32[]{:S(2)}) collective-permute-start(bf16[512,768]{1,0:T(8,128)(2,1)S(1)} %pad_maximum_fusion.1), channel_id=1, source_target_pairs={{0,6},{2,0},{4,2},{6,4},{1,7},{3,1},{5,3},{7,5},{8,14},{10,8},{12,... | collective-permute-start | bytes 2359304 | tf_op jit(solution)/shard_map/ppermute | solution.py:47
  166.6 26.4 %collective-permute-start.9 = (bf16[512,768]{1,0:T(8,128)(2,1)S(1)}, bf16[512,768]{1,0:T(8,128)(2,1)}, u32[]{:S(2)}, u32[]{:S(2)}) collective-permute-start(bf16[512,768]{1,0:T(8,128)(2,1)S(1)} %pad_maximum_fusion), channel_id=1, source_target_pairs={{0,2},{2,4},{4,6},{6,0},{1,3},{3,5},{5,7},{7,1},{8,10},{10,12},{12... | collective-permute-start | bytes 2359304 | tf_op jit(solution)/shard_map/ppermute | solution.py:47
  177.2 32.4 %collective-permute-start.17 = (bf16[256,768]{1,0:T(8,128)(2,1)}, bf16[256,768]{1,0:T(8,128)(2,1)}, u32[]{:S(2)}, u32[]{:S(2)}) collective-permute-start(bf16[256,768]{1,0:T(8,128)(2,1)} %get-tuple-element.49), channel_id=1, source_target_pairs={{0,2},{2,4},{4,6},{6,0},{1,3},{3,5},{5,7},{7,1},{8,10},{10,12},{12... | collective-permute-start | bytes 1179656 | tf_op jit(solution)/shard_map/ppermute | solution.py:47
  177.6 14.2 %copy-start.8 = (bf16[512,768]{1,0:T(8,128)(2,1)S(1)}, bf16[512,768]{1,0:T(8,128)(2,1)}, u32[]{:S(2)}) copy-start(bf16[512,768]{1,0:T(8,128)(2,1)} %get-tuple-element.50) | copy-start | bytes 2359300
  191.7 74.7 %collective-permute-start.22 = (bf16[768,3072]{1,0:T(8,128)(2,1)}, bf16[768,3072]{1,0:T(8,128)(2,1)}, u32[]{:S(2)}, u32[]{:S(2)}) collective-permute-start(bf16[768,3072]{1,0:T(8,128)(2,1)} %get-tuple-element.54), channel_id=1, source_target_pairs={{0,1},{1,0},{2,3},{3,2},{4,5},{5,4},{6,7},{7,6},{8,9},{9,8},{10,11... | collective-permute-start | bytes 14155784 | tf_op jit(solution)/shard_map/ppermute | solution.py:51
  195.6 14.0 %copy-start.6 = (bf16[512,768]{1,0:T(8,128)(2,1)S(1)}, bf16[512,768]{1,0:T(8,128)(2,1)}, u32[]{:S(2)}) copy-start(bf16[512,768]{1,0:T(8,128)(2,1)} %get-tuple-element.48) | copy-start | bytes 2359300
  195.6 36.6 %all-to-all-start.2 = ((bf16[16,32,768]{2,0,1:T(8,128)(2,1)}), bf16[16,32,768]{2,0,1:T(8,128)(2,1)S(1)}, u32[]{:S(2)}, u32[]{:S(2)}) async-start(bf16[16,32,768]{2,0,1:T(8,128)(2,1)} %bitcast.23), calls=%async_computation.2 | async-start | bytes 1572864 | tf_op jit(solution)/shard_map/all_to_all | solution.py:55
  206.3 24.8 %copy-start.10 = (bf16[512,768]{1,0:T(8,128)(2,1)S(1)}, bf16[512,768]{1,0:T(8,128)(2,1)}, u32[]{:S(2)}) copy-start(bf16[512,768]{1,0:T(8,128)(2,1)} %get-tuple-element.47) | copy-start | bytes 2359300
  206.3 20.1 %collective-permute-start.20 = (bf16[512,768]{1,0:T(8,128)(2,1)S(1)}, bf16[512,768]{1,0:T(8,128)(2,1)S(1)}, u32[]{:S(2)}, u32[]{:S(2)}) collective-permute-start(bf16[512,768]{1,0:T(8,128)(2,1)S(1)} %pad_maximum_fusion.3), channel_id=1, source_target_pairs={{0,6},{2,0},{4,2},{6,4},{1,7},{3,1},{5,3},{7,5},{8,14},{10,8},{12,... | collective-permute-start | bytes 2359304 | tf_op jit(solution)/shard_map/ppermute | solution.py:47
  210.7 20.3 %collective-permute-start.18 = (bf16[512,768]{1,0:T(8,128)(2,1)S(1)}, bf16[512,768]{1,0:T(8,128)(2,1)S(1)}, u32[]{:S(2)}, u32[]{:S(2)}) collective-permute-start(bf16[512,768]{1,0:T(8,128)(2,1)S(1)} %pad_maximum_fusion.2), channel_id=1, source_target_pairs={{0,2},{2,4},{4,6},{6,0},{1,3},{3,5},{5,7},{7,1},{8,10},{10,12},{12... | collective-permute-start | bytes 2359304 | tf_op jit(solution)/shard_map/ppermute | solution.py:47
  232.2 10.1 %copy-start.24 = (f32[64]{0:T(128)S(1)}, f32[64]{0:T(128)}, u32[]{:S(2)}) copy-start(f32[64]{0:T(128)} %copy-done.23) | copy-start | bytes 772
  232.2 31.8 %all-to-all-start.4 = ((bf16[16,32,768]{2,0,1:T(8,128)(2,1)}), bf16[16,32,768]{2,0,1:T(8,128)(2,1)S(1)}, u32[]{:S(2)}, u32[]{:S(2)}) async-start(bf16[16,32,768]{2,0,1:T(8,128)(2,1)} %bitcast.29), calls=%async_computation.4 | async-start | bytes 1572864 | tf_op jit(solution)/shard_map/all_to_all | solution.py:55
  242.0 22.3 %copy-start.12 = (f32[128,256]{1,0:T(8,128)S(1)}, f32[128,256]{1,0:T(8,128)}, u32[]{:S(2)}) copy-start(f32[128,256]{1,0:T(8,128)} %copy-done.11) | copy-start | bytes 393220
  242.0 22.3 %copy-start.16 = (bf16[128,384]{1,0:T(8,128)(2,1)S(1)}, bf16[128,384]{1,0:T(8,128)(2,1)}, u32[]{:S(2)}) copy-start(bf16[128,384]{1,0:T(8,128)(2,1)} %param.9) | copy-start | bytes 294916
  242.1 23.5 %copy-start.19 = (bf16[128,256]{1,0:T(8,128)(2,1)S(1)}, bf16[128,256]{1,0:T(8,128)(2,1)}, u32[]{:S(2)}) copy-start(bf16[128,256]{1,0:T(8,128)(2,1)} %copy-done.18) | copy-start | bytes 196612
  242.2 23.5 %copy-start.25 = (bf16[128,384]{1,0:T(8,128)(2,1)S(1)}, bf16[128,384]{1,0:T(8,128)(2,1)}, u32[]{:S(2)}) copy-start(bf16[128,384]{1,0:T(8,128)(2,1)} %param.16) | copy-start | bytes 294916
  242.2 1.4 collective-permute-start.12
  264.2 1.4 collective-permute-start.21
  (9 other events, 13.4 us)

commit v3 on v2

--- a/solution.py
+++ b/solution.py
@@ -21,26 +21,75 @@
 bf16, f32 = jnp.bfloat16, jnp.float32
 
 
-def route_tables(expert_ids, route_share, capacity):
-    experts_iota = jnp.arange(EXPERTS, dtype=jnp.int32)
-    first_hot = (expert_ids[:, 0:1] == experts_iota[None, :]).astype(jnp.int32)
-    second_hot = (expert_ids[:, 1:2] == experts_iota[None, :]).astype(jnp.int32)
-    first_rank = jnp.sum((jnp.cumsum(first_hot, axis=0) - first_hot) * first_hot, axis=1)
-    second_before = (
-        jnp.cumsum(second_hot, axis=0) - second_hot + jnp.sum(first_hot, axis=0)[None, :]
-    )
-    second_rank = jnp.sum(second_before * second_hot, axis=1)
-    route_ranks = jnp.stack([first_rank, second_rank], axis=1)
-    route_kept = route_ranks < capacity
-    half = capacity // 2
-    slot_index = (route_ranks // half) * (EXPERTS * half) + expert_ids * half + route_ranks % half
-    slot_index = jnp.where(route_kept, slot_index, -1)
-    shares = jnp.stack([route_share, 1.0 - route_share], axis=1) * route_kept.astype(f32)
-    slot_iota = jnp.arange(EXPERTS * capacity, dtype=jnp.int32)
-    matches = (slot_index[:, :, None] == slot_iota[None, None, :]).astype(f32)
-    picker = jnp.sum(matches, axis=1)
-    mixing = jnp.sum(matches * shares[:, :, None], axis=1)
-    return (picker, mixing)
+def route_kernel(at_ref, ids_ref, share_ref, tokens_ref, upstream_ref, *refs):
+    mine_ref, theirs_ref, meta_ref, picker_ref, mixing_ref, both, meta = refs
+    count, slots = picker_ref.shape
+    local_width = tokens_ref.shape[1]
+    half_cap = slots // (2 * EXPERTS)
+    lane = lax.broadcasted_iota(jnp.int32, (count, count), 1)
+    row = lax.broadcasted_iota(jnp.int32, (count, count), 0)
+    earlier = (lane < row).astype(f32)
+    hot = [(lane == ids_ref[:, pl.ds(i, 1)]).astype(f32) for i in (0, 1)]
+    before = [plain(earlier.astype(bf16), h.astype(bf16)) for h in hot]
+    before[1] = before[1] + jnp.sum(hot[0], axis=0, keepdims=True)
+    slot_iota = lax.broadcasted_iota(jnp.int32, (count, slots), 1)
+    share = share_ref[...]
+    picker = jnp.zeros((count, slots), f32)
+    mixing = jnp.zeros((count, slots), f32)
+    for i, weight in ((0, share), (1, 1.0 - share)):
+        rank = jnp.sum(before[i] * hot[i], axis=1, keepdims=True).astype(jnp.int32)
+        late = (rank >= half_cap).astype(jnp.int32)
+        slot = late * (slots // 2 - half_cap) + ids_ref[:, pl.ds(i, 1)] * half_cap + rank
+        slot = jnp.where(rank < 2 * half_cap, slot, -1)
+        match = (slot_iota == slot).astype(f32)
+        picker = picker + match
+        mixing = mixing + match * weight
+    picker_ref[...] = picker.astype(bf16)
+    mixing_ref[...] = mixing
+    by_slot = picker.T.astype(bf16)
+    shares = mixing.T
+    slot_share = jnp.sum(shares, axis=1, keepdims=True)
+    both[:, pl.ds(0, local_width)] = plain(by_slot, tokens_ref[...]).astype(bf16)
+    both[:, pl.ds(local_width, local_width)] = (
+        plain(by_slot, upstream_ref[...]) * slot_share
+    ).astype(bf16)
+    lane = lax.broadcasted_iota(jnp.int32, (slots, count), 1)
+    table = jnp.zeros((slots, count), f32)
+    for seq in range(count // SEQ_LEN):
+        part = jnp.where(lane // SEQ_LEN == seq, shares, 0.0)
+        part = jnp.sum(part, axis=1, keepdims=True)
+        high = part.astype(bf16).astype(f32)
+        table = jnp.where(lane == 2 * seq, high, table)
+        table = jnp.where(lane == 2 * seq + 1, part - high, table)
+    meta[...] = table.astype(bf16)
+    half = slots // 2
+    core = at_ref[1]
+    own = pl.ds(pl.multiple_of(core * half, half), half)
+    other = pl.ds(pl.multiple_of((1 - core) * half, half), half)
+    mine_ref[...] = both[own]
+    theirs_ref[...] = both[other]
+    meta_ref[...] = meta[own]
+
+
+def pack_kernel(at_ref, mine_ref, got_ref, meta_ref, token_ref, grad_ref):
+    local_width = mine_ref.shape[1] // 2
+    half_cap = mine_ref.shape[0] // EXPERTS
+    replicas = token_ref.shape[0] // mine_ref.shape[0]
+    for core in (0, 1):
+        low, high = (mine_ref, got_ref) if core == 0 else (got_ref, mine_ref)
+
+        @pl.when(at_ref[1] == core)
+        def _(low=low, high=high):
+            for i in range(EXPERTS * replicas):
+                src = pl.ds(i // replicas * half_cap, half_cap)
+                dst = pl.ds(i * half_cap, half_cap)
+                token_ref[dst, pl.ds(0, local_width)] = low[src, pl.ds(0, local_width)]
+                token_ref[dst, pl.ds(local_width, local_width)] = high[src, pl.ds(0, local_width)]
+                grad_ref[dst, pl.ds(0, local_width)] = low[src, pl.ds(local_width, local_width)]
+                grad_ref[dst, pl.ds(local_width, local_width)] = high[
+                    src, pl.ds(local_width, local_width)
+                ]
+                token_ref[dst, pl.ds(2 * local_width, 128)] = meta_ref[src]
 
 
 def rot(value, shift):
@@ -356,53 +405,54 @@
     rows = ep_size * half_cap
     hid = w_gate.shape[0]
     core = lax.axis_index("tp_c")
-    place = lax.axis_index("tp_y").astype(jnp.int32).reshape(1)
+    place = jnp.stack([lax.axis_index("tp_y"), core]).astype(jnp.int32)
 
     wg_other, wu_other, wd_other = swap(w_gate), swap(w_up), swap(w_down)
 
-    picker, mixing = route_tables(expert_ids, route_share, capacity)
     seq_local = tok_count // SEQ_LEN
-    over_tokens = (((0,), (0,)), ((), ()))
-    both = lax.dot_general(
-        picker.astype(bf16),
-        jnp.concatenate([tokens, upstream], axis=1),
-        over_tokens,
-        preferred_element_type=f32,
-    )
-    slot_share = jnp.sum(mixing, axis=0)
-    column = lax.broadcasted_iota(jnp.int32, (1, 2 * local_width), 1)
-    both = both * jnp.where(column < local_width, 1.0, slot_share[:, None])
-    both = both.astype(bf16).reshape(2, EXPERTS * half_cap, 2 * local_width)
-    mine = lax.dynamic_index_in_dim(both, core, 0, keepdims=False)
-    theirs = swap(lax.dynamic_index_in_dim(both, 1 - core, 0, keepdims=False))
-    low = jnp.where(core == 0, mine, theirs)
-    high = jnp.where(core == 0, theirs, mine)
-    token_block = jnp.concatenate([low[:, :local_width], high[:, :local_width]], axis=1)
-    grad_block = jnp.concatenate([low[:, local_width:], high[:, local_width:]], axis=1)
-
-    token_seq = lax.broadcasted_iota(jnp.int32, (tok_count, 128), 0) // SEQ_LEN
-    lane = lax.broadcasted_iota(jnp.int32, (tok_count, 128), 1)
-    my_mixing = jnp.where(
-        core == 0, mixing[:, : EXPERTS * half_cap], mixing[:, EXPERTS * half_cap :]
-    )
-    meta = lax.dot_general(
-        my_mixing,
-        (token_seq == lane // 2).astype(f32),
-        over_tokens,
-        precision=lax.Precision.HIGHEST,
-        preferred_element_type=f32,
-    )
-    meta_high = lax.reduce_precision(meta, 8, 7)
-    meta = jnp.where(lane[:1] % 2 == 0, meta_high, meta - meta_high).astype(bf16)
-    grad_block = jnp.concatenate([grad_block, meta], axis=1)
+    half_slots = EXPERTS * half_cap
+    half_rows = jax.ShapeDtypeStruct((half_slots, block), bf16)
+    mine, theirs, meta, picker, mixing = call(
+        route_kernel,
+        1,
+        [whole((tok_count, 2)), whole((tok_count, 1))] + [whole((tok_count, local_width))] * 2,
+        [whole((half_slots, block))] * 2
+        + [whole((half_slots, 128))]
+        + [whole((tok_count, 2 * half_slots))] * 2,
+        [
+            half_rows,
+            half_rows,
+            jax.ShapeDtypeStruct((half_slots, 128), bf16),
+            jax.ShapeDtypeStruct((tok_count, 2 * half_slots), bf16),
+            jax.ShapeDtypeStruct((tok_count, 2 * half_slots), f32),
+        ],
+        [
+            pltpu.VMEM((2 * half_slots, block), bf16),
+            pltpu.VMEM((2 * half_slots, 128), bf16),
+        ],
+        1_000_000,
+        (place, expert_ids, route_share[:, None], tokens, upstream),
+    )
+    token_block, grad_block = call(
+        pack_kernel,
+        1,
+        [whole((half_slots, block))] * 2 + [whole((half_slots, 128))],
+        [whole((rows, block + 128)), whole((rows, block))],
+        [
+            jax.ShapeDtypeStruct((rows, block + 128), bf16),
+            jax.ShapeDtypeStruct((rows, block), bf16),
+        ],
+        [],
+        1_000_000,
+        (place, mine, swap(theirs), meta),
+    )
 
     def to_experts(block_rows):
         width = block_rows.shape[1]
-        block_rows = block_rows.reshape(EXPERTS, half_cap, width)
-        return exchange(jnp.repeat(block_rows, replicas, axis=0)).reshape(rows, width)
-
-    token_rows = to_experts(token_block)
-    grad_full = to_experts(grad_block)
+        return exchange(block_rows.reshape(ep_size, half_cap, width)).reshape(rows, width)
+
+    token_full = to_experts(token_block)
+    grad_rows = to_experts(grad_block)
 
     head = lax.all_gather(reward_head, TP, axis=0, tiled=True)
     head_own = jnp.sum(w_down.astype(f32) * head[None, :], axis=1)
@@ -413,10 +463,10 @@
     seq_total = pair_order.shape[0]
     offset = lax.axis_index(EP) * seq_local
     placed = lax.dynamic_update_slice(jnp.zeros((seq_total,), f32), local_rewards, (offset,))
-    token_rows, head_row, placed = lax.optimization_barrier((token_rows, head_row, placed))
-
-    token_pieces = gather_features(token_rows)
-    grad_pieces = gather_features(grad_full[:, :block])
+    token_full, head_row, placed = lax.optimization_barrier((token_full, head_row, placed))
+
+    token_pieces = gather_features(token_full[:, :block])
+    grad_pieces = gather_features(grad_rows)
 
     slots_hid = (rows, 2 * hid)
     meta_spec = pl.BlockSpec((rows, 128), lambda k, y: (0, block // 128))
@@ -446,7 +496,7 @@
         + [jax.ShapeDtypeStruct(slots_hid, bf16), jax.ShapeDtypeStruct((ep_size, 128), f32)],
         [pltpu.VMEM(slots_hid, f32)] * 2 + [pltpu.VMEM((rows, block), bf16)],
         work,
-        (place, far_low, far_high, *gate_weights, head_row, grad_full, gate, up),
+        (place, far_low, far_high, *gate_weights, head_row, token_full, gate, up),
     )
     placed = (placed + score[:, :seq_local].reshape(seq_total)).reshape(2, 1, seq_total // 2)
     everyone = lax.axis_size(EP_TP)
@@ -515,7 +565,7 @@
         + [jax.ShapeDtypeStruct((rows // 2, block), bf16)] * 2,
         [],
         work,
-        (place, *gate_weights, head_row, grad_full, scaled, partial, slope, silu),
+        (place, *gate_weights, head_row, token_full, scaled, partial, slope, silu),
     )
     own_sums, ahead_sums, back_sums = call(
         rest_kernel,
@@ -561,7 +611,7 @@
 
     mixed_sum = plain(mixing, come_back(down_sums).astype(f32))
     layer_out = (tokens.astype(f32) + mixed_sum).astype(bf16)
-    returned = plain(picker.astype(bf16), come_back(input_sums))
+    returned = plain(picker, come_back(input_sums))
     grad_tokens = (grad_out.astype(f32) + returned).astype(bf16)
     return (layer_out, rewards, pair_loss, grad_tokens, grad_gate, grad_up, grad_down)
 

time: 276 us -> 297 us (1.076)
  Pallas kernels: 54.5 us -> 66.4 us
  blocking collectives: 12.8 us -> 23.9 us
    pallas_call x8 -> x10, Pallas kernels: 54.5 us -> 66.4 us  [call(): pl.pallas_call(kernel, grid_spec=pltpu.PrefetchScalarGridSpec(num_scalar_...]
    all_gather x1, blocking collectives: 12.8 us -> 23.9 us  [layer(): head = lax.all_gather(reward_head, TP, axis=0, tiled=True)]
    ppermute x16, waiting for transfers between devices: 41.8 us -> 48.1 us  [rot(): return lax.ppermute(value, 'tp_y', [(i, (i + shift) % 4) for i in range(4)])]
    all_to_all x4, waiting for transfers between devices: 48.8 us -> 43.7 us  [exchange(): lax.all_to_all(blocks.transpose(1, 0, 2), EP, split_axis=1, concat_axis=1...]
    ppermute x16, starting transfers between devices: 20.5 us -> 23.8 us  [rot(): return lax.ppermute(value, 'tp_y', [(i, (i + shift) % 4) for i in range(4)])]
  transfers between devices with their start and end apart: 28 -> 28, of which waited for: 14 -> 10; matrix products, arithmetic and copies ran while one was open for 9% -> 7% of each run, Pallas kernels for 20% -> 18%
where the time goes in v3:
time: 297 us; the launch traced here: 294 us
  waiting for transfers between devices  94.3 us (32%)
  starting transfers between devices  72.3 us (24%)
  Pallas kernels  66.4 us (22%)
  blocking collectives  23.9 us (8%)
  other arithmetic  17 us (6%)
  local copies, waits for them, and re-layouts  16.1 us (5%)
    pallas_call x10, Pallas kernels, call(): pl.pallas_call(kernel, grid_spec=pltpu.PrefetchScalarGridSpec(num_scalar_...  66.4 us
    ppermute x16, waiting for transfers between devices, rot(): return lax.ppermute(value, 'tp_y', [(i, (i + shift) % 4) for i in range(4)])  48.1 us
    all_to_all x4, waiting for transfers between devices, exchange(): lax.all_to_all(blocks.transpose(1, 0, 2), EP, split_axis=1, concat_axis=1...  43.7 us
    all_to_all x4, starting transfers between devices, exchange(): lax.all_to_all(blocks.transpose(1, 0, 2), EP, split_axis=1, concat_axis=1...  36.9 us
    all_gather x1, blocking collectives, layer(): head = lax.all_gather(reward_head, TP, axis=0, tiled=True)  23.9 us
    ppermute x16, starting transfers between devices, rot(): return lax.ppermute(value, 'tp_y', [(i, (i + shift) % 4) for i in range(4)])  23.8 us
    convert_element_type x7, other arithmetic, add(): sum((t.astype(f32) for t in terms[1:]), terms[0].astype(f32)).astype(bf16)  13.1 us
    all_to_all x1, starting transfers between devices, layer(): lax.all_to_all(spread, EP_TP, split_axis=1, concat_axis=1, tiled=True)  10.7 us
  transfers between devices with their start and end apart: 28, of which 10 were waited for; matrix products, arithmetic and copies ran while one was open for 7% of the time, Pallas kernels for 18%

profile of v3, /device:TPU:32, one launch (start us, length us, event | category | flops | bytes accessed | tf_op | source)
XLA Modules:
  0.0 294.5 jit_solution(10205573636524460550)
XLA Ops:
  0.6 1.5 copy.22.ids_ref
  2.2 1.4 copy.23.share_ref
  4.2 3.2 %shard_map.144 = (bf16[128,768]{1,0:T(8,128)(2,1)}, bf16[128,768]{1,0:T(8,128)(2,1)}, bf16[128,128]{1,0:T(8,128)(2,1)}, bf16[128,256]{1,0:T(8,128)(2,1)}, f32[128,256]{1,0:T(8,128)}) custom-call(s32[2]{0:T(128)} %pad_add_fusion.at_ref.y_ref, s32[128,2]{1,0:T(8,128)} %copy.22.ids_ref, f32[128,1]{1,0:T(8,128)} %copy.23.share_ref, bf16[128,384]{1,0:T(8,128)(2,1)} %tokens_ref.1, ...), custom_call_target="tpu_custom_call" | custom-call | flops 1000000 | bytes 20000000 | tf_op jit(solution)/shard_map/pallas_call | solution.py:379
  7.5 1.6 collective-permute-done.got_ref
  9.8 3.0 %shard_map.145 = (bf16[512,896]{1,0:T(8,128)(2,1)}, bf16[512,768]{1,0:T(8,128)(2,1)}) custom-call(s32[2]{0:T(128)} %pad_add_fusion.at_ref.y_ref, bf16[128,768]{1,0:T(8,128)(2,1)} %get-tuple-element.39.mine_ref, bf16[128,768]{1,0:T(8,128)(2,1)} %copy-done.14, bf16[128,128]{1,0:T(8,128)(2,1)} %get-tuple-element.41.meta_ref), custom_call_target="tpu_custom_call" | custom-call | flops 1000000 | bytes 20000000 | tf_op jit(solution)/shard_map/pallas_call | solution.py:379
  12.8 11.4 %all-to-all-start.3 = ((bf16[16,32,768]{2,0,1:T(8,128)(2,1)}), bf16[16,32,768]{2,0,1:T(8,128)(2,1)}, u32[]{:S(2)}, u32[]{:S(2)}) async-start(bf16[16,32,768]{2,0,1:T(8,128)(2,1)} %bitcast.42), calls=%async_computation.3 | async-start | bytes 1572864 | tf_op jit(solution)/shard_map/all_to_all | solution.py:104
  24.3 23.2 %all-to-all-done.3 = bf16[16,32,768]{2,0,1:T(8,128)(2,1)} async-done(((bf16[16,32,768]{2,0,1:T(8,128)(2,1)}), bf16[16,32,768]{2,0,1:T(8,128)(2,1)}, u32[]{:S(2)}, u32[]{:S(2)}) %all-to-all-start.3) | async-done | bytes 786464 | tf_op jit(solution)/shard_map/all_to_all | solution.py:104
  47.5 5.2 %all-to-all-start = ((bf16[16,32,896]{2,0,1:T(8,128)(2,1)}), bf16[16,32,896]{2,0,1:T(8,128)(2,1)}, u32[]{:S(2)}, u32[]{:S(2)}) async-start(bf16[16,32,896]{2,0,1:T(8,128)(2,1)} %bitcast.41), calls=%async_computation | async-start | bytes 1835008 | tf_op jit(solution)/shard_map/all_to_all | solution.py:104
  52.7 1.7 collective-permute-start.14
  55.4 23.9 %all-gather = f32[8,1,384]{2,1,0:T(1,128)S(1)} all-gather(f32[1,1,384]{2,1,0:T(1,128)S(1)} %reshape.100), channel_id=1, replica_groups=mesh['ep_x'=4,'ep_z'=8,'tp_y'=4,'tp_c'=2] {'tp_y','tp_c'}, dimensions={0}, use_global_device_ids=true | all-gather | bytes 13824 | tf_op jit(solution)/shard_map/all_gather | solution.py:457
  82.0 1.2 slice.78.refs_0_
  83.2 1.2 collective-permute-start.2
  84.4 2.1 collective-permute-start.4
  86.5 1.0 slice.108
  87.5 14.2 %collective-permute-done.13.refs_1_.refs_6_ = bf16[512,768]{1,0:T(8,128)(2,1)S(1)} collective-permute-done((bf16[512,768]{1,0:T(8,128)(2,1)}, bf16[512,768]{1,0:T(8,128)(2,1)S(1)}, u32[]{:S(2)}, u32[]{:S(2)}) %collective-permute-start.13) | collective-permute-done | bytes 786464 | tf_op jit(solution)/shard_map/ppermute | solution.py:96
  101.7 1.3 collective-permute-start.15
  104.0 1.1 collective-permute-start.16
  105.9 12.7 %collective-permute-done.4.refs_1_ = bf16[512,768]{1,0:T(8,128)(2,1)S(1)} collective-permute-done((bf16[512,768]{1,0:T(8,128)(2,1)S(1)}, bf16[512,768]{1,0:T(8,128)(2,1)S(1)}, u32[]{:S(2)}, u32[]{:S(2)}) %collective-permute-start.4) | collective-permute-done | bytes 786464 | tf_op jit(solution)/shard_map/ppermute | solution.py:96
  118.5 1.3 collective-permute-start.3
  120.6 2.2 collective-permute-start.5
  123.1 8.4 %shard_map.146 = (f32[512,512]{1,0:T(8,128)}, f32[512,512]{1,0:T(8,128)}) custom-call(s32[2]{0:T(128)} %pad_add_fusion.at_ref.y_ref, bf16[512,768]{1,0:T(8,128)(2,1)} %copy-done.4, bf16[512,768]{1,0:T(8,128)(2,1)} %copy-done.13, bf16[512,768]{1,0:T(8,128)(2,1)} %copy-done.12, bf16[256,3072]{1,0:T(8,128)(2,1)} %refs_0_.3, ...), custom_call_target="tpu_custom_call" | custom-call | flops 2415919104 | bytes 20000000 | tf_op jit(solution)/shard_map/pallas_call | solution.py:379
  131.5 7.1 %shard_map.150.refs_7_ = f32[512,512]{1,0:T(8,128)} custom-call(s32[2]{0:T(128)} %pad_add_fusion.at_ref.y_ref, bf16[512,768]{1,0:T(8,128)(2,1)} %bitcast.17.refs_0_.refs_5_, bf16[512,768]{1,0:T(8,128)(2,1)} %copy-done.2, bf16[256,768]{1,0:T(8,128)(2,1)} %collective-permute-done.15.refs_2_.refs_7_, bf16[256,768]{1,0:T(8,128)(2,1)} %collective-permute-done.16.refs_3_.refs_8_, ...), custom_call_target="tpu_custom_call" | custom-call | flops 1610612736 | bytes 20000000 | tf_op jit(solution)/shard_map/pallas_call | solution.py:379
  139.4 6.6 %shard_map.147 = (f32[512,512]{1,0:T(8,128)}, f32[512,512]{1,0:T(8,128)}, bf16[512,512]{1,0:T(8,128)(2,1)}, f32[32,128]{1,0:T(8,128)}) custom-call(s32[2]{0:T(128)} %pad_add_fusion.at_ref.y_ref, bf16[256,768]{1,0:T(8,128)(2,1)} %copy-done.10, bf16[256,768]{1,0:T(8,128)(2,1)} %copy-done.11, bf16[256,3072]{1,0:T(8,128)(2,1)} %refs_0_.3, ...), custom_call_target="tpu_custom_call" | custom-call | flops 805306368 | bytes 20000000 | tf_op jit(solution)/shard_map/pallas_call | solution.py:379
  147.7 10.7 %all-to-all-start.2 = ((f32[2,256,32]{2,0,1:T(2,128)}), f32[2,256,32]{2,0,1:T(2,128)S(1)}, u32[]{:S(2)}, u32[]{:S(2)}) async-start(f32[2,256,32]{2,0,1:T(2,128)} %broadcast_in_dim.36), calls=%async_computation.2 | async-start | bytes 524288 | tf_op jit(solution)/shard_map/all_to_all | solution.py:504
  158.4 3.3 %shard_map.149 = (bf16[256,768]{1,0:T(8,128)(2,1)}, bf16[256,768]{1,0:T(8,128)(2,1)}) custom-call(s32[2]{0:T(128)} %pad_add_fusion.at_ref.y_ref, bf16[512,512]{1,0:T(8,128)(2,1)} %get-tuple-element.47.hidden_ref.refs_10_, bf16[256,3072]{1,0:T(8,128)(2,1)} %refs_5_.3, bf16[256,3072]{1,0:T(8,128)(2,1)} %copy-done.1), custom_call_target="tpu_custom_call" | custom-call | flops 402653184 | bytes 20000000 | tf_op jit(solution)/shard_map/pallas_call | solution.py:379
  161.8 2.9 collective-permute-start.10
  164.6 6.2 %shard_map.148 = (bf16[512,768]{1,0:T(8,128)(2,1)}, bf16[512,768]{1,0:T(8,128)(2,1)}, bf16[512,768]{1,0:T(8,128)(2,1)}) custom-call(s32[2]{0:T(128)} %pad_add_fusion.at_ref.y_ref, bf16[512,512]{1,0:T(8,128)(2,1)} %get-tuple-element.47.hidden_ref.refs_10_, bf16[256,3072]{1,0:T(8,128)(2,1)} %refs_5_.3, bf16[256,3072]{1,0:T(8,128)(2,1)} %copy-done.1), custom_call_target="tpu_custom_call" | custom-call | flops 1207959552 | bytes 20000000 | tf_op jit(solution)/shard_map/pallas_call | solution.py:379
  170.8 1.0 slice.83
  171.9 1.0 slice.82
  175.0 6.1 %shard_map.151 = (bf16[512,512]{1,0:T(8,128)(2,1)}, bf16[512,512]{1,0:T(8,128)(2,1)}, f32[512,1]{1,0:T(8,128)}, bf16[256,768]{1,0:T(8,128)(2,1)}, bf16[256,768]{1,0:T(8,128)(2,1)}) custom-call(s32[2]{0:T(128)} %pad_add_fusion.at_ref.y_ref, bf16[256,3072]{1,0:T(8,128)(2,1)} %refs_0_.3, bf16[256,3072]{1,0:T(8,128)(2,1)} %collective-permute-done.6.refs_4_.refs_3_.refs_1_, ...), custom_call_target="tpu_custom_call" | custom-call | flops 805306368 | bytes 20000000 | tf_op jit(solution)/shard_map/pallas_call | solution.py:379
  181.1 3.3 %collective-permute-start.19 = (bf16[256,768]{1,0:T(8,128)(2,1)}, bf16[256,768]{1,0:T(8,128)(2,1)S(1)}, u32[]{:S(2)}, u32[]{:S(2)}) collective-permute-start(bf16[256,768]{1,0:T(8,128)(2,1)} %get-tuple-element.65), channel_id=1, source_target_pairs={{0,6},{2,0},{4,2},{6,4},{1,7},{3,1},{5,3},{7,5},{8,14},{10,8},{12,... | collective-permute-start | bytes 1179656 | tf_op jit(solution)/shard_map/ppermute | solution.py:96
  184.4 1.1 add_convert_fusion.7
  185.9 2.0 collective-permute-start.9
  187.9 7.8 %shard_map.152 = (bf16[512,768]{1,0:T(8,128)(2,1)}, bf16[512,768]{1,0:T(8,128)(2,1)}, bf16[512,768]{1,0:T(8,128)(2,1)}) custom-call(s32[2]{0:T(128)} %pad_add_fusion.at_ref.y_ref, bf16[256,3072]{1,0:T(8,128)(2,1)} %refs_0_.3, bf16[256,3072]{1,0:T(8,128)(2,1)} %collective-permute-done.6.refs_4_.refs_3_.refs_1_, bf16[256,3072]{1,0:T(8,128)(2,1)} %refs_2_.5, ...), custom_call_target="tpu_custom_call" | custom-call | flops 2415919104 | bytes 20000000 | tf_op jit(solution)/shard_map/pallas_call | solution.py:379
  195.7 1.0 slice.94
  196.7 1.0 slice.93
  198.1 14.7 %shard_map.153 = (bf16[768,3072]{1,0:T(8,128)(2,1)}, bf16[768,3072]{1,0:T(8,128)(2,1)}) custom-call(s32[2]{0:T(128)} %pad_add_fusion.at_ref.y_ref, bf16[512,768]{1,0:T(8,128)(2,1)} %copy-done.4, bf16[512,768]{1,0:T(8,128)(2,1)} %copy-done.13, bf16[256,768]{1,0:T(8,128)(2,1)} %copy-done.10, bf16[256,768]{1,0:T(8,128)(2,1)} %copy-done.11, ...), custom_call_target="tpu_custom_call" | custom-call | flops 4831838208 | bytes 20000000 | tf_op jit(solution)/shard_map/pallas_call | solution.py:379
  212.8 1.2 add_convert_fusion.5
  214.0 2.6 add_convert_fusion.4
  216.6 10.6 %all-to-all-start.1 = ((bf16[16,32,768]{2,0,1:T(8,128)(2,1)}), bf16[16,32,768]{2,0,1:T(8,128)(2,1)S(1)}, u32[]{:S(2)}, u32[]{:S(2)}) async-start(bf16[16,32,768]{2,0,1:T(8,128)(2,1)} %bitcast.10), calls=%async_computation.1 | async-start | bytes 1572864 | tf_op jit(solution)/shard_map/all_to_all | solution.py:104
  227.3 3.3 %collective-permute-start.20 = (bf16[512,768]{1,0:T(8,128)(2,1)S(1)}, bf16[512,768]{1,0:T(8,128)(2,1)S(1)}, u32[]{:S(2)}, u32[]{:S(2)}) collective-permute-start(bf16[512,768]{1,0:T(8,128)(2,1)S(1)} %pad_maximum_fusion.3), channel_id=1, source_target_pairs={{0,6},{2,0},{4,2},{6,4},{1,7},{3,1},{5,3},{7,5},{8,14},{10,8},{12,... | collective-permute-start | bytes 2359304 | tf_op jit(solution)/shard_map/ppermute | solution.py:96
  230.6 1.1 add_convert_fusion.6
  231.8 15.6 %collective-permute-done.20 = bf16[512,768]{1,0:T(8,128)(2,1)S(1)} collective-permute-done((bf16[512,768]{1,0:T(8,128)(2,1)S(1)}, bf16[512,768]{1,0:T(8,128)(2,1)S(1)}, u32[]{:S(2)}, u32[]{:S(2)}) %collective-permute-start.20) | collective-permute-done | bytes 786464 | tf_op jit(solution)/shard_map/ppermute | solution.py:96
  247.4 4.6 %collective-permute-done.18 = bf16[512,768]{1,0:T(8,128)(2,1)S(1)} collective-permute-done((bf16[512,768]{1,0:T(8,128)(2,1)S(1)}, bf16[512,768]{1,0:T(8,128)(2,1)S(1)}, u32[]{:S(2)}, u32[]{:S(2)}) %collective-permute-start.18) | collective-permute-done | bytes 786464 | tf_op jit(solution)/shard_map/ppermute | solution.py:96
  252.0 1.2 add_convert_fusion.3
  253.2 9.8 %all-to-all-start.4 = ((bf16[16,32,768]{2,0,1:T(8,128)(2,1)}), bf16[16,32,768]{2,0,1:T(8,128)(2,1)S(1)}, u32[]{:S(2)}, u32[]{:S(2)}) async-start(bf16[16,32,768]{2,0,1:T(8,128)(2,1)} %bitcast.20), calls=%async_computation.4 | async-start | bytes 1572864 | tf_op jit(solution)/shard_map/all_to_all | solution.py:104
  264.6 20.5 %all-to-all-done.4 = bf16[16,32,768]{2,0,1:T(8,128)(2,1)S(1)} async-done(((bf16[16,32,768]{2,0,1:T(8,128)(2,1)}), bf16[16,32,768]{2,0,1:T(8,128)(2,1)S(1)}, u32[]{:S(2)}, u32[]{:S(2)}) %all-to-all-start.4) | async-done | bytes 786464 | tf_op jit(solution)/shard_map/all_to_all | solution.py:104
  287.5 5.9 %add_convert_fusion = (bf16[256,3072]{1,0:T(8,128)(2,1)}, bf16[256,3072]{1,0:T(8,128)(2,1)}, bf16[256,3072]{1,0:T(8,128)(2,1)}) fusion(bf16[768,3072]{1,0:T(8,128)(2,1)} %collective-permute-done.22, bf16[768,3072]{1,0:T(8,128)(2,1)} %get-tuple-element.67), kind=kLoop, calls=%fused_computation | loop fusion | flops 9437184 | bytes 14155776 | tf_op jit(solution)/shard_map/convert_element_type | solution.py:118
  (119 shorter events, 16.9 us)
Async XLA Ops:
  0.6 23.5 %copy-start = (bf16[256,3072]{1,0:T(8,128)(2,1)S(1)}, bf16[256,3072]{1,0:T(8,128)(2,1)}, u32[]{:S(2)}) copy-start(bf16[256,3072]{1,0:T(8,128)(2,1)} %refs_5_.3) | copy-start | bytes 4718596
  7.5 1.7 collective-permute-start
  12.8 42.1 %copy-start.18 = (f32[384]{0:T(512)S(1)}, f32[384]{0:T(512)}, u32[]{:S(2)}) copy-start(f32[384]{0:T(512)} %param.15) | copy-start | bytes 4612
  12.8 42.1 %copy-start.3 = (bf16[128,384]{1,0:T(8,128)(2,1)S(1)}, bf16[128,384]{1,0:T(8,128)(2,1)}, u32[]{:S(2)}) copy-start(bf16[128,384]{1,0:T(8,128)(2,1)} %tokens_ref.1) | copy-start | bytes 294916
  12.8 34.7 %all-to-all-start.3 = ((bf16[16,32,768]{2,0,1:T(8,128)(2,1)}), bf16[16,32,768]{2,0,1:T(8,128)(2,1)}, u32[]{:S(2)}, u32[]{:S(2)}) async-start(bf16[16,32,768]{2,0,1:T(8,128)(2,1)} %bitcast.42), calls=%async_computation.3 | async-start | bytes 1572864 | tf_op jit(solution)/shard_map/all_to_all | solution.py:104
  24.2 55.1 %collective-permute-start.1 = (bf16[256,3072]{1,0:T(8,128)(2,1)S(1)}, bf16[256,3072]{1,0:T(8,128)(2,1)S(1)}, u32[]{:S(2)}, u32[]{:S(2)}) collective-permute-start(bf16[256,3072]{1,0:T(8,128)(2,1)S(1)} %copy-done), channel_id=1, source_target_pairs={{0,1},{1,0},{2,3},{3,2},{4,5},{5,4},{6,7},{7,6},{8,9},{9,8},{10,11... | collective-permute-start | bytes 4718600 | tf_op jit(solution)/shard_map/ppermute | solution.py:100
  47.5 34.5 %all-to-all-start = ((bf16[16,32,896]{2,0,1:T(8,128)(2,1)}), bf16[16,32,896]{2,0,1:T(8,128)(2,1)}, u32[]{:S(2)}, u32[]{:S(2)}) async-start(bf16[16,32,896]{2,0,1:T(8,128)(2,1)} %bitcast.41), calls=%async_computation | async-start | bytes 1835008 | tf_op jit(solution)/shard_map/all_to_all | solution.py:104
  52.7 31.7 %collective-permute-start.14 = (bf16[512,768]{1,0:T(8,128)(2,1)}, bf16[512,768]{1,0:T(8,128)(2,1)}, u32[]{:S(2)}, u32[]{:S(2)}) collective-permute-start(bf16[512,768]{1,0:T(8,128)(2,1)} %bitcast.17.refs_0_.refs_5_), channel_id=1, source_target_pairs={{0,2},{2,4},{4,6},{6,0},{1,3},{3,5},{5,7},{7,1},{8,10},{10,12},{12... | collective-permute-start | bytes 2359304 | tf_op jit(solution)/shard_map/ppermute | solution.py:96
  54.3 66.3 %collective-permute-start.6 = (bf16[256,3072]{1,0:T(8,128)(2,1)}, bf16[256,3072]{1,0:T(8,128)(2,1)}, u32[]{:S(2)}, u32[]{:S(2)}) collective-permute-start(bf16[256,3072]{1,0:T(8,128)(2,1)} %refs_0_.3), channel_id=1, source_target_pairs={{0,1},{1,0},{2,3},{3,2},{4,5},{5,4},{6,7},{7,6},{8,9},{9,8},{10,11... | collective-permute-start | bytes 4718600 | tf_op jit(solution)/shard_map/ppermute | solution.py:100
  54.3 68.7 %collective-permute-start.7 = (bf16[256,3072]{1,0:T(8,128)(2,1)}, bf16[256,3072]{1,0:T(8,128)(2,1)}, u32[]{:S(2)}, u32[]{:S(2)}) collective-permute-start(bf16[256,3072]{1,0:T(8,128)(2,1)} %refs_2_.5), channel_id=1, source_target_pairs={{0,1},{1,0},{2,3},{3,2},{4,5},{5,4},{6,7},{7,6},{8,9},{9,8},{10,11... | collective-permute-start | bytes 4718600 | tf_op jit(solution)/shard_map/ppermute | solution.py:100
  79.3 1.1 copy-start.1
  81.1 20.6 %collective-permute-start.13 = (bf16[512,768]{1,0:T(8,128)(2,1)}, bf16[512,768]{1,0:T(8,128)(2,1)S(1)}, u32[]{:S(2)}, u32[]{:S(2)}) collective-permute-start(bf16[512,768]{1,0:T(8,128)(2,1)} %bitcast.17.refs_0_.refs_5_), channel_id=1, source_target_pairs={{0,6},{2,0},{4,2},{6,4},{1,7},{3,1},{5,3},{7,5},{8,14},{10,8},{12,... | collective-permute-start | bytes 2359304 | tf_op jit(solution)/shard_map/ppermute | solution.py:96
  83.2 37.4 %copy-start.4 = (bf16[512,768]{1,0:T(8,128)(2,1)}, bf16[512,768]{1,0:T(8,128)(2,1)S(1)}, u32[]{:S(2)}) copy-start(bf16[512,768]{1,0:T(8,128)(2,1)S(1)} %slice.78.refs_0_) | copy-start | bytes 2359300
  83.2 39.7 %copy-start.21 = (s32[64]{0:T(128)S(1)}, s32[64]{0:T(128)}, u32[]{:S(2)}) copy-start(s32[64]{0:T(128)} %param.17) | copy-start | bytes 772
  83.2 20.8 %collective-permute-start.2 = (bf16[512,768]{1,0:T(8,128)(2,1)S(1)}, bf16[512,768]{1,0:T(8,128)(2,1)S(1)}, u32[]{:S(2)}, u32[]{:S(2)}) collective-permute-start(bf16[512,768]{1,0:T(8,128)(2,1)S(1)} %slice.78.refs_0_), channel_id=1, source_target_pairs={{0,2},{2,4},{4,6},{6,0},{1,3},{3,5},{5,7},{7,1},{8,10},{10,12},{12... | collective-permute-start | bytes 2359304 | tf_op jit(solution)/shard_map/ppermute | solution.py:96
  84.4 34.2 %collective-permute-start.4 = (bf16[512,768]{1,0:T(8,128)(2,1)S(1)}, bf16[512,768]{1,0:T(8,128)(2,1)S(1)}, u32[]{:S(2)}, u32[]{:S(2)}) collective-permute-start(bf16[512,768]{1,0:T(8,128)(2,1)S(1)} %slice.78.refs_0_), channel_id=1, source_target_pairs={{0,6},{2,0},{4,2},{6,4},{1,7},{3,1},{5,3},{7,5},{8,14},{10,8},{12,... | collective-permute-start | bytes 2359304 | tf_op jit(solution)/shard_map/ppermute | solution.py:96
  101.7 29.8 %copy-start.2 = (bf16[512,768]{1,0:T(8,128)(2,1)}, bf16[512,768]{1,0:T(8,128)(2,1)S(1)}, u32[]{:S(2)}) copy-start(bf16[512,768]{1,0:T(8,128)(2,1)S(1)} %collective-permute-done.13.refs_1_.refs_6_) | copy-start | bytes 2359300
  101.7 29.8 %collective-permute-start.15 = (bf16[256,768]{1,0:T(8,128)(2,1)S(1)}, bf16[256,768]{1,0:T(8,128)(2,1)}, u32[]{:S(2)}, u32[]{:S(2)}) collective-permute-start(bf16[256,768]{1,0:T(8,128)(2,1)S(1)} %slice.108), channel_id=1, source_target_pairs={{0,2},{2,4},{4,6},{6,0},{1,3},{3,5},{5,7},{7,1},{8,10},{10,12},{12... | collective-permute-start | bytes 1179656 | tf_op jit(solution)/shard_map/ppermute | solution.py:96
  104.0 16.6 %copy-start.12 = (bf16[512,768]{1,0:T(8,128)(2,1)}, bf16[512,768]{1,0:T(8,128)(2,1)S(1)}, u32[]{:S(2)}) copy-start(bf16[512,768]{1,0:T(8,128)(2,1)S(1)} %collective-permute-done.2.refs_2_.refs_4_) | copy-start | bytes 2359300
  104.0 27.5 %collective-permute-start.16 = (bf16[256,768]{1,0:T(8,128)(2,1)S(1)}, bf16[256,768]{1,0:T(8,128)(2,1)}, u32[]{:S(2)}, u32[]{:S(2)}) collective-permute-start(bf16[256,768]{1,0:T(8,128)(2,1)S(1)} %slice.109), channel_id=1, source_target_pairs={{0,6},{2,0},{4,2},{6,4},{1,7},{3,1},{5,3},{7,5},{8,14},{10,8},{12,... | collective-permute-start | bytes 1179656 | tf_op jit(solution)/shard_map/ppermute | solution.py:96
  118.5 2.1 copy-start.13
  118.5 20.0 %collective-permute-start.3 = (bf16[256,768]{1,0:T(8,128)(2,1)}, bf16[256,768]{1,0:T(8,128)(2,1)S(1)}, u32[]{:S(2)}, u32[]{:S(2)}) collective-permute-start(bf16[256,768]{1,0:T(8,128)(2,1)} %slice.104), channel_id=1, source_target_pairs={{0,2},{2,4},{4,6},{6,0},{1,3},{3,5},{5,7},{7,1},{8,10},{10,12},{12... | collective-permute-start | bytes 1179656 | tf_op jit(solution)/shard_map/ppermute | solution.py:96
  120.6 17.9 %collective-permute-start.5 = (bf16[256,768]{1,0:T(8,128)(2,1)}, bf16[256,768]{1,0:T(8,128)(2,1)S(1)}, u32[]{:S(2)}, u32[]{:S(2)}) collective-permute-start(bf16[256,768]{1,0:T(8,128)(2,1)} %slice.105), channel_id=1, source_target_pairs={{0,6},{2,0},{4,2},{6,4},{1,7},{3,1},{5,3},{7,5},{8,14},{10,8},{12,... | collective-permute-start | bytes 1179656 | tf_op jit(solution)/shard_map/ppermute | solution.py:96
  138.6 0.8 copy-start.10
  138.6 0.9 copy-start.11
  147.7 25.2 %all-to-all-start.2 = ((f32[2,256,32]{2,0,1:T(2,128)}), f32[2,256,32]{2,0,1:T(2,128)S(1)}, u32[]{:S(2)}, u32[]{:S(2)}) async-start(f32[2,256,32]{2,0,1:T(2,128)} %broadcast_in_dim.36), calls=%async_computation.2 | async-start | bytes 524288 | tf_op jit(solution)/shard_map/all_to_all | solution.py:504
  161.8 22.6 %collective-permute-start.10 = (bf16[256,768]{1,0:T(8,128)(2,1)}, bf16[256,768]{1,0:T(8,128)(2,1)}, u32[]{:S(2)}, u32[]{:S(2)}) collective-permute-start(bf16[256,768]{1,0:T(8,128)(2,1)} %get-tuple-element.52), channel_id=1, source_target_pairs={{0,6},{2,0},{4,2},{6,4},{1,7},{3,1},{5,3},{7,5},{8,14},{10,8},{12,... | collective-permute-start | bytes 1179656 | tf_op jit(solution)/shard_map/ppermute | solution.py:96
  172.9 12.8 %collective-permute-start.8 = (bf16[256,768]{1,0:T(8,128)(2,1)}, bf16[256,768]{1,0:T(8,128)(2,1)S(1)}, u32[]{:S(2)}, u32[]{:S(2)}) collective-permute-start(bf16[256,768]{1,0:T(8,128)(2,1)} %get-tuple-element.50), channel_id=1, source_target_pairs={{0,2},{2,4},{4,6},{6,0},{1,3},{3,5},{5,7},{7,1},{8,10},{10,12},{12... | collective-permute-start | bytes 1179656 | tf_op jit(solution)/shard_map/ppermute | solution.py:96
  173.4 7.7 %copy-start.19 = (f32[64]{0:T(128)}, f32[64]{0:T(128)S(1)}, u32[]{:S(2)}) copy-start(f32[64]{0:T(128)S(1)} %div.26) | copy-start | bytes 772
  175.0 9.4 %copy-start.7 = (bf16[512,768]{1,0:T(8,128)(2,1)S(1)}, bf16[512,768]{1,0:T(8,128)(2,1)}, u32[]{:S(2)}) copy-start(bf16[512,768]{1,0:T(8,128)(2,1)} %get-tuple-element.51) | copy-start | bytes 2359300
  181.1 4.6 %copy-start.6 = (bf16[512,768]{1,0:T(8,128)(2,1)S(1)}, bf16[512,768]{1,0:T(8,128)(2,1)}, u32[]{:S(2)}) copy-start(bf16[512,768]{1,0:T(8,128)(2,1)} %get-tuple-element.49) | copy-start | bytes 2359300
  181.1 31.7 %collective-permute-start.19 = (bf16[256,768]{1,0:T(8,128)(2,1)}, bf16[256,768]{1,0:T(8,128)(2,1)S(1)}, u32[]{:S(2)}, u32[]{:S(2)}) collective-permute-start(bf16[256,768]{1,0:T(8,128)(2,1)} %get-tuple-element.65), channel_id=1, source_target_pairs={{0,6},{2,0},{4,2},{6,4},{1,7},{3,1},{5,3},{7,5},{8,14},{10,8},{12,... | collective-permute-start | bytes 1179656 | tf_op jit(solution)/shard_map/ppermute | solution.py:96
  185.6 28.4 %collective-permute-start.11 = (bf16[512,768]{1,0:T(8,128)(2,1)S(1)}, bf16[512,768]{1,0:T(8,128)(2,1)}, u32[]{:S(2)}, u32[]{:S(2)}) collective-permute-start(bf16[512,768]{1,0:T(8,128)(2,1)S(1)} %pad_maximum_fusion.1), channel_id=1, source_target_pairs={{0,6},{2,0},{4,2},{6,4},{1,7},{3,1},{5,3},{7,5},{8,14},{10,8},{12,... | collective-permute-start | bytes 2359304 | tf_op jit(solution)/shard_map/ppermute | solution.py:96
  185.9 28.1 %collective-permute-start.9 = (bf16[512,768]{1,0:T(8,128)(2,1)S(1)}, bf16[512,768]{1,0:T(8,128)(2,1)}, u32[]{:S(2)}, u32[]{:S(2)}) collective-permute-start(bf16[512,768]{1,0:T(8,128)(2,1)S(1)} %pad_maximum_fusion), channel_id=1, source_target_pairs={{0,2},{2,4},{4,6},{6,0},{1,3},{3,5},{5,7},{7,1},{8,10},{10,12},{12... | collective-permute-start | bytes 2359304 | tf_op jit(solution)/shard_map/ppermute | solution.py:96
  197.7 32.8 %collective-permute-start.17 = (bf16[256,768]{1,0:T(8,128)(2,1)}, bf16[256,768]{1,0:T(8,128)(2,1)}, u32[]{:S(2)}, u32[]{:S(2)}) collective-permute-start(bf16[256,768]{1,0:T(8,128)(2,1)} %get-tuple-element.63), channel_id=1, source_target_pairs={{0,2},{2,4},{4,6},{6,0},{1,3},{3,5},{5,7},{7,1},{8,10},{10,12},{12... | collective-permute-start | bytes 1179656 | tf_op jit(solution)/shard_map/ppermute | solution.py:96
  212.7 1.3 copy-start.8
  212.7 74.7 %collective-permute-start.22 = (bf16[768,3072]{1,0:T(8,128)(2,1)}, bf16[768,3072]{1,0:T(8,128)(2,1)}, u32[]{:S(2)}, u32[]{:S(2)}) collective-permute-start(bf16[768,3072]{1,0:T(8,128)(2,1)} %get-tuple-element.68), channel_id=1, source_target_pairs={{0,1},{1,0},{2,3},{3,2},{4,5},{5,4},{6,7},{7,6},{8,9},{9,8},{10,11... | collective-permute-start | bytes 14155784 | tf_op jit(solution)/shard_map/ppermute | solution.py:100
  216.6 36.6 %all-to-all-start.1 = ((bf16[16,32,768]{2,0,1:T(8,128)(2,1)}), bf16[16,32,768]{2,0,1:T(8,128)(2,1)S(1)}, u32[]{:S(2)}, u32[]{:S(2)}) async-start(bf16[16,32,768]{2,0,1:T(8,128)(2,1)} %bitcast.10), calls=%async_computation.1 | async-start | bytes 1572864 | tf_op jit(solution)/shard_map/all_to_all | solution.py:104
  227.2 3.4 %copy-start.5 = (bf16[512,768]{1,0:T(8,128)(2,1)S(1)}, bf16[512,768]{1,0:T(8,128)(2,1)}, u32[]{:S(2)}) copy-start(bf16[512,768]{1,0:T(8,128)(2,1)} %get-tuple-element.62) | copy-start | bytes 2359300
  227.3 24.8 %copy-start.9 = (bf16[512,768]{1,0:T(8,128)(2,1)S(1)}, bf16[512,768]{1,0:T(8,128)(2,1)}, u32[]{:S(2)}) copy-start(bf16[512,768]{1,0:T(8,128)(2,1)} %get-tuple-element.61) | copy-start | bytes 2359300
  227.3 20.1 %collective-permute-start.20 = (bf16[512,768]{1,0:T(8,128)(2,1)S(1)}, bf16[512,768]{1,0:T(8,128)(2,1)S(1)}, u32[]{:S(2)}, u32[]{:S(2)}) collective-permute-start(bf16[512,768]{1,0:T(8,128)(2,1)S(1)} %pad_maximum_fusion.3), channel_id=1, source_target_pairs={{0,6},{2,0},{4,2},{6,4},{1,7},{3,1},{5,3},{7,5},{8,14},{10,8},{12,... | collective-permute-start | bytes 2359304 | tf_op jit(solution)/shard_map/ppermute | solution.py:96
  231.7 20.3 %collective-permute-start.18 = (bf16[512,768]{1,0:T(8,128)(2,1)S(1)}, bf16[512,768]{1,0:T(8,128)(2,1)S(1)}, u32[]{:S(2)}, u32[]{:S(2)}) collective-permute-start(bf16[512,768]{1,0:T(8,128)(2,1)S(1)} %pad_maximum_fusion.2), channel_id=1, source_target_pairs={{0,2},{2,4},{4,6},{6,0},{1,3},{3,5},{5,7},{7,1},{8,10},{10,12},{12... | collective-permute-start | bytes 2359304 | tf_op jit(solution)/shard_map/ppermute | solution.py:96
  253.2 31.8 %all-to-all-start.4 = ((bf16[16,32,768]{2,0,1:T(8,128)(2,1)}), bf16[16,32,768]{2,0,1:T(8,128)(2,1)S(1)}, u32[]{:S(2)}, u32[]{:S(2)}) async-start(bf16[16,32,768]{2,0,1:T(8,128)(2,1)} %bitcast.20), calls=%async_computation.4 | async-start | bytes 1572864 | tf_op jit(solution)/shard_map/all_to_all | solution.py:104
  263.0 22.3 %copy-start.15 = (f32[128,256]{1,0:T(8,128)S(1)}, f32[128,256]{1,0:T(8,128)}, u32[]{:S(2)}) copy-start(f32[128,256]{1,0:T(8,128)} %get-tuple-element.38) | copy-start | bytes 393220
  263.1 23.5 %copy-start.16 = (bf16[128,384]{1,0:T(8,128)(2,1)S(1)}, bf16[128,384]{1,0:T(8,128)(2,1)}, u32[]{:S(2)}) copy-start(bf16[128,384]{1,0:T(8,128)(2,1)} %upstream_ref.1) | copy-start | bytes 294916
  263.1 23.5 %copy-start.20 = (bf16[128,256]{1,0:T(8,128)(2,1)S(1)}, bf16[128,256]{1,0:T(8,128)(2,1)}, u32[]{:S(2)}) copy-start(bf16[128,256]{1,0:T(8,128)(2,1)} %get-tuple-element.55) | copy-start | bytes 196612
  263.2 1.4 collective-permute-start.12
  285.2 1.4 collective-permute-start.21
  (2 other events, 1.4 us)
